TPU v7x, 32 devices: a whole 2x2x4 slice. The times are simulated.
32 devices in a mesh: tm: 8 (over z, y), space: 4 (over x, core).
Axes of the slice: x: 2, y: 2, z: 4, core: 2. Of those that a mesh axis runs over, the one named last changes fastest.
Arguments:
- start_values: float32 [8, 2, 1024, 1024], P('tm', None, 'space'), may hold values from -6 to 6
- node_values: float32 [8, 2, 2, 1024, 1024], P('tm', None, None, 'space'), may hold values from -6 to 6
Outputs:
- next_start: float32 [8, 2, 1024, 1024], P('tm', None, 'space')
- next_nodes: float32 [8, 2, 2, 1024, 1024], P('tm', None, None, 'space')
All inputs are finite; a program needn't handle non-finite values.
Results may differ from a plain program's by a relative error of at most 0.00002.
Values sent between devices are 32-bit elements; how exact they have to be, the bound alone decides.
No kernel may reach another device: no remote copies, remote signals or barrier semaphores. Data moves between devices by JAX's collectives and lax.ppermute only.
A program may use at most 64 MiB of HBM per device.

v0:
```python
import jax
import jax.numpy as jnp
from jax import lax
from jax.sharding import PartitionSpec as P

KX = 1024
KY = 1024
CX = 256


diffusion = 1.5
drift = 0.8
shear = 0.6
first_weights = (5.0 / 24.0, 1.0 / 3.0, -1.0 / 24.0)
second_weights = (-1.0 / 24.0, 1.0 / 3.0, 5.0 / 24.0)
whole_weights = (1.0 / 6.0, 2.0 / 3.0, 1.0 / 6.0)


def with_halo(shard, sides, width):
    for axis, dim in sides:
        peers, length = (lax.axis_size(axis), shard.shape[dim])
        up = [(i, (i + 1) % peers) for i in range(peers - 1)]
        down = [(j, i) for i, j in up]
        last = lax.slice_in_dim(shard, length - width, length, axis=dim)
        first = lax.slice_in_dim(shard, 0, width, axis=dim)
        before = lax.ppermute(last, axis, up)
        after = lax.ppermute(first, axis, down)
        shard = jnp.concatenate([before, shard, after], axis=dim)
    return shard


def from_behind(value, axis, steps):
    count = lax.axis_size(axis)
    first, last = (max(0, -steps), min(count, count - steps))
    return lax.ppermute(value, axis, [(source, source + steps) for source in range(first, last)])


def spectrum(row_index, column_index):
    along = (row_index.astype(jnp.float32) - KX // 2) / (KX // 2)
    across = (column_index.astype(jnp.float32) - KY // 2) / (KY // 2)
    real_rate = -diffusion * (along[:, None] * along[:, None] + across[None, :] * across[None, :])
    imag_rate = -drift * across[None, :] + 0.0 * along[:, None]
    return (real_rate, imag_rate, across)


def multiply(real_rate, imag_rate, field):
    return jnp.stack(
        [
            real_rate * field[..., 0, :, :] - imag_rate * field[..., 1, :, :],
            real_rate * field[..., 1, :, :] + imag_rate * field[..., 0, :, :],
        ],
        axis=-3,
    )


def divide(real_part, imag_part, field):
    modulus = real_part * real_part + imag_part * imag_part
    return jnp.stack(
        [
            (field[..., 0, :, :] * real_part + field[..., 1, :, :] * imag_part) / modulus,
            (field[..., 1, :, :] * real_part - field[..., 0, :, :] * imag_part) / modulus,
        ],
        axis=-3,
    )


def explicit(field, across):
    padded = with_halo(field, (("space", 2),), 1)
    sums = padded[..., 2:, :] + padded[..., :-2, :]
    factor = shear * across
    return jnp.stack([factor * sums[..., 1, :, :], -factor * sums[..., 0, :, :]], axis=-3)


def body(start_values, node_values):
    begin_value = start_values[0]
    old_nodes = node_values[0]
    slab_rows = begin_value.shape[1]
    slab_columns = begin_value.shape[2]
    leader = lax.axis_index("tm") == 0
    rank = lax.axis_index("space")
    row_index = rank * slab_rows + lax.iota(jnp.int32, slab_rows)
    real_rate, imag_rate, across = spectrum(row_index, lax.iota(jnp.int32, slab_columns))
    stacked = jnp.stack([begin_value, old_nodes[0], old_nodes[1]])
    old_coupling = explicit(stacked, across)
    old_slopes = multiply(real_rate, imag_rate, stacked) + old_coupling
    sum_one = (
        first_weights[0] * old_slopes[0]
        + first_weights[1] * old_slopes[1]
        + first_weights[2] * old_slopes[2]
    )
    sum_two = (
        second_weights[0] * old_slopes[0]
        + second_weights[1] * old_slopes[1]
        + second_weights[2] * old_slopes[2]
    )
    half_real = 1.0 - 0.5 * real_rate
    half_imag = -0.5 * imag_rate
    node_one = divide(
        half_real,
        half_imag,
        begin_value - 0.5 * multiply(real_rate, imag_rate, old_nodes[0]) + sum_one,
    )
    one_coupling = explicit(node_one[None], across)[0]
    node_two = divide(
        half_real,
        half_imag,
        node_one
        + 0.5 * (one_coupling - old_coupling[1])
        - 0.5 * multiply(real_rate, imag_rate, old_nodes[1])
        + sum_two,
    )
    two_coupling = explicit(node_two[None], across)[0]
    integral = (
        whole_weights[0] * old_slopes[0]
        + whole_weights[1] * (multiply(real_rate, imag_rate, node_one) + one_coupling)
        + whole_weights[2] * (multiply(real_rate, imag_rate, node_two) + two_coupling)
    )
    low_row = KX // 2 - CX // 2
    low_column = KY // 2 - CX // 2
    row_mask = ((row_index >= low_row) & (row_index < low_row + CX)).astype(jnp.float32)[:, None]

    def restrict(field):
        return field[..., low_column : low_column + CX] * row_mask

    def enlarge(field):
        return jnp.pad(field, ((0, 0), (0, 0), (low_column, slab_columns - low_column - CX)))

    coarse_real = real_rate[:, low_column : low_column + CX]
    coarse_imag = imag_rate[:, low_column : low_column + CX]
    begin_coarse = restrict(begin_value)
    end_coarse = restrict(node_two)
    tau = restrict(integral) - 0.5 * multiply(coarse_real, coarse_imag, begin_coarse + end_coarse)
    offset = 0.5 * multiply(coarse_real, coarse_imag, begin_coarse - end_coarse) + tau
    step_real = 1.0 - coarse_real
    step_imag = -coarse_imag

    def relay(counter, begin_now):
        finish = divide(step_real, step_imag, begin_now + offset)
        incoming = from_behind(finish, "tm", 1)
        return jnp.where(leader, begin_coarse, incoming)

    begin_new = lax.fori_loop(0, lax.axis_size("tm") - 1, relay, begin_coarse)
    end_new = divide(step_real, step_imag, begin_new + offset)
    delta_begin = begin_new - begin_coarse
    delta_end = end_new - end_coarse
    fixed_one = node_one + enlarge(0.5 * (delta_begin + delta_end))
    fixed_two = node_two + enlarge(delta_end)
    arrived = from_behind(fixed_two, "tm", 1)
    next_start = jnp.where(leader, begin_value, arrived)
    next_nodes = jnp.stack([fixed_one, fixed_two])
    return (next_start[None], next_nodes[None])


def solution(mesh):
    in_specs = (P("tm", None, "space", None), P("tm", None, None, "space", None))
    out_specs = (P("tm", None, "space", None), P("tm", None, None, "space", None))
    return jax.shard_map(body, mesh=mesh, in_specs=in_specs, out_specs=out_specs, check_vma=False)
```

profile of v0, /device:TPU:8, one launch (start us, length us, event | category | flops | bytes accessed | tf_op | source)
XLA Modules:
  0.0 233.1 jit_solution(17927046781905600992)
XLA Ops:
  0.6 2.7 %slice_bitcast_fusion.1 = (f32[1,2,256,1024]{3,2,1,0:T(8,128)S(1)}, f32[1,2,256,1024]{3,2,1,0:T(8,128)S(1)}) fusion(f32[1,2,2,256,1024]{4,3,2,1,0:T(8,128)} %param.5), kind=kLoop, calls=%fused_computation.70 | loop fusion | bytes 8388608 | tf_op jit(solution)/shard_map/slice | solution.py:101
  3.5 1.1 copy-done.9
  5.3 1.7 collective-permute-start.2
  7.1 1.3 collective-permute-start.1
  8.4 1.1 broadcast_add_fusion
  9.6 5.0 %fusion.32 = (f32[1,256,1024]{2,1,0:T(8,128)}, f32[1,256,1024]{2,1,0:T(8,128)}, f32[1,256,1024]{2,1,0:T(8,128)}, f32[1,256,1024]{2,1,0:T(8,128)}) fusion(f32[1,2,2,256,1024]{4,3,2,1,0:T(8,128)} %param.5, f32[256]{0:T(256)S(1)} %get-tuple-element.187, f32[1024]{0:T(1024)S(1)} %get-tuple-element.191, f32[1024]{0:T(1024)S(1)} %get-tuple-element.190, ...), kind=kLoop, calls=%fused_computation.83 | loop fusion | flops 3932160 | bytes 8398848 | tf_op jit(solution)/shard_map/sub | solution.py:49
  14.8 7.6 %pad_maximum_fusion.8 = (f32[3,2,256,1024]{3,2,1,0:T(8,128)S(1)}, f32[3,2,256,1024]{3,2,1,0:T(8,128)S(1)}) fusion(f32[1,2,256,1024]{3,2,1,0:T(8,128)} %copy-done.10, f32[1,2,256,1024]{3,2,1,0:T(8,128)} %copy-done.9, f32[1,2,256,1024]{3,2,1,0:T(8,128)S(1)} %copy-done, f32[3,2,1,1024]{3,2,1,0:T(1,128)S(1)} %collective-permute-done.2, ...), kind=kLoop, calls=%fused_computation.21 | loop fusion | flops 14155776 | bytes 18923520 | tf_op jit(solution)/shard_map/stack | solution.py:83
  22.5 1.8 multiply_subtract_fusion
  24.2 0.7 slice_multiply_fusion
  25.0 1.4 fusion.4
  26.5 1.3 fusion.21
  27.8 0.9 fusion.36
  29.0 4.3 %collective-permute-start.4 = (f32[1,2,1,1024]{3,2,1,0:T(1,128)S(1)}, f32[1,2,1,1024]{3,2,1,0:T(1,128)S(1)}, u32[]{:S(2)}, u32[]{:S(2)}) collective-permute-start(f32[1,2,1,1024]{3,2,1,0:T(1,128)S(1)} %get-tuple-element.182), channel_id=1, source_target_pairs={{0,1},{1,2},{2,3},{4,5},{5,6},{6,7},{8,9},{9,10},{10,11},{12,13},{... | collective-permute-start | bytes 24584 | tf_op jit(solution)/shard_map/ppermute | solution.py:26
  33.3 1.3 collective-permute-start.3
  35.0 2.6 %collective-permute-done.3 = f32[1,2,1,1024]{3,2,1,0:T(1,128)S(1)} collective-permute-done((f32[1,2,1,1024]{3,2,1,0:T(1,128)S(1)}, f32[1,2,1,1024]{3,2,1,0:T(1,128)S(1)}, u32[]{:S(2)}, u32[]{:S(2)}) %collective-permute-start.3) | collective-permute-done | bytes 8224 | tf_op jit(solution)/shard_map/ppermute | solution.py:27
  38.4 0.8 copy-done.15
  39.5 1.7 fusion.17
  41.3 0.9 fusion.38
  43.0 4.3 %collective-permute-start.6 = (f32[1,2,1,1024]{3,2,1,0:T(1,128)S(1)}, f32[1,2,1,1024]{3,2,1,0:T(1,128)S(1)}, u32[]{:S(2)}, u32[]{:S(2)}) collective-permute-start(f32[1,2,1,1024]{3,2,1,0:T(1,128)S(1)} %get-tuple-element.178), channel_id=1, source_target_pairs={{0,1},{1,2},{2,3},{4,5},{5,6},{6,7},{8,9},{9,10},{10,11},{12,13},{... | collective-permute-start | bytes 24584 | tf_op jit(solution)/shard_map/ppermute | solution.py:26
  47.3 1.5 collective-permute-start.5
  49.0 2.0 subtract_bitcast_fusion
  52.1 1.1 fusion.60
  53.3 129.6 %while.13 = (s32[]{:T(128)}, f32[2,256,256]{2,1,0:T(8,128)S(1)}, pred[]{:T(512)}, f32[2,256,256]{2,1,0:T(8,128)}, f32[256,256]{1,0:T(8,128)S(1)}, /*index=5*/f32...) while((s32[]{:T(128)}, f32[2,256,256]{2,1,0:T(8,128)S(1)}, pred[]{:T(512)}, ...), condition=%wide.region_1.2_spmd, body=%wide.region_0.1_spmd.sunk | while | flops 917506 | bytes 8126598 | solution.py:142
  53.3 1.1 add.686
  54.4 1.1 fusion.78
  55.6 3.4 %collective-permute-start = (f32[2,256,256]{2,1,0:T(8,128)S(1)}, f32[2,256,256]{2,1,0:T(8,128)}, u32[]{:S(2)}, u32[]{:S(2)}) collective-permute-start(f32[2,256,256]{2,1,0:T(8,128)S(1)} %pad_maximum_fusion.20), channel_id=1, source_target_pairs={{0,4},{4,8},{8,12},{12,16},{16,20},{20,24},{24,28},{1,5},{5,9},{9,... | collective-permute-start | bytes 1572872 | tf_op jit(solution)/shard_map/while/body/eval_jaxpr/ppermute | solution.py:35
  59.0 14.1 %collective-permute-done = f32[2,256,256]{2,1,0:T(8,128)} collective-permute-done((f32[2,256,256]{2,1,0:T(8,128)S(1)}, f32[2,256,256]{2,1,0:T(8,128)}, u32[]{:S(2)}, u32[]{:S(2)}) %collective-permute-start) | collective-permute-done | bytes 524320 | tf_op jit(solution)/shard_map/while/body/eval_jaxpr/ppermute | solution.py:35
  73.1 1.1 broadcast_select_fusion.2
  74.2 1.1 add.686
  75.3 1.1 fusion.78
  76.5 2.5 %collective-permute-start = (f32[2,256,256]{2,1,0:T(8,128)S(1)}, f32[2,256,256]{2,1,0:T(8,128)}, u32[]{:S(2)}, u32[]{:S(2)}) collective-permute-start(f32[2,256,256]{2,1,0:T(8,128)S(1)} %pad_maximum_fusion.20), channel_id=1, source_target_pairs={{0,4},{4,8},{8,12},{12,16},{16,20},{20,24},{24,28},{1,5},{5,9},{9,... | collective-permute-start | bytes 1572872 | tf_op jit(solution)/shard_map/while/body/eval_jaxpr/ppermute | solution.py:35
  79.0 14.3 %collective-permute-done = f32[2,256,256]{2,1,0:T(8,128)} collective-permute-done((f32[2,256,256]{2,1,0:T(8,128)S(1)}, f32[2,256,256]{2,1,0:T(8,128)}, u32[]{:S(2)}, u32[]{:S(2)}) %collective-permute-start) | collective-permute-done | bytes 524320 | tf_op jit(solution)/shard_map/while/body/eval_jaxpr/ppermute | solution.py:35
  93.4 1.1 broadcast_select_fusion.2
  94.5 1.1 add.686
  95.6 1.1 fusion.78
  96.8 1.9 collective-permute-start
  98.7 14.1 %collective-permute-done = f32[2,256,256]{2,1,0:T(8,128)} collective-permute-done((f32[2,256,256]{2,1,0:T(8,128)S(1)}, f32[2,256,256]{2,1,0:T(8,128)}, u32[]{:S(2)}, u32[]{:S(2)}) %collective-permute-start) | collective-permute-done | bytes 524320 | tf_op jit(solution)/shard_map/while/body/eval_jaxpr/ppermute | solution.py:35
  112.7 1.1 broadcast_select_fusion.2
  113.9 1.1 add.686
  115.0 1.1 fusion.78
  116.2 1.9 collective-permute-start
  118.1 13.2 %collective-permute-done = f32[2,256,256]{2,1,0:T(8,128)} collective-permute-done((f32[2,256,256]{2,1,0:T(8,128)S(1)}, f32[2,256,256]{2,1,0:T(8,128)}, u32[]{:S(2)}, u32[]{:S(2)}) %collective-permute-start) | collective-permute-done | bytes 524320 | tf_op jit(solution)/shard_map/while/body/eval_jaxpr/ppermute | solution.py:35
  131.3 1.1 broadcast_select_fusion.2
  132.4 1.1 add.686
  133.5 1.1 fusion.78
  134.7 1.9 collective-permute-start
  136.6 12.3 %collective-permute-done = f32[2,256,256]{2,1,0:T(8,128)} collective-permute-done((f32[2,256,256]{2,1,0:T(8,128)S(1)}, f32[2,256,256]{2,1,0:T(8,128)}, u32[]{:S(2)}, u32[]{:S(2)}) %collective-permute-start) | collective-permute-done | bytes 524320 | tf_op jit(solution)/shard_map/while/body/eval_jaxpr/ppermute | solution.py:35
  149.0 1.1 broadcast_select_fusion.2
  150.1 1.1 add.686
  151.2 1.1 fusion.78
  152.4 1.9 collective-permute-start
  154.3 11.5 %collective-permute-done = f32[2,256,256]{2,1,0:T(8,128)} collective-permute-done((f32[2,256,256]{2,1,0:T(8,128)S(1)}, f32[2,256,256]{2,1,0:T(8,128)}, u32[]{:S(2)}, u32[]{:S(2)}) %collective-permute-start) | collective-permute-done | bytes 524320 | tf_op jit(solution)/shard_map/while/body/eval_jaxpr/ppermute | solution.py:35
  165.8 1.1 broadcast_select_fusion.2
  166.9 1.1 add.686
  168.0 1.1 fusion.78
  169.2 1.9 collective-permute-start
  171.1 10.6 %collective-permute-done = f32[2,256,256]{2,1,0:T(8,128)} collective-permute-done((f32[2,256,256]{2,1,0:T(8,128)S(1)}, f32[2,256,256]{2,1,0:T(8,128)}, u32[]{:S(2)}, u32[]{:S(2)}) %collective-permute-start) | collective-permute-done | bytes 524320 | tf_op jit(solution)/shard_map/while/body/eval_jaxpr/ppermute | solution.py:35
  181.8 1.1 broadcast_select_fusion.2
  182.9 1.2 add.374
  184.1 1.3 divide_bitcast_fusion.1
  186.0 2.1 collective-permute-start.7
  188.5 2.3 maximum_bitcast_fusion
  190.8 40.6 %collective-permute-done.7 = f32[2,256,1024]{2,1,0:T(8,128)S(1)} collective-permute-done((f32[2,256,1024]{2,1,0:T(8,128)S(1)}, f32[2,256,1024]{2,1,0:T(8,128)S(1)}, u32[]{:S(2)}, u32[]{:S(2)}) %collective-permute-start.7) | collective-permute-done | bytes 2097184 | tf_op jit(solution)/shard_map/ppermute | solution.py:35
  231.4 1.7 select_bitcast_fusion
  (74 shorter events, 6.1 us)
Async XLA Ops:
  0.6 2.9 %copy-start = (f32[1,2,256,1024]{3,2,1,0:T(8,128)S(1)}, f32[1,2,256,1024]{3,2,1,0:T(8,128)}, u32[]{:S(2)}) copy-start(f32[1,2,256,1024]{3,2,1,0:T(8,128)} %param.4) | copy-start | bytes 6291460
  3.3 1.3 copy-start.9
  3.3 2.0 copy-start.10
  5.3 9.5 %collective-permute-start.2 = (f32[3,2,1,1024]{3,2,1,0:T(1,128)S(1)}, f32[3,2,1,1024]{3,2,1,0:T(1,128)S(1)}, u32[]{:S(2)}, u32[]{:S(2)}) collective-permute-start(f32[3,2,1,1024]{3,2,1,0:T(1,128)S(1)} %get-tuple-element.159), channel_id=1, source_target_pairs={{0,1},{1,2},{2,3},{4,5},{5,6},{6,7},{8,9},{9,10},{10,11},{12,13},{... | collective-permute-start | bytes 73736 | tf_op jit(solution)/shard_map/ppermute | solution.py:26
  7.1 7.7 %collective-permute-start.1 = (f32[3,2,1,1024]{3,2,1,0:T(1,128)S(1)}, f32[3,2,1,1024]{3,2,1,0:T(1,128)S(1)}, u32[]{:S(2)}, u32[]{:S(2)}) collective-permute-start(f32[3,2,1,1024]{3,2,1,0:T(1,128)S(1)} %get-tuple-element.158), channel_id=1, source_target_pairs={{1,0},{2,1},{3,2},{5,4},{6,5},{7,6},{9,8},{10,9},{11,10},{13,12},{... | collective-permute-start | bytes 73736 | tf_op jit(solution)/shard_map/ppermute | solution.py:27
  14.7 7.7 %copy-start.11 = (f32[256,1024]{1,0:T(8,128)}, f32[256,1024]{1,0:T(8,128)S(1)}, u32[]{:S(2)}) copy-start(f32[256,1024]{1,0:T(8,128)S(1)} %add_multiply_fusion.11) | copy-start | bytes 3145732
  14.8 7.7 %copy-start.12 = (f32[256,1024]{1,0:T(8,128)S(1)}, f32[256,1024]{1,0:T(8,128)}, u32[]{:S(2)}) copy-start(f32[256,1024]{1,0:T(8,128)} %broadcast_add_fusion) | copy-start | bytes 3145732
  25.0 1.4 copy-start.17
  25.0 1.5 copy-start.18
  28.7 13.7 %copy-start.5 = (f32[1,256,1024]{2,1,0:T(8,128)}, f32[1,256,1024]{2,1,0:T(8,128)S(1)}, u32[]{:S(2)}) copy-start(f32[1,256,1024]{2,1,0:T(8,128)S(1)} %get-tuple-element.145) | copy-start | bytes 3145732
  28.7 13.7 %copy-start.7 = (f32[1,256,1024]{2,1,0:T(8,128)}, f32[1,256,1024]{2,1,0:T(8,128)S(1)}, u32[]{:S(2)}) copy-start(f32[1,256,1024]{2,1,0:T(8,128)S(1)} %get-tuple-element.146) | copy-start | bytes 3145732
  29.0 6.0 %collective-permute-start.4 = (f32[1,2,1,1024]{3,2,1,0:T(1,128)S(1)}, f32[1,2,1,1024]{3,2,1,0:T(1,128)S(1)}, u32[]{:S(2)}, u32[]{:S(2)}) collective-permute-start(f32[1,2,1,1024]{3,2,1,0:T(1,128)S(1)} %get-tuple-element.182), channel_id=1, source_target_pairs={{0,1},{1,2},{2,3},{4,5},{5,6},{6,7},{8,9},{9,10},{10,11},{12,13},{... | collective-permute-start | bytes 24584 | tf_op jit(solution)/shard_map/ppermute | solution.py:26
  33.3 4.3 %collective-permute-start.3 = (f32[1,2,1,1024]{3,2,1,0:T(1,128)S(1)}, f32[1,2,1,1024]{3,2,1,0:T(1,128)S(1)}, u32[]{:S(2)}, u32[]{:S(2)}) collective-permute-start(f32[1,2,1,1024]{3,2,1,0:T(1,128)S(1)} %get-tuple-element.181), channel_id=1, source_target_pairs={{1,0},{2,1},{3,2},{5,4},{6,5},{7,6},{9,8},{10,9},{11,10},{13,12},{... | collective-permute-start | bytes 24584 | tf_op jit(solution)/shard_map/ppermute | solution.py:27
  38.0 1.2 copy-start.15
  38.0 1.5 copy-start.16
  42.2 6.6 %copy-start.1 = (f32[1,256,1024]{2,1,0:T(8,128)}, f32[1,256,1024]{2,1,0:T(8,128)S(1)}, u32[]{:S(2)}) copy-start(f32[1,256,1024]{2,1,0:T(8,128)S(1)} %get-tuple-element.148) | copy-start | bytes 3145732
  42.2 6.6 %copy-start.3 = (f32[1,256,1024]{2,1,0:T(8,128)}, f32[1,256,1024]{2,1,0:T(8,128)S(1)}, u32[]{:S(2)}) copy-start(f32[1,256,1024]{2,1,0:T(8,128)S(1)} %get-tuple-element.149) | copy-start | bytes 3145732
  43.0 8.4 %collective-permute-start.6 = (f32[1,2,1,1024]{3,2,1,0:T(1,128)S(1)}, f32[1,2,1,1024]{3,2,1,0:T(1,128)S(1)}, u32[]{:S(2)}, u32[]{:S(2)}) collective-permute-start(f32[1,2,1,1024]{3,2,1,0:T(1,128)S(1)} %get-tuple-element.178), channel_id=1, source_target_pairs={{0,1},{1,2},{2,3},{4,5},{5,6},{6,7},{8,9},{9,10},{10,11},{12,13},{... | collective-permute-start | bytes 24584 | tf_op jit(solution)/shard_map/ppermute | solution.py:26
  47.3 4.1 %collective-permute-start.5 = (f32[1,2,1,1024]{3,2,1,0:T(1,128)S(1)}, f32[1,2,1,1024]{3,2,1,0:T(1,128)S(1)}, u32[]{:S(2)}, u32[]{:S(2)}) collective-permute-start(f32[1,2,1,1024]{3,2,1,0:T(1,128)S(1)} %get-tuple-element.177), channel_id=1, source_target_pairs={{1,0},{2,1},{3,2},{5,4},{6,5},{7,6},{9,8},{10,9},{11,10},{13,12},{... | collective-permute-start | bytes 24584 | tf_op jit(solution)/shard_map/ppermute | solution.py:27
  49.0 2.1 copy-start.13
  55.6 17.5 %collective-permute-start = (f32[2,256,256]{2,1,0:T(8,128)S(1)}, f32[2,256,256]{2,1,0:T(8,128)}, u32[]{:S(2)}, u32[]{:S(2)}) collective-permute-start(f32[2,256,256]{2,1,0:T(8,128)S(1)} %pad_maximum_fusion.20), channel_id=1, source_target_pairs={{0,4},{4,8},{8,12},{12,16},{16,20},{20,24},{24,28},{1,5},{5,9},{9,... | collective-permute-start | bytes 1572872 | tf_op jit(solution)/shard_map/while/body/eval_jaxpr/ppermute | solution.py:35
  76.5 16.8 %collective-permute-start = (f32[2,256,256]{2,1,0:T(8,128)S(1)}, f32[2,256,256]{2,1,0:T(8,128)}, u32[]{:S(2)}, u32[]{:S(2)}) collective-permute-start(f32[2,256,256]{2,1,0:T(8,128)S(1)} %pad_maximum_fusion.20), channel_id=1, source_target_pairs={{0,4},{4,8},{8,12},{12,16},{16,20},{20,24},{24,28},{1,5},{5,9},{9,... | collective-permute-start | bytes 1572872 | tf_op jit(solution)/shard_map/while/body/eval_jaxpr/ppermute | solution.py:35
  96.8 16.0 %collective-permute-start = (f32[2,256,256]{2,1,0:T(8,128)S(1)}, f32[2,256,256]{2,1,0:T(8,128)}, u32[]{:S(2)}, u32[]{:S(2)}) collective-permute-start(f32[2,256,256]{2,1,0:T(8,128)S(1)} %pad_maximum_fusion.20), channel_id=1, source_target_pairs={{0,4},{4,8},{8,12},{12,16},{16,20},{20,24},{24,28},{1,5},{5,9},{9,... | collective-permute-start | bytes 1572872 | tf_op jit(solution)/shard_map/while/body/eval_jaxpr/ppermute | solution.py:35
  116.2 15.1 %collective-permute-start = (f32[2,256,256]{2,1,0:T(8,128)S(1)}, f32[2,256,256]{2,1,0:T(8,128)}, u32[]{:S(2)}, u32[]{:S(2)}) collective-permute-start(f32[2,256,256]{2,1,0:T(8,128)S(1)} %pad_maximum_fusion.20), channel_id=1, source_target_pairs={{0,4},{4,8},{8,12},{12,16},{16,20},{20,24},{24,28},{1,5},{5,9},{9,... | collective-permute-start | bytes 1572872 | tf_op jit(solution)/shard_map/while/body/eval_jaxpr/ppermute | solution.py:35
  134.7 14.3 %collective-permute-start = (f32[2,256,256]{2,1,0:T(8,128)S(1)}, f32[2,256,256]{2,1,0:T(8,128)}, u32[]{:S(2)}, u32[]{:S(2)}) collective-permute-start(f32[2,256,256]{2,1,0:T(8,128)S(1)} %pad_maximum_fusion.20), channel_id=1, source_target_pairs={{0,4},{4,8},{8,12},{12,16},{16,20},{20,24},{24,28},{1,5},{5,9},{9,... | collective-permute-start | bytes 1572872 | tf_op jit(solution)/shard_map/while/body/eval_jaxpr/ppermute | solution.py:35
  152.4 13.4 %collective-permute-start = (f32[2,256,256]{2,1,0:T(8,128)S(1)}, f32[2,256,256]{2,1,0:T(8,128)}, u32[]{:S(2)}, u32[]{:S(2)}) collective-permute-start(f32[2,256,256]{2,1,0:T(8,128)S(1)} %pad_maximum_fusion.20), channel_id=1, source_target_pairs={{0,4},{4,8},{8,12},{12,16},{16,20},{20,24},{24,28},{1,5},{5,9},{9,... | collective-permute-start | bytes 1572872 | tf_op jit(solution)/shard_map/while/body/eval_jaxpr/ppermute | solution.py:35
  169.2 12.6 %collective-permute-start = (f32[2,256,256]{2,1,0:T(8,128)S(1)}, f32[2,256,256]{2,1,0:T(8,128)}, u32[]{:S(2)}, u32[]{:S(2)}) collective-permute-start(f32[2,256,256]{2,1,0:T(8,128)S(1)} %pad_maximum_fusion.20), channel_id=1, source_target_pairs={{0,4},{4,8},{8,12},{12,16},{16,20},{20,24},{24,28},{1,5},{5,9},{9,... | collective-permute-start | bytes 1572872 | tf_op jit(solution)/shard_map/while/body/eval_jaxpr/ppermute | solution.py:35
  182.9 2.5 %copy-start.14 = (f32[2,256,256]{2,1,0:T(8,128)S(1)}, f32[2,256,256]{2,1,0:T(8,128)}, u32[]{:S(2)}) copy-start(f32[2,256,256]{2,1,0:T(8,128)} %copy-done.13) | copy-start | bytes 1572868
  184.1 1.5 copy-start.2
  184.1 1.7 copy-start.4
  186.0 2.3 copy-start.6
  186.0 2.3 copy-start.8
  186.0 45.4 %collective-permute-start.7 = (f32[2,256,1024]{2,1,0:T(8,128)S(1)}, f32[2,256,1024]{2,1,0:T(8,128)S(1)}, u32[]{:S(2)}, u32[]{:S(2)}) collective-permute-start(f32[2,256,1024]{2,1,0:T(8,128)S(1)} %pad_add_fusion), channel_id=1, source_target_pairs={{0,4},{4,8},{8,12},{12,16},{16,20},{20,24},{24,28},{1,5},{5,9},{9,... | collective-permute-start | bytes 6291464 | tf_op jit(solution)/shard_map/ppermute | solution.py:35
where the time goes:
time: 235 us; the launch traced here: 233 us
  waiting for transfers between devices  133 us (57%)
  other arithmetic  59.9 us (25%)
  starting transfers between devices  32 us (14%)
  local copies, waits for them, and re-layouts  6.28 us (3%)
    ppermute x8, waiting for transfers between devices, from_behind(): lax.ppermute(value, axis, [(source, source + steps) for source in range(f...  131 us
    ppermute x8, starting transfers between devices, from_behind(): lax.ppermute(value, axis, [(source, source + steps) for source in range(f...  17.6 us
    ppermute x3, starting transfers between devices, with_halo(): before = lax.ppermute(last, axis, up)  10.3 us
    sub x4, other arithmetic, multiply(): real_rate * field[..., 0, :, :] - imag_rate * field[..., 1, :, :]  8.57 us
    div x7, other arithmetic, divide(): (field[..., 0, :, :] * real_part + field[..., 1, :, :] * imag_part) / mod...  7.85 us
    add x7, other arithmetic, relay(): finish = divide(step_real, step_imag, begin_now + offset)  7.77 us
    select_n x7, other arithmetic, relay(): return jnp.where(leader, begin_coarse, incoming)  7.77 us
    another operation x1, other arithmetic, body(): stacked = jnp.stack([begin_value, old_nodes[0], old_nodes[1]])  7.62 us
  transfers between devices with their start and end apart: 14, of which 9 were waited for; matrix products, arithmetic and copies ran while one was open for 5% of the time, Pallas kernels for 0%

commit v1 on v0

v1 whole, which is shorter than its diff:
```python
import functools

import jax
import jax.numpy as jnp
from jax import lax
from jax.experimental import pallas as pl
from jax.experimental.pallas import tpu as pltpu
from jax.sharding import PartitionSpec as P

COARSE_SHARE = 4
LANES = 128
STRIP = 32
HALO = 4
PAD = 8

diffusion = 1.5
drift = 0.8
shear = 0.6


def rates(row_start, rows, column_start, columns, size_x, size_y):
    row = row_start + lax.broadcasted_iota(jnp.int32, (rows, columns), 0)
    column = column_start + lax.broadcasted_iota(jnp.int32, (rows, columns), 1)
    along = (row.astype(jnp.float32) - size_x // 2) * (2.0 / size_x)
    across = (column.astype(jnp.float32) - size_y // 2) * (2.0 / size_y)
    real = -diffusion * (along * along + across * across)
    return real, -drift * across, shear * across


def turned(real, imag, first, second):
    return real * first - imag * second, real * second + imag * first


def fine_kernel(*refs, blocks, first_block, coarse, size_x, size_y, coarse_rows, pieces, aliased):
    begin, old, before, after = refs[:4]
    refs = refs[4 + aliased:]
    nodes, refs = refs[0], refs[1:]
    sends, refs = refs[: len(pieces)], refs[len(pieces):]
    offset = None
    if coarse:
        offset, refs = refs[0], refs[1:]
    wide_one, wide_two, inner, inverse = refs
    rows = begin.shape[1]
    rank = lax.axis_index("space")
    ranks = lax.axis_size("space")
    block = first_block + pl.program_id(0)
    row_base = rank * rows
    column_base = block * LANES
    has_before = rank > 0
    has_after = rank < ranks - 1
    tiles = [("in", start, min(STRIP, rows - start)) for start in range(0, rows, STRIP)]
    tiles = [("before", -HALO, HALO)] + tiles + [("after", rows, HALO)]

    def fields(kind, start, count):
        if kind == "in":
            here = pl.ds(start, count)
            return ([begin[0, here, :], begin[1, here, :]],
                    [old[0, 0, here, :], old[0, 1, here, :]],
                    [old[1, 0, here, :], old[1, 1, here, :]])
        side = before if kind == "before" else after
        return ([side[0], side[1]], [side[2], side[3]], [side[4], side[5]])

    def kept(kind, value):
        if kind == "before":
            return jnp.where(has_before, value, 0.0)
        if kind == "after":
            return jnp.where(has_after, value, 0.0)
        return value

    def sums(ref, part, start, count):
        return ref[part, pl.ds(PAD + start - 1, count), :] + ref[part, pl.ds(PAD + start + 1, count), :]

    for kind, start, count in tiles:
        b, one, two = fields(kind, start, count)
        for part in range(2):
            third = (1.0 / 3.0) * one[part]
            wide_one[part, pl.ds(PAD + start, count), :] = (5.0 / 24.0) * b[part] + third - (1.0 / 24.0) * two[part]
            wide_two[part, pl.ds(PAD + start, count), :] = third - (1.0 / 24.0) * b[part] + (5.0 / 24.0) * two[part] - 0.5 * one[part]
    for kind, start, count in tiles:
        real, imag, factor = rates(row_base + start, count, column_base, LANES, size_x, size_y)
        b, one, _ = fields(kind, start, count)
        here = pl.ds(PAD + start, count)
        u = [wide_one[part, here, :] - 0.5 * one[part] for part in range(2)]
        lu = turned(real, imag, u[0], u[1])
        top = (b[0] + lu[0] + factor * sums(wide_one, 1, start, count),
               b[1] + lu[1] - factor * sums(wide_one, 0, start, count))
        half_real = 1.0 - 0.5 * real
        half_imag = -0.5 * imag
        share = 1.0 / (half_real * half_real + half_imag * half_imag)
        half_real = half_real * share
        half_imag = half_imag * share
        inverse[0, here, :] = half_real
        inverse[1, here, :] = half_imag
        node = (top[0] * half_real + top[1] * half_imag, top[1] * half_real - top[0] * half_imag)
        for part in range(2):
            value = kept(kind, node[part])
            if kind == "in":
                nodes[0, part, pl.ds(start, count), :] = value
            inner[part, here, :] = value
    for kind, start, count in tiles:
        here = pl.ds(PAD + start, count)
        for part in range(2):
            wide_one[part, here, :] = 0.5 * inner[part, here, :] + wide_two[part, here, :]
    for kind, start, count in tiles:
        if kind != "in" and not coarse:
            continue
        real, imag, factor = rates(row_base + start, count, column_base, LANES, size_x, size_y)
        b, one, two = fields(kind, start, count)
        here = pl.ds(PAD + start, count)
        u = [wide_two[part, here, :] + 0.5 * (one[part] - two[part]) for part in range(2)]
        lu = turned(real, imag, u[0], u[1])
        n1 = [inner[part, here, :] for part in range(2)]
        top = (n1[0] + lu[0] + factor * sums(wide_one, 1, start, count),
               n1[1] + lu[1] - factor * sums(wide_one, 0, start, count))
        half_real = inverse[0, here, :]
        half_imag = inverse[1, here, :]
        node = (top[0] * half_real + top[1] * half_imag, top[1] * half_real - top[0] * half_imag)
        for part in range(2):
            value = kept(kind, node[part])
            if kind == "in":
                nodes[1, part, pl.ds(start, count), :] = value
                for (low, high), send in zip(pieces, sends):
                    a, z = max(low, start), min(high, start + count)
                    if a < z:
                        send[part, pl.ds(a - low, z - a), :] = value[a - start:z - start]
            if coarse:
                inner[part, here, :] = (1.0 / 6.0) * b[part] + (2.0 / 3.0) * n1[part] + (1.0 / 6.0) * value
    if coarse:
        def offsets(shift):
            for start in range(0, coarse_rows, STRIP):
                count = min(STRIP, coarse_rows - start)
                at = shift + start
                real, imag, factor = rates(row_base + at, count, column_base, LANES, size_x, size_y)
                v = [inner[part, pl.ds(PAD + at, count), :] for part in range(2)]
                e = [nodes[1, part, pl.ds(at, count), :] for part in range(2)]
                lu = turned(real, imag, v[0] - e[0], v[1] - e[1])
                off = (lu[0] + factor * sums(inner, 1, at, count),
                       lu[1] - factor * sums(inner, 0, at, count))
                step_real = 1.0 - real
                step_imag = -imag
                share = 1.0 / (step_real * step_real + step_imag * step_imag)
                lead = lax.axis_index("tm") == 0
                off = tuple(off[part] + jnp.where(lead, begin[part, pl.ds(at, count), :], 0.0) for part in range(2))
                offset[0, pl.ds(start, count), :] = (off[0] * step_real + off[1] * step_imag) * share
                offset[1, pl.ds(start, count), :] = (off[1] * step_real - off[0] * step_imag) * share

        low_shift = rows - coarse_rows
        if low_shift == 0:
            offsets(0)
        else:
            upper = rank >= ranks // 2

            @pl.when(upper)
            def _():
                offsets(0)

            @pl.when(jnp.logical_not(upper))
            def _():
                offsets(low_shift)


def fine_call(begin, old, before, after, nodes, first, width, coarse, pieces, size_x, coarse_rows):
    rows, columns = begin.shape[1:]
    blocks = width // LANES
    base = first // LANES
    f32 = jnp.float32
    out_shape = [jax.ShapeDtypeStruct((2, 2, rows, columns), f32)]
    out_specs = [pl.BlockSpec((2, 2, rows, LANES), lambda j: (0, 0, 0, base + j))]
    for low, high in pieces:
        out_shape.append(jax.ShapeDtypeStruct((2, high - low, width), f32))
        out_specs.append(pl.BlockSpec((2, high - low, LANES), lambda j: (0, 0, j)))
    if coarse:
        out_shape.append(jax.ShapeDtypeStruct((2, coarse_rows, width), f32))
        out_specs.append(pl.BlockSpec((2, coarse_rows, LANES), lambda j: (0, 0, j)))
    in_specs = [
        pl.BlockSpec((2, rows, LANES), lambda j: (0, 0, base + j)),
        pl.BlockSpec((2, 2, rows, LANES), lambda j: (0, 0, 0, base + j)),
        pl.BlockSpec((6, HALO, LANES), lambda j: (0, 0, base + j)),
        pl.BlockSpec((6, HALO, LANES), lambda j: (0, 0, base + j)),
    ]
    operands = [begin, old, before, after]
    aliases = {}
    if nodes is not None:
        operands.append(nodes)
        in_specs.append(pl.BlockSpec(memory_space=pl.ANY))
        aliases = {4: 0}
    kernel = functools.partial(
        fine_kernel, blocks=blocks, first_block=base, coarse=coarse, size_x=size_x, size_y=columns,
        coarse_rows=coarse_rows, pieces=pieces, aliased=len(aliases))
    scratch = [pltpu.VMEM((2, rows + 2 * PAD, LANES), f32) for _ in range(4)]
    return pl.pallas_call(
        kernel, grid=(blocks,), in_specs=in_specs, out_specs=out_specs, out_shape=out_shape,
        scratch_shapes=scratch, input_output_aliases=aliases, name="fine_coarse" if coarse else "fine",
    )(*operands)


def place_kernel(*refs, targets, patch, aliased, coarse_rows, low_column):
    count = len(targets)
    begin = refs[0]
    arrived = refs[1:1 + count]
    refs = refs[1 + count:]
    rank = lax.axis_index("space")
    ranks = lax.axis_size("space")
    lead = lax.axis_index("tm") == 0
    if patch:
        fresh, finish = refs[:2]
        refs = refs[3 + aliased:]
        start, nodes, sems, block_begin, block_nodes, fixed = refs
    else:
        start, sems = refs[aliased:]
    rows = begin.shape[1]
    if patch:
        shift = jnp.where(rank >= ranks // 2, 0, rows - coarse_rows)
        middle = jnp.logical_or(rank == ranks // 2, rank == ranks // 2 - 1)
        shift = pl.multiple_of(shift, 8)
        width = fresh.shape[2]
        spot = (slice(None), pl.ds(shift, coarse_rows), pl.ds(low_column, width))
        loads = [pltpu.make_async_copy(begin.at[spot], block_begin, sems.at[count]),
                 pltpu.make_async_copy(nodes.at[(slice(None),) + spot], block_nodes, sems.at[count + 1])]

        @pl.when(middle)
        def _():
            for copy in loads:
                copy.start()

    copies = []
    for k, (low, high, first, width_k, skip) in enumerate(targets):
        where = (slice(None), pl.ds(low, high - low), pl.ds(first, width_k))
        own = pltpu.make_async_copy(begin.at[where], start.at[where], sems.at[k])
        moved = pltpu.make_async_copy(arrived[k], start.at[where], sems.at[k])
        live = jnp.bool_(True)
        for other in skip:
            live = jnp.logical_and(live, rank != other)
        copies.append((own, moved, live))

        @pl.when(lead)
        def _():
            own.start()

        @pl.when(jnp.logical_and(jnp.logical_not(lead), live))
        def _():
            moved.start()

    if patch:
        @pl.when(middle)
        def _():
            for copy in loads:
                copy.wait()
            for part in range(2):
                old_begin = block_begin[part]
                n1 = block_nodes[0, part]
                n2 = block_nodes[1, part]
                now = jnp.where(lead, old_begin, fresh[part])
                end = finish[part]
                change = end - n2
                fixed[0, part] = n1 + 0.5 * ((now - old_begin) + change)
                fixed[1, part] = n2 + change
                block_begin[part] = now
            store = pltpu.make_async_copy(fixed, nodes.at[(slice(None),) + spot], sems.at[count])
            store.start()

            @pl.when(jnp.logical_not(lead))
            def _():
                put = pltpu.make_async_copy(block_begin, start.at[spot], sems.at[count + 1])
                put.start()
                put.wait()

            store.wait()

    for own, moved, live in copies:
        @pl.when(jnp.logical_or(lead, live))
        def _():
            own.wait()


def place_call(begin, arrived, targets, start, coarse_part, nodes, coarse_rows, low_column):
    f32 = jnp.float32
    anywhere = pl.BlockSpec(memory_space=pl.ANY)
    vmem = pl.BlockSpec(memory_space=pltpu.VMEM)
    operands = [begin] + list(arrived)
    in_specs = [anywhere] * len(operands)
    out_shape = [jax.ShapeDtypeStruct(begin.shape, f32)]
    out_specs = [anywhere]
    scratch = []
    aliases = {}
    patch = coarse_part is not None
    if patch:
        operands += list(coarse_part) + [nodes]
        in_specs += [vmem, vmem, anywhere]
        out_shape.append(jax.ShapeDtypeStruct(nodes.shape, f32))
        out_specs.append(anywhere)
        aliases[len(operands) - 1] = 1
        block = (2,) + coarse_part[0].shape[1:]
        scratch = [pltpu.VMEM(block, f32), pltpu.VMEM((2,) + block, f32), pltpu.VMEM((2,) + block, f32)]
    aliased = 0
    if start is not None:
        aliases[len(operands)] = 0
        operands.append(start)
        in_specs.append(anywhere)
        aliased = 1
    kernel = functools.partial(place_kernel, targets=targets, patch=patch, aliased=aliased,
                               coarse_rows=coarse_rows, low_column=low_column)
    return pl.pallas_call(
        kernel, in_specs=in_specs, out_specs=out_specs, out_shape=out_shape,
        scratch_shapes=[pltpu.SemaphoreType.DMA((len(targets) + 2,))] + scratch,
        input_output_aliases=aliases, name="place_patch" if patch else "place",
    )(*operands)


def powers(row_base, rows, low_column, width, size_x, size_y):
    real, imag, _ = rates(row_base, rows, low_column, width, size_x, size_y)
    step_real = 1.0 - real
    step_imag = -imag
    share = 1.0 / (step_real * step_real + step_imag * step_imag)
    return step_real * share, -step_imag * share


def body(start_values, node_values):
    begin = start_values[0]
    old = node_values[0]
    rows, columns = begin.shape[1:]
    slices, ranks = lax.axis_size("tm"), lax.axis_size("space")
    size_x = rows * ranks
    width = columns // COARSE_SHARE
    low_column = columns // 2 - width // 2
    coarse_rows = min(rows, size_x // COARSE_SHARE // 2)
    lower, upper = ranks // 2 - 1, ranks // 2
    rank = lax.axis_index("space")
    lead = lax.axis_index("tm") == 0

    def edge(low):
        cut = [begin[:, low:low + HALO], old[0, :, low:low + HALO], old[1, :, low:low + HALO]]
        return jnp.concatenate(cut, axis=0)

    up = [(i, i + 1) for i in range(ranks - 1)]
    before = lax.ppermute(edge(rows - HALO), "space", up)
    after = lax.ppermute(edge(0), "space", [(j, i) for i, j in up])

    def ahead(value, steps, members):
        pairs = [(n * ranks + s, (n + steps) * ranks + s) for n in range(slices - steps) for s in members]
        return lax.ppermute(value, ("tm", "space"), pairs)

    everyone = range(ranks)
    middle = (lower, upper)
    if rows == coarse_rows:
        pieces = [(0, rows)]
        holders = [[s for s in everyone if s not in middle]]
    else:
        cuts = [0, coarse_rows, rows - coarse_rows, rows]
        pieces = [(a, b) for a, b in zip(cuts, cuts[1:]) if a < b]
        holders = [[s for s in everyone
                    if not (s == upper and b <= coarse_rows) and not (s == lower and a >= rows - coarse_rows)]
                   for a, b in pieces]
    made = fine_call(begin, old, before, after, None, low_column, width, True, pieces, size_x, coarse_rows)
    nodes, inner_sends, offset = made[0], made[1:-1], made[-1]
    one_back = ahead(offset, 1, middle)
    two_back = ahead(offset, 2, middle)
    rest = columns - low_column - width
    nodes, left = fine_call(begin, old, before, after, nodes, 0, low_column, False, [(0, rows)], size_x, coarse_rows)
    left = ahead(left, 1, everyone)
    nodes, right = fine_call(begin, old, before, after, nodes, low_column + width, rest, False, [(0, rows)], size_x, coarse_rows)

    shift = jnp.where(rank >= ranks // 2, 0, rows - coarse_rows)
    d_real, d_imag = powers(rank * rows + shift, coarse_rows, low_column, width, size_x, columns)

    def add(total, field, real, imag):
        grown = turned(real, imag, field[0], field[1])
        return jnp.stack([total[0] + grown[0], total[1] + grown[1]])

    total = add(one_back, two_back, d_real, d_imag)
    inner = [ahead(piece, 1, members) for piece, members in zip(inner_sends, holders)]
    right = ahead(right, 1, everyone)
    power = turned(d_real, d_imag, d_real, d_imag)
    reach = 2
    while reach < slices:
        total = add(total, ahead(total, reach, middle), *power)
        power = turned(power[0], power[1], power[0], power[1])
        reach *= 2
    end = add(offset, jnp.where(lead, 0.0, total), d_real, d_imag)
    targets = [(a, b, low_column, width, tuple(s for s in everyone if s not in members))
               for (a, b), members in zip(pieces, holders)]
    arrived = list(inner)
    targets.append((0, rows, 0, low_column, ()))
    arrived.append(left)
    next_start, nodes = place_call(begin, arrived, targets, None, (total, end), nodes, coarse_rows, low_column)
    (next_start,) = place_call(begin, [right], [(0, rows, low_column + width, rest, ())], next_start,
                               None, None, coarse_rows, low_column)
    return next_start[None], nodes[None]


def solution(mesh):
    in_specs = (P("tm", None, "space", None), P("tm", None, None, "space", None))
    out_specs = (P("tm", None, "space", None), P("tm", None, None, "space", None))
    return jax.shard_map(body, mesh=mesh, in_specs=in_specs, out_specs=out_specs, check_vma=False)
```

time: 235 us -> 142 us (0.60)
  the two profiles are of different devices: /device:TPU:8 before, /device:TPU:2 now
where the time goes in v1:
time: 142 us
  Pallas kernels  79.1 us (56%)
  starting transfers between devices  34.4 us (24%)
  waiting for transfers between devices  20.8 us (15%)
  local copies, waits for them, and re-layouts  4.41 us (3%)
  other arithmetic  2.22 us (2%)
    pallas_call x2, Pallas kernels, place_call(): pl.pallas_call(kernel, in_specs=in_specs, out_specs=out_specs, out_shape=...  66.8 us
    ppermute x8, starting transfers between devices, ahead(): return lax.ppermute(value, ('tm', 'space'), pairs)  28.9 us
    ppermute x8, waiting for transfers between devices, ahead(): return lax.ppermute(value, ('tm', 'space'), pairs)  18.6 us
    pallas_call x3, Pallas kernels, fine_call(): pl.pallas_call(kernel, grid=(blocks,), in_specs=in_specs, out_specs=out_s...  12.3 us
    ppermute x1, starting transfers between devices, body(): after = lax.ppermute(edge(0), 'space', [(j, i) for i, j in up])  3.64 us
  transfers between devices with their start and end apart: 10, of which 6 were waited for; matrix products, arithmetic and copies ran while one was open for 1% of the time, Pallas kernels for 36%

profile of v1, /device:TPU:2, one launch (start us, length us, event | category | flops | bytes accessed | tf_op | source)
XLA Modules:
  0.0 141.8 jit_solution(16988820447884472685)
XLA Ops:
  0.6 0.9 fusion.3
  1.5 1.0 slice_bitcast_fusion.1
  2.5 1.9 %collective-permute-start = (f32[6,4,1024]{2,1,0:T(4,128)S(1)}, f32[6,4,1024]{2,1,0:T(4,128)S(1)}, u32[]{:S(2)}, u32[]{:S(2)}) collective-permute-start(f32[6,4,1024]{2,1,0:T(4,128)S(1)} %pad_maximum_fusion.4), channel_id=1, source_target_pairs={{0,1},{1,2},{2,3},{4,5},{5,6},{6,7},{8,9},{9,10},{10,11},{12,13},{... | collective-permute-start | bytes 294920 | tf_op jit(solution)/shard_map/ppermute | solution.py:336
  4.5 3.6 %collective-permute-start.1 = (f32[6,4,1024]{2,1,0:T(4,128)S(1)}, f32[6,4,1024]{2,1,0:T(4,128)S(1)}, u32[]{:S(2)}, u32[]{:S(2)}) collective-permute-start(f32[6,4,1024]{2,1,0:T(4,128)S(1)} %pad_maximum_fusion.5), channel_id=1, source_target_pairs={{1,0},{2,1},{3,2},{5,4},{6,5},{7,6},{9,8},{10,9},{11,10},{13,12},{... | collective-permute-start | bytes 294920 | tf_op jit(solution)/shard_map/ppermute | solution.py:337
  8.1 0.3 collective-permute-done.refs_2_
  8.5 0.0 copy-start
  8.5 1.9 %collective-permute-done.1.refs_3_ = f32[6,4,1024]{2,1,0:T(4,128)S(1)} collective-permute-done((f32[6,4,1024]{2,1,0:T(4,128)S(1)}, f32[6,4,1024]{2,1,0:T(4,128)S(1)}, u32[]{:S(2)}, u32[]{:S(2)}) %collective-permute-start.1) | collective-permute-done | bytes 98336 | tf_op jit(solution)/shard_map/ppermute | solution.py:337
  10.3 0.0 copy-done
  10.3 0.0 copy-start.1
  10.3 0.6 copy-done.1
  11.0 3.3 %fine_coarse.1 = (f32[2,2,256,1024]{3,2,1,0:T(8,128)}, f32[2,128,256]{2,1,0:T(8,128)}, f32[2,128,256]{2,1,0:T(8,128)}, f32[2,128,256]{2,1,0:T(8,128)}) custom-call(f32[2,256,1024]{2,1,0:T(8,128)} %bitcast.13, f32[2,2,256,1024]{3,2,1,0:T(8,128)} %bitcast.19, f32[6,4,1024]{2,1,0:T(4,128)} %copy-done, f32[6,4,1024]{2,1,0:T(4,128)} %copy-done.1), custom_call_target="tpu_custom_call" | custom-call | tf_op jit(solution)/shard_map/fine_coarse/pallas_call | solution.py:191
  14.2 3.5 %collective-permute-start.7 = (f32[2,128,256]{2,1,0:T(8,128)}, f32[2,128,256]{2,1,0:T(8,128)S(1)}, u32[]{:S(2)}, u32[]{:S(2)}) collective-permute-start(f32[2,128,256]{2,1,0:T(8,128)} %get-tuple-element.18), channel_id=1, source_target_pairs={{1,9},{2,10},{5,13},{6,14},{9,17},{10,18},{13,21},{14,22},{17,25},... | collective-permute-start | bytes 786440 | tf_op jit(solution)/shard_map/ppermute | solution.py:341
  17.7 3.4 %collective-permute-start.6 = (f32[2,128,256]{2,1,0:T(8,128)}, f32[2,128,256]{2,1,0:T(8,128)S(1)}, u32[]{:S(2)}, u32[]{:S(2)}) collective-permute-start(f32[2,128,256]{2,1,0:T(8,128)} %get-tuple-element.18), channel_id=1, source_target_pairs={{1,5},{2,6},{5,9},{6,10},{9,13},{10,14},{13,17},{14,18},{17,21},{1... | collective-permute-start | bytes 786440 | tf_op jit(solution)/shard_map/ppermute | solution.py:341
  21.2 0.7 collective-permute-done.7
  21.9 5.6 %collective-permute-done.6 = f32[2,128,256]{2,1,0:T(8,128)S(1)} collective-permute-done((f32[2,128,256]{2,1,0:T(8,128)}, f32[2,128,256]{2,1,0:T(8,128)S(1)}, u32[]{:S(2)}, u32[]{:S(2)}) %collective-permute-start.6) | collective-permute-done | bytes 262176 | tf_op jit(solution)/shard_map/ppermute | solution.py:341
  27.5 0.1 slice_add_fusion.1
  27.6 5.2 %collective-permute-start.8 = (f32[2,128,256]{2,1,0:T(8,128)S(1)}, f32[2,128,256]{2,1,0:T(8,128)S(1)}, u32[]{:S(2)}, u32[]{:S(2)}) collective-permute-start(f32[2,128,256]{2,1,0:T(8,128)S(1)} %pad_maximum_fusion), channel_id=1, source_target_pairs={{1,9},{2,10},{5,13},{6,14},{9,17},{10,18},{13,21},{14,22},{17,25},... | collective-permute-start | bytes 786440 | tf_op jit(solution)/shard_map/ppermute | solution.py:341
  32.9 3.9 %collective-permute-done.8 = f32[2,128,256]{2,1,0:T(8,128)S(1)} collective-permute-done((f32[2,128,256]{2,1,0:T(8,128)S(1)}, f32[2,128,256]{2,1,0:T(8,128)S(1)}, u32[]{:S(2)}, u32[]{:S(2)}) %collective-permute-start.8) | collective-permute-done | bytes 262176 | tf_op jit(solution)/shard_map/ppermute | solution.py:341
  36.7 0.2 subtract_add_fusion.2
  36.9 5.4 %collective-permute-start.9 = (f32[2,128,256]{2,1,0:T(8,128)S(1)}, f32[2,128,256]{2,1,0:T(8,128)S(1)}, u32[]{:S(2)}, u32[]{:S(2)}) collective-permute-start(f32[2,128,256]{2,1,0:T(8,128)S(1)} %pad_maximum_fusion.1), channel_id=1, source_target_pairs={{1,17},{2,18},{5,21},{6,22},{9,25},{10,26},{13,29},{14,30}} | collective-permute-start | bytes 786440 | tf_op jit(solution)/shard_map/ppermute | solution.py:341
  42.3 4.5 %fine.2 = (f32[2,2,256,1024]{3,2,1,0:T(8,128)}, f32[2,256,384]{2,1,0:T(8,128)}) custom-call(f32[2,256,1024]{2,1,0:T(8,128)} %bitcast.14, f32[2,2,256,1024]{3,2,1,0:T(8,128)} %bitcast.20, f32[6,4,1024]{2,1,0:T(4,128)} %copy-done, f32[6,4,1024]{2,1,0:T(4,128)} %copy-done.1, f32[2,2,256,1024]{3,2,1,0:T(8,128)} %get-tuple-element.12.refs_4_), custom_call_target="tpu_custom_call", output_to_operand_aliasing={{0}: (4, {})} | custom-call | tf_op jit(solution)/shard_map/fine/pallas_call | solution.py:191
  46.8 5.4 %collective-permute-start.5 = (f32[2,256,384]{2,1,0:T(8,128)}, f32[2,256,384]{2,1,0:T(8,128)S(1)}, u32[]{:S(2)}, u32[]{:S(2)}) collective-permute-start(f32[2,256,384]{2,1,0:T(8,128)} %get-tuple-element.17), channel_id=1, source_target_pairs={{0,4},{1,5},{2,6},{3,7},{4,8},{5,9},{6,10},{7,11},{8,12},{9,13},{1... | collective-permute-start | bytes 2359304 | tf_op jit(solution)/shard_map/ppermute | solution.py:341
  52.2 0.0 copy-start.7
  52.2 0.0 copy-start.6
  52.2 4.6 %fine.3 = (f32[2,2,256,1024]{3,2,1,0:T(8,128)}, f32[2,256,384]{2,1,0:T(8,128)}) custom-call(f32[2,256,1024]{2,1,0:T(8,128)} %bitcast.15, f32[2,2,256,1024]{3,2,1,0:T(8,128)} %bitcast.21, f32[6,4,1024]{2,1,0:T(4,128)} %copy-done, f32[6,4,1024]{2,1,0:T(4,128)} %copy-done.1, f32[2,2,256,1024]{3,2,1,0:T(8,128)} %get-tuple-element.13.refs_4_), custom_call_target="tpu_custom_call", output_to_operand_aliasing={{0}: (4, {})} | custom-call | tf_op jit(solution)/shard_map/fine/pallas_call | solution.py:191
  56.8 1.9 %collective-permute-start.2 = (f32[2,256,384]{2,1,0:T(8,128)}, f32[2,256,384]{2,1,0:T(8,128)S(1)}, u32[]{:S(2)}, u32[]{:S(2)}) collective-permute-start(f32[2,256,384]{2,1,0:T(8,128)} %get-tuple-element.14), channel_id=1, source_target_pairs={{0,4},{1,5},{2,6},{3,7},{4,8},{5,9},{6,10},{7,11},{8,12},{9,13},{1... | collective-permute-start | bytes 2359304 | tf_op jit(solution)/shard_map/ppermute | solution.py:341
  58.7 0.7 collective-permute-start.3
  59.4 0.0 copy-done.7
  59.4 3.3 %collective-permute-start.4 = (f32[2,128,256]{2,1,0:T(8,128)S(1)}, f32[2,128,256]{2,1,0:T(8,128)S(1)}, u32[]{:S(2)}, u32[]{:S(2)}) collective-permute-start(f32[2,128,256]{2,1,0:T(8,128)S(1)} %copy-done.7), channel_id=1, source_target_pairs={{0,4},{2,6},{3,7},{4,8},{6,10},{7,11},{8,12},{10,14},{11,15},{12,1... | collective-permute-start | bytes 786440 | tf_op jit(solution)/shard_map/ppermute | solution.py:341
  62.8 0.0 collective-permute-done.9
  62.8 0.2 subtract_add_fusion.1
  63.0 0.8 broadcast_select_fusion
  63.7 0.0 copy-done.6
  63.7 0.1 subtract_add_fusion
  63.9 0.7 pad_maximum_fusion.3.refs_5_
  64.6 0.0 collective-permute-done.3.refs_1_
  64.6 0.0 copy-start.4
  64.6 8.5 %collective-permute-done.4.refs_2_ = f32[2,128,256]{2,1,0:T(8,128)S(1)} collective-permute-done((f32[2,128,256]{2,1,0:T(8,128)S(1)}, f32[2,128,256]{2,1,0:T(8,128)S(1)}, u32[]{:S(2)}, u32[]{:S(2)}) %collective-permute-start.4) | collective-permute-done | bytes 262176 | tf_op jit(solution)/shard_map/ppermute | solution.py:341
  73.1 0.0 copy-start.5
  73.1 0.0 collective-permute-done.5.refs_3_
  73.1 0.0 copy-start.3
  73.1 0.0 copy-done.4
  73.1 0.7 copy-done.5
  73.8 0.3 copy-done.3
  74.1 41.9 %place_patch.1 = (f32[2,256,1024]{2,1,0:T(8,128)}, f32[2,2,256,1024]{3,2,1,0:T(8,128)}) custom-call(f32[2,256,1024]{2,1,0:T(8,128)} %bitcast.16, f32[2,128,256]{2,1,0:T(8,128)} %copy-done.4, f32[2,128,256]{2,1,0:T(8,128)} %copy-done.5, f32[2,256,384]{2,1,0:T(8,128)} %copy-done.3, ...), custom_call_target="tpu_custom_call", output_to_operand_aliasing={{1}: (6, {})} | custom-call | tf_op jit(solution)/shard_map/place_patch/pallas_call | solution.py:303
  116.0 0.0 collective-permute-done.2.refs_1_
  116.0 0.0 copy-start.2
  116.0 0.9 copy-done.2
  116.9 24.9 %place.1 = f32[2,256,1024]{2,1,0:T(8,128)} custom-call(f32[2,256,1024]{2,1,0:T(8,128)} %bitcast.17, f32[2,256,384]{2,1,0:T(8,128)} %copy-done.2, f32[2,256,1024]{2,1,0:T(8,128)} %get-tuple-element.20.refs_2_), custom_call_target="tpu_custom_call", output_to_operand_aliasing={{}: (2, {})} | custom-call | tf_op jit(solution)/shard_map/place/pallas_call | solution.py:303
  (7 shorter events, 0.1 us)
Async XLA Ops:
  2.5 5.9 %collective-permute-start = (f32[6,4,1024]{2,1,0:T(4,128)S(1)}, f32[6,4,1024]{2,1,0:T(4,128)S(1)}, u32[]{:S(2)}, u32[]{:S(2)}) collective-permute-start(f32[6,4,1024]{2,1,0:T(4,128)S(1)} %pad_maximum_fusion.4), channel_id=1, source_target_pairs={{0,1},{1,2},{2,3},{4,5},{5,6},{6,7},{8,9},{9,10},{10,11},{12,13},{... | collective-permute-start | bytes 294920 | tf_op jit(solution)/shard_map/ppermute | solution.py:336
  4.5 5.8 %collective-permute-start.1 = (f32[6,4,1024]{2,1,0:T(4,128)S(1)}, f32[6,4,1024]{2,1,0:T(4,128)S(1)}, u32[]{:S(2)}, u32[]{:S(2)}) collective-permute-start(f32[6,4,1024]{2,1,0:T(4,128)S(1)} %pad_maximum_fusion.5), channel_id=1, source_target_pairs={{1,0},{2,1},{3,2},{5,4},{6,5},{7,6},{9,8},{10,9},{11,10},{13,12},{... | collective-permute-start | bytes 294920 | tf_op jit(solution)/shard_map/ppermute | solution.py:337
  8.5 1.9 %copy-start = (f32[6,4,1024]{2,1,0:T(4,128)}, f32[6,4,1024]{2,1,0:T(4,128)S(1)}, u32[]{:S(2)}) copy-start(f32[6,4,1024]{2,1,0:T(4,128)S(1)} %collective-permute-done.refs_2_) | copy-start | bytes 294916
  10.3 0.6 copy-start.1
  14.2 7.7 %collective-permute-start.7 = (f32[2,128,256]{2,1,0:T(8,128)}, f32[2,128,256]{2,1,0:T(8,128)S(1)}, u32[]{:S(2)}, u32[]{:S(2)}) collective-permute-start(f32[2,128,256]{2,1,0:T(8,128)} %get-tuple-element.18), channel_id=1, source_target_pairs={{1,9},{2,10},{5,13},{6,14},{9,17},{10,18},{13,21},{14,22},{17,25},... | collective-permute-start | bytes 786440 | tf_op jit(solution)/shard_map/ppermute | solution.py:341
  17.7 9.7 %collective-permute-start.6 = (f32[2,128,256]{2,1,0:T(8,128)}, f32[2,128,256]{2,1,0:T(8,128)S(1)}, u32[]{:S(2)}, u32[]{:S(2)}) collective-permute-start(f32[2,128,256]{2,1,0:T(8,128)} %get-tuple-element.18), channel_id=1, source_target_pairs={{1,5},{2,6},{5,9},{6,10},{9,13},{10,14},{13,17},{14,18},{17,21},{1... | collective-permute-start | bytes 786440 | tf_op jit(solution)/shard_map/ppermute | solution.py:341
  27.6 9.1 %collective-permute-start.8 = (f32[2,128,256]{2,1,0:T(8,128)S(1)}, f32[2,128,256]{2,1,0:T(8,128)S(1)}, u32[]{:S(2)}, u32[]{:S(2)}) collective-permute-start(f32[2,128,256]{2,1,0:T(8,128)S(1)} %pad_maximum_fusion), channel_id=1, source_target_pairs={{1,9},{2,10},{5,13},{6,14},{9,17},{10,18},{13,21},{14,22},{17,25},... | collective-permute-start | bytes 786440 | tf_op jit(solution)/shard_map/ppermute | solution.py:341
  36.9 25.8 %collective-permute-start.9 = (f32[2,128,256]{2,1,0:T(8,128)S(1)}, f32[2,128,256]{2,1,0:T(8,128)S(1)}, u32[]{:S(2)}, u32[]{:S(2)}) collective-permute-start(f32[2,128,256]{2,1,0:T(8,128)S(1)} %pad_maximum_fusion.1), channel_id=1, source_target_pairs={{1,17},{2,18},{5,21},{6,22},{9,25},{10,26},{13,29},{14,30}} | collective-permute-start | bytes 786440 | tf_op jit(solution)/shard_map/ppermute | solution.py:341
  46.8 26.3 %collective-permute-start.5 = (f32[2,256,384]{2,1,0:T(8,128)}, f32[2,256,384]{2,1,0:T(8,128)S(1)}, u32[]{:S(2)}, u32[]{:S(2)}) collective-permute-start(f32[2,256,384]{2,1,0:T(8,128)} %get-tuple-element.17), channel_id=1, source_target_pairs={{0,4},{1,5},{2,6},{3,7},{4,8},{5,9},{6,10},{7,11},{8,12},{9,13},{1... | collective-permute-start | bytes 2359304 | tf_op jit(solution)/shard_map/ppermute | solution.py:341
  52.2 7.2 %copy-start.7 = (f32[2,128,256]{2,1,0:T(8,128)S(1)}, f32[2,128,256]{2,1,0:T(8,128)}, u32[]{:S(2)}) copy-start(f32[2,128,256]{2,1,0:T(8,128)} %get-tuple-element.16) | copy-start | bytes 786436
  52.2 11.5 %copy-start.6 = (f32[2,128,256]{2,1,0:T(8,128)S(1)}, f32[2,128,256]{2,1,0:T(8,128)}, u32[]{:S(2)}) copy-start(f32[2,128,256]{2,1,0:T(8,128)} %get-tuple-element.18) | copy-start | bytes 786436
  56.8 59.2 %collective-permute-start.2 = (f32[2,256,384]{2,1,0:T(8,128)}, f32[2,256,384]{2,1,0:T(8,128)S(1)}, u32[]{:S(2)}, u32[]{:S(2)}) collective-permute-start(f32[2,256,384]{2,1,0:T(8,128)} %get-tuple-element.14), channel_id=1, source_target_pairs={{0,4},{1,5},{2,6},{3,7},{4,8},{5,9},{6,10},{7,11},{8,12},{9,13},{1... | collective-permute-start | bytes 2359304 | tf_op jit(solution)/shard_map/ppermute | solution.py:341
  58.7 5.9 %collective-permute-start.3 = (f32[2,128,256]{2,1,0:T(8,128)}, f32[2,128,256]{2,1,0:T(8,128)S(1)}, u32[]{:S(2)}, u32[]{:S(2)}) collective-permute-start(f32[2,128,256]{2,1,0:T(8,128)} %get-tuple-element.15), channel_id=1, source_target_pairs={{0,4},{1,5},{3,7},{4,8},{5,9},{7,11},{8,12},{9,13},{11,15},{12,16}... | collective-permute-start | bytes 786440 | tf_op jit(solution)/shard_map/ppermute | solution.py:341
  59.4 13.7 %collective-permute-start.4 = (f32[2,128,256]{2,1,0:T(8,128)S(1)}, f32[2,128,256]{2,1,0:T(8,128)S(1)}, u32[]{:S(2)}, u32[]{:S(2)}) collective-permute-start(f32[2,128,256]{2,1,0:T(8,128)S(1)} %copy-done.7), channel_id=1, source_target_pairs={{0,4},{2,6},{3,7},{4,8},{6,10},{7,11},{8,12},{10,14},{11,15},{12,1... | collective-permute-start | bytes 786440 | tf_op jit(solution)/shard_map/ppermute | solution.py:341
  64.6 8.5 %copy-start.4 = (f32[2,128,256]{2,1,0:T(8,128)}, f32[2,128,256]{2,1,0:T(8,128)S(1)}, u32[]{:S(2)}) copy-start(f32[2,128,256]{2,1,0:T(8,128)S(1)} %collective-permute-done.3.refs_1_) | copy-start | bytes 786436
  73.1 0.7 copy-start.5
  73.1 1.0 copy-start.3
  116.0 0.9 copy-start.2

commit v2 on v1

v2 whole, which is shorter than its diff:
```python
import functools

import jax
import jax.numpy as jnp
from jax import lax
from jax.experimental import pallas as pl
from jax.experimental.pallas import tpu as pltpu
from jax.sharding import PartitionSpec as P

COARSE_SHARE = 4
LANES = 128
STRIP = 32
HALO = 4
PAD = 8

diffusion = 1.5
drift = 0.8
shear = 0.6


def rates(row_start, rows, column_start, columns, size_x, size_y):
    row = row_start + lax.broadcasted_iota(jnp.int32, (rows, columns), 0)
    column = column_start + lax.broadcasted_iota(jnp.int32, (rows, columns), 1)
    along = (row.astype(jnp.float32) - size_x // 2) * (2.0 / size_x)
    across = (column.astype(jnp.float32) - size_y // 2) * (2.0 / size_y)
    real = -diffusion * (along * along + across * across)
    return real, -drift * across, shear * across


def turned(real, imag, first, second):
    return real * first - imag * second, real * second + imag * first


def fine_kernel(*refs, first_block, coarse, size_x, size_y, coarse_rows, pieces, aliased):
    begin, old = refs[:2]
    refs = refs[2:]
    if coarse:
        before, after = refs[:2]
        refs = refs[2:]
    refs = refs[aliased:]
    nodes, refs = refs[0], refs[1:]
    sends, refs = refs[: len(pieces)], refs[len(pieces):]
    offset = None
    if coarse:
        offset, refs = refs[0], refs[1:]
    wide_one, wide_two, inner, inverse = refs
    rows = begin.shape[1]
    rank = lax.axis_index("space")
    ranks = lax.axis_size("space")
    spot = pl.ds(pl.multiple_of(pl.program_id(0) * LANES, LANES), LANES)
    row_base = rank * rows
    column_base = (first_block + pl.program_id(0)) * LANES
    has_before = rank > 0
    has_after = rank < ranks - 1
    tiles = [("in", start, min(STRIP, rows - start)) for start in range(0, rows, STRIP)]
    if coarse:
        whole = pl.ds((first_block + pl.program_id(0)) * LANES, LANES)
        tiles = [("before", -HALO, HALO)] + tiles + [("after", rows, HALO)]

    def fields(kind, start, count):
        if kind == "in":
            here = pl.ds(start, count)
            return ([begin[0, here, :], begin[1, here, :]],
                    [old[0, 0, here, :], old[0, 1, here, :]],
                    [old[1, 0, here, :], old[1, 1, here, :]])
        side = before if kind == "before" else after
        part = [side[k, :, whole] for k in range(6)]
        return (part[:2], part[2:4], part[4:])

    def kept(kind, value):
        if kind == "before":
            return jnp.where(has_before, value, 0.0)
        if kind == "after":
            return jnp.where(has_after, value, 0.0)
        return value

    def sums(ref, part, start, count):
        return ref[part, pl.ds(PAD + start - 1, count), :] + ref[part, pl.ds(PAD + start + 1, count), :]

    for kind, start, count in tiles:
        b, one, two = fields(kind, start, count)
        for part in range(2):
            third = (1.0 / 3.0) * one[part]
            wide_one[part, pl.ds(PAD + start, count), :] = (5.0 / 24.0) * b[part] + third - (1.0 / 24.0) * two[part]
            wide_two[part, pl.ds(PAD + start, count), :] = third - (1.0 / 24.0) * b[part] + (5.0 / 24.0) * two[part] - 0.5 * one[part]
    for kind, start, count in tiles:
        real, imag, factor = rates(row_base + start, count, column_base, LANES, size_x, size_y)
        b, one, _ = fields(kind, start, count)
        here = pl.ds(PAD + start, count)
        u = [wide_one[part, here, :] - 0.5 * one[part] for part in range(2)]
        lu = turned(real, imag, u[0], u[1])
        top = (b[0] + lu[0] + factor * sums(wide_one, 1, start, count),
               b[1] + lu[1] - factor * sums(wide_one, 0, start, count))
        half_real = 1.0 - 0.5 * real
        half_imag = -0.5 * imag
        share = 1.0 / (half_real * half_real + half_imag * half_imag)
        half_real = half_real * share
        half_imag = half_imag * share
        inverse[0, here, :] = half_real
        inverse[1, here, :] = half_imag
        node = (top[0] * half_real + top[1] * half_imag, top[1] * half_real - top[0] * half_imag)
        for part in range(2):
            value = kept(kind, node[part])
            if kind == "in":
                nodes[0, part, pl.ds(start, count), :] = value
            inner[part, here, :] = value
    for kind, start, count in tiles:
        here = pl.ds(PAD + start, count)
        for part in range(2):
            wide_one[part, here, :] = 0.5 * inner[part, here, :] + wide_two[part, here, :]
    for kind, start, count in tiles:
        if kind != "in" and not coarse:
            continue
        real, imag, factor = rates(row_base + start, count, column_base, LANES, size_x, size_y)
        b, one, two = fields(kind, start, count)
        here = pl.ds(PAD + start, count)
        u = [wide_two[part, here, :] + 0.5 * (one[part] - two[part]) for part in range(2)]
        lu = turned(real, imag, u[0], u[1])
        n1 = [inner[part, here, :] for part in range(2)]
        top = (n1[0] + lu[0] + factor * sums(wide_one, 1, start, count),
               n1[1] + lu[1] - factor * sums(wide_one, 0, start, count))
        half_real = inverse[0, here, :]
        half_imag = inverse[1, here, :]
        node = (top[0] * half_real + top[1] * half_imag, top[1] * half_real - top[0] * half_imag)
        for part in range(2):
            value = kept(kind, node[part])
            if kind == "in":
                nodes[1, part, pl.ds(start, count), :] = value
                for (low, high), send in zip(pieces, sends):
                    a, z = max(low, start), min(high, start + count)
                    if a < z:
                        send[part, pl.ds(a - low, z - a), spot] = value[a - start:z - start]
            if coarse:
                inner[part, here, :] = (1.0 / 6.0) * b[part] + (2.0 / 3.0) * n1[part] + (1.0 / 6.0) * value
    if coarse:
        def offsets(shift):
            for start in range(0, coarse_rows, STRIP):
                count = min(STRIP, coarse_rows - start)
                at = shift + start
                real, imag, factor = rates(row_base + at, count, column_base, LANES, size_x, size_y)
                v = [inner[part, pl.ds(PAD + at, count), :] for part in range(2)]
                e = [nodes[1, part, pl.ds(at, count), :] for part in range(2)]
                lu = turned(real, imag, v[0] - e[0], v[1] - e[1])
                off = (lu[0] + factor * sums(inner, 1, at, count),
                       lu[1] - factor * sums(inner, 0, at, count))
                step_real = 1.0 - real
                step_imag = -imag
                share = 1.0 / (step_real * step_real + step_imag * step_imag)
                lead = lax.axis_index("tm") == 0
                off = tuple(off[part] + jnp.where(lead, begin[part, pl.ds(at, count), :], 0.0) for part in range(2))
                offset[0, pl.ds(start, count), spot] = (off[0] * step_real + off[1] * step_imag) * share
                offset[1, pl.ds(start, count), spot] = (off[1] * step_real - off[0] * step_imag) * share

        low_shift = rows - coarse_rows
        if low_shift == 0:
            offsets(0)
        else:
            upper = rank >= ranks // 2

            @pl.when(upper)
            def _():
                offsets(0)

            @pl.when(jnp.logical_not(upper))
            def _():
                offsets(low_shift)


VMEM = pl.BlockSpec(memory_space=pltpu.VMEM)
ANY = pl.BlockSpec(memory_space=pl.ANY)
PARAMS = pltpu.CompilerParams(vmem_limit_bytes=28 * 1024 * 1024)


def fine_call(begin, old, halo, nodes, first, width, pieces, size_x, coarse_rows):
    rows, columns = begin.shape[1:]
    coarse = halo is not None
    base = first // LANES
    f32 = jnp.float32
    out_shape = [jax.ShapeDtypeStruct((2, 2, rows, columns), f32)]
    out_specs = [pl.BlockSpec((2, 2, rows, LANES), lambda j: (0, 0, 0, base + j))]
    for low, high in pieces:
        out_shape.append(jax.ShapeDtypeStruct((2, high - low, width), f32))
        out_specs.append(VMEM)
    if coarse:
        out_shape.append(jax.ShapeDtypeStruct((2, coarse_rows, width), f32))
        out_specs.append(VMEM)
    in_specs = [
        pl.BlockSpec((2, rows, LANES), lambda j: (0, 0, base + j)),
        pl.BlockSpec((2, 2, rows, LANES), lambda j: (0, 0, 0, base + j)),
    ]
    operands = [begin, old]
    if coarse:
        operands += list(halo)
        in_specs += [VMEM, VMEM]
    aliases = {}
    if nodes is not None:
        aliases = {len(operands): 0}
        operands.append(nodes)
        in_specs.append(ANY)
    kernel = functools.partial(
        fine_kernel, first_block=base, coarse=coarse, size_x=size_x, size_y=columns,
        coarse_rows=coarse_rows, pieces=pieces, aliased=len(aliases))
    scratch = [pltpu.VMEM((2, rows + 2 * PAD, LANES), f32) for _ in range(4)]
    return pl.pallas_call(
        kernel, grid=(width // LANES,), in_specs=in_specs, out_specs=out_specs, out_shape=out_shape,
        scratch_shapes=scratch, input_output_aliases=aliases, compiler_params=PARAMS,
        name="fine_coarse" if coarse else "fine",
    )(*operands)


def edge_kernel(begin_top, old_top, begin_end, old_end, before, after, _, nodes, send, wide, fixed, sems,
                *, rows, size_x, size_y, outer):
    rank = lax.axis_index("space")
    ranks = lax.axis_size("space")
    side_rows = begin_top.shape[1]
    height = HALO + side_rows
    copies = []
    for k, (low, width, spot) in enumerate(outer):
        cut = pl.ds(low, width)
        for top in (True, False):
            begin, old, halo = (begin_top, old_top, before) if top else (begin_end, old_end, after)
            base = rank * rows + (-HALO if top else rows - side_rows)

            def field(index):
                if index < 2:
                    near = begin[index, :, cut]
                else:
                    near = old[index // 2 - 1, index % 2, :, cut]
                far = halo[index, :, cut]
                return jnp.concatenate([far, near] if top else [near, far], axis=0)

            real, imag, factor = rates(base, height, low, width, size_x, size_y)
            b, one, two = [[field(2 * k + part) for part in range(2)] for k in range(3)]

            def coupled(pair):
                moved = []
                for part in range(2):
                    wide[part, pl.ds(PAD, height), :] = pair[part]
                    moved.append(wide[part, pl.ds(PAD - 1, height), :] + wide[part, pl.ds(PAD + 1, height), :])
                return factor * moved[1], -factor * moved[0]

            half_real = 1.0 - 0.5 * real
            half_imag = -0.5 * imag
            share = 1.0 / (half_real * half_real + half_imag * half_imag)

            def divided(x, y):
                return (x * half_real + y * half_imag) * share, (y * half_real - x * half_imag) * share

            w1 = [(5.0 / 24.0) * b[p] + (1.0 / 3.0) * one[p] - (1.0 / 24.0) * two[p] for p in range(2)]
            w2 = [(1.0 / 3.0) * one[p] - (1.0 / 24.0) * b[p] + (5.0 / 24.0) * two[p] for p in range(2)]
            lu = turned(real, imag, w1[0] - 0.5 * one[0], w1[1] - 0.5 * one[1])
            cw = coupled(w1)
            n1 = divided(b[0] + lu[0] + cw[0], b[1] + lu[1] + cw[1])
            row = base + lax.broadcasted_iota(jnp.int32, (height, width), 0)
            inside = jnp.logical_and(row >= 0, row < size_x)
            n1 = [jnp.where(inside, value, 0.0) for value in n1]
            cw = coupled([0.5 * (n1[p] - one[p]) + w2[p] for p in range(2)])
            lu = turned(real, imag, w2[0] - 0.5 * two[0], w2[1] - 0.5 * two[1])
            n2 = divided(n1[0] + lu[0] + cw[0], n1[1] + lu[1] + cw[1])
            keep = slice(HALO, HALO + PAD) if top else slice(side_rows - PAD, side_rows)
            at = 0 if top else PAD
            for part in range(2):
                fixed[0, part, pl.ds(at, PAD), pl.ds(spot, width)] = n1[part][keep]
                fixed[1, part, pl.ds(at, PAD), pl.ds(spot, width)] = n2[part][keep]
                send[part, pl.ds(at, PAD), pl.ds(spot, width)] = n2[part][keep]
            copy = pltpu.make_async_copy(
                fixed.at[:, :, pl.ds(at, PAD), pl.ds(spot, width)],
                nodes.at[:, :, pl.ds(0 if top else rows - PAD, PAD), cut], sems.at[2 * k + (not top)])
            copy.start()
            copies.append(copy)
    for copy in copies:
        copy.wait()


def edge_call(begin, old, halo, nodes, outer, size_x):
    rows, columns = begin.shape[1:]
    side = 2 * PAD
    last = rows // side - 1
    total = sum(width for _, width in outer)
    f32 = jnp.float32
    spots, at = [], 0
    for low, width in outer:
        spots.append((low, width, at))
        at += width
    widest = max(width for _, width in outer)
    assert all(width == widest for _, width in outer)
    kernel = functools.partial(edge_kernel, rows=rows, size_x=size_x, size_y=columns, outer=spots)
    return pl.pallas_call(
        kernel, grid=(1,),
        in_specs=[pl.BlockSpec((2, side, columns), lambda j: (0, 0, 0)),
                  pl.BlockSpec((2, 2, side, columns), lambda j: (0, 0, 0, 0)),
                  pl.BlockSpec((2, side, columns), lambda j: (0, last, 0)),
                  pl.BlockSpec((2, 2, side, columns), lambda j: (0, 0, last, 0)),
                  VMEM, VMEM, ANY],
        out_specs=[ANY, VMEM],
        out_shape=[jax.ShapeDtypeStruct(nodes.shape, f32), jax.ShapeDtypeStruct((2, side, total), f32)],
        scratch_shapes=[pltpu.VMEM((2, 2 * PAD + HALO + side + PAD, widest), f32),
                        pltpu.VMEM((2, 2, side, total), f32), pltpu.SemaphoreType.DMA((2 * len(outer),))],
        input_output_aliases={6: 0}, compiler_params=PARAMS, name="edges",
    )(begin, old, begin, old, halo[0], halo[1], nodes)


def patch_kernel(*refs, count, pieces, coarse_rows):
    begin, nodes_in = refs[:2]
    arrived = refs[2:2 + count]
    fresh, finish, start, nodes = refs[2 + count:]
    rows = begin.shape[1]
    rank = lax.axis_index("space")
    ranks = lax.axis_size("space")
    lead = lax.axis_index("tm") == 0
    spot = pl.ds(pl.multiple_of(pl.program_id(0) * LANES, LANES), LANES)
    middle = jnp.logical_or(rank == ranks // 2, rank == ranks // 2 - 1)
    for (low, high), piece in zip(pieces, arrived):
        here = pl.ds(low, high - low)
        for part in range(2):
            start[part, here, :] = jnp.where(lead, begin[part, here, :], piece[part, :, spot])
    nodes[...] = nodes_in[...]

    def fix(shift):
        here = pl.ds(shift, coarse_rows)
        for part in range(2):
            old_begin = begin[part, here, :]
            n2 = nodes_in[1, part, here, :]
            now = jnp.where(lead, old_begin, fresh[part, :, spot])
            change = finish[part, :, spot] - n2
            nodes[0, part, here, :] = nodes_in[0, part, here, :] + 0.5 * ((now - old_begin) + change)
            nodes[1, part, here, :] = n2 + change
            start[part, here, :] = now

    if rows == coarse_rows:
        @pl.when(middle)
        def _():
            fix(0)
    else:
        @pl.when(rank == ranks // 2)
        def _():
            fix(0)

        @pl.when(rank == ranks // 2 - 1)
        def _():
            fix(rows - coarse_rows)


def patch_call(begin, nodes, arrived, pieces, fresh, finish, low_column, coarse_rows):
    rows = begin.shape[1]
    base = low_column // LANES
    begin_spec = pl.BlockSpec((2, rows, LANES), lambda j: (0, 0, base + j))
    nodes_spec = pl.BlockSpec((2, 2, rows, LANES), lambda j: (0, 0, 0, base + j))
    kernel = functools.partial(patch_kernel, count=len(arrived), pieces=pieces, coarse_rows=coarse_rows)
    return pl.pallas_call(
        kernel, grid=(fresh.shape[2] // LANES,),
        in_specs=[begin_spec, nodes_spec] + [VMEM] * (len(arrived) + 2),
        out_specs=[begin_spec, nodes_spec],
        out_shape=[jax.ShapeDtypeStruct(begin.shape, jnp.float32), jax.ShapeDtypeStruct(nodes.shape, jnp.float32)],
        input_output_aliases={1: 1}, compiler_params=PARAMS, name="patch",
    )(begin, nodes, *arrived, fresh, finish)


def place_kernel(begin, middle, edges, _, start, *, spot):
    lead = lax.axis_index("tm") == 0
    rows = begin.shape[1]
    here = pl.ds(pl.multiple_of(pl.program_id(0) * LANES, LANES), LANES)
    side = pl.ds(pl.multiple_of(spot + pl.program_id(0) * LANES, LANES), LANES)
    for part in range(2):
        start[part, pl.ds(0, PAD), :] = jnp.where(lead, begin[part, pl.ds(0, PAD), :], edges[part, pl.ds(0, PAD), side])
        start[part, pl.ds(PAD, rows - 2 * PAD), :] = jnp.where(
            lead, begin[part, pl.ds(PAD, rows - 2 * PAD), :], middle[part, :, here])
        start[part, pl.ds(rows - PAD, PAD), :] = jnp.where(
            lead, begin[part, pl.ds(rows - PAD, PAD), :], edges[part, pl.ds(PAD, PAD), side])


def place_call(begin, middle, edges, start, first, spot):
    rows = begin.shape[1]
    base = first // LANES
    spec = pl.BlockSpec((2, rows, LANES), lambda j: (0, 0, base + j))
    return pl.pallas_call(
        functools.partial(place_kernel, spot=spot), grid=(middle.shape[2] // LANES,),
        in_specs=[spec, VMEM, VMEM, ANY], out_specs=spec,
        out_shape=jax.ShapeDtypeStruct(begin.shape, jnp.float32),
        input_output_aliases={3: 0}, compiler_params=PARAMS, name="place",
    )(begin, middle, edges, start)


def powers(row_base, rows, low_column, width, size_x, size_y):
    real, imag, _ = rates(row_base, rows, low_column, width, size_x, size_y)
    step_real = 1.0 - real
    step_imag = -imag
    share = 1.0 / (step_real * step_real + step_imag * step_imag)
    return step_real * share, -step_imag * share


def body(start_values, node_values):
    begin = start_values[0]
    old = node_values[0]
    rows, columns = begin.shape[1:]
    slices, ranks = lax.axis_size("tm"), lax.axis_size("space")
    size_x = rows * ranks
    width = columns // COARSE_SHARE
    low_column = columns // 2 - width // 2
    coarse_rows = min(rows, size_x // COARSE_SHARE // 2)
    lower, upper = ranks // 2 - 1, ranks // 2
    rank = lax.axis_index("space")
    lead = lax.axis_index("tm") == 0

    def edge(low):
        cut = [begin[:, low:low + HALO], old[0, :, low:low + HALO], old[1, :, low:low + HALO]]
        return jnp.concatenate(cut, axis=0)

    up = [(i, i + 1) for i in range(ranks - 1)]
    before = lax.ppermute(edge(rows - HALO), "space", up)
    after = lax.ppermute(edge(0), "space", [(j, i) for i, j in up])

    def ahead(value, steps, members):
        pairs = [(n * ranks + s, (n + steps) * ranks + s) for n in range(slices - steps) for s in members]
        return lax.ppermute(value, ("tm", "space"), pairs)

    everyone = range(ranks)
    middle = (lower, upper)
    if rows == coarse_rows:
        pieces = [(0, rows)]
        holders = [[s for s in everyone if s not in middle]]
    else:
        cuts = [0, coarse_rows, rows - coarse_rows, rows]
        pieces = [(a, b) for a, b in zip(cuts, cuts[1:]) if a < b]
        holders = [[s for s in everyone
                    if not (s == upper and b <= coarse_rows) and not (s == lower and a >= rows - coarse_rows)]
                   for a, b in pieces]
    second = low_column + width
    rest = columns - second
    inside = [(PAD, rows - PAD)]
    nodes, left = fine_call(begin, old, None, None, 0, low_column, inside, size_x, coarse_rows)
    left = ahead(left, 1, everyone)
    nodes, right = fine_call(begin, old, None, nodes, second, rest, inside, size_x, coarse_rows)
    made = fine_call(begin, old, (before, after), nodes, low_column, width, pieces, size_x, coarse_rows)
    nodes, inner_sends, offset = made[0], made[1:-1], made[-1]
    one_back = ahead(offset, 1, middle)
    two_back = ahead(offset, 2, middle)
    right = ahead(right, 1, everyone)
    nodes, edges = edge_call(begin, old, (before, after), nodes, [(0, low_column), (second, rest)], size_x)
    edges = ahead(edges, 1, everyone)

    shift = jnp.where(rank >= ranks // 2, 0, rows - coarse_rows)
    d_real, d_imag = powers(rank * rows + shift, coarse_rows, low_column, width, size_x, columns)

    def add(total, field, real, imag):
        grown = turned(real, imag, field[0], field[1])
        return jnp.stack([total[0] + grown[0], total[1] + grown[1]])

    total = add(one_back, two_back, d_real, d_imag)
    inner = [ahead(piece, 1, members) for piece, members in zip(inner_sends, holders)]
    power = turned(d_real, d_imag, d_real, d_imag)
    reach = 2
    while reach < slices:
        total = add(total, ahead(total, reach, middle), *power)
        power = turned(power[0], power[1], power[0], power[1])
        reach *= 2
    end = add(offset, jnp.where(lead, 0.0, total), d_real, d_imag)
    next_start, nodes = patch_call(begin, nodes, inner, pieces, total, end, low_column, coarse_rows)
    next_start = place_call(begin, left, edges, next_start, 0, 0)
    next_start = place_call(begin, right, edges, next_start, second, low_column)
    return next_start[None], nodes[None]


def solution(mesh):
    in_specs = (P("tm", None, "space", None), P("tm", None, None, "space", None))
    out_specs = (P("tm", None, "space", None), P("tm", None, None, "space", None))
    return jax.shard_map(body, mesh=mesh, in_specs=in_specs, out_specs=out_specs, check_vma=False)
```

time: 142 us -> 94.3 us (0.66)
  the two profiles are of different devices: /device:TPU:2 before, /device:TPU:18 now
where the time goes in v2:
time: 94.3 us; the launch traced here: 93.6 us
  waiting for transfers between devices  31.9 us (34%)
  starting transfers between devices  30 us (32%)
  Pallas kernels  15.6 us (17%)
  local copies, waits for them, and re-layouts  12.5 us (13%)
  other arithmetic  2.54 us (3%)
  between operations  1.07 us (1%)
    ppermute x9, waiting for transfers between devices, ahead(): return lax.ppermute(value, ('tm', 'space'), pairs)  31.9 us
    ppermute x9, starting transfers between devices, ahead(): return lax.ppermute(value, ('tm', 'space'), pairs)  24.4 us
    unnamed x42, local copies, waits for them, and re-layouts  10.7 us
    pallas_call x3, Pallas kernels, fine_call(): pl.pallas_call(kernel, grid=(width // LANES,), in_specs=in_specs, out_spe...  7.85 us
    pallas_call x2, Pallas kernels, place_call(): pl.pallas_call(functools.partial(place_kernel, spot=spot), grid=(middle.s...  4.22 us
    ppermute x1, starting transfers between devices, body(): after = lax.ppermute(edge(0), 'space', [(j, i) for i, j in up])  3.64 us
    pallas_call x1, Pallas kernels, patch_call(): pl.pallas_call(kernel, grid=(fresh.shape[2] // LANES,), in_specs=[begin_s...  2.32 us
    ppermute x1, starting transfers between devices, body(): before = lax.ppermute(edge(rows - HALO), 'space', up)  1.92 us
  transfers between devices with their start and end apart: 11, of which 4 were waited for; matrix products, arithmetic and copies ran while one was open for 2% of the time, Pallas kernels for 13%

profile of v2, /device:TPU:18, one launch (start us, length us, event | category | flops | bytes accessed | tf_op | source)
XLA Modules:
  0.0 93.6 jit_solution(17025445462330985747)
XLA Ops:
  0.6 0.9 fusion.3
  1.5 1.0 %slice_bitcast_fusion.1 = (f32[2,4,1024]{2,1,0:T(4,128)S(1)}, f32[2,4,1024]{2,1,0:T(4,128)S(1)}, f32[2,4,1024]{2,1,0:T(4,128)S(1)}, f32[2,4,1024]{2,1,0:T(4,128)S(1)}) fusion(f32[2,2,256,1024]{3,2,1,0:T(8,128)} %bitcast.21), kind=kLoop, calls=%fused_computation.23 | loop fusion | bytes 262144 | tf_op jit(solution)/shard_map/squeeze | solution.py:406
  2.5 1.9 %collective-permute-start.1 = (f32[6,4,1024]{2,1,0:T(4,128)S(1)}, f32[6,4,1024]{2,1,0:T(4,128)S(1)}, u32[]{:S(2)}, u32[]{:S(2)}) collective-permute-start(f32[6,4,1024]{2,1,0:T(4,128)S(1)} %pad_maximum_fusion.4), channel_id=1, source_target_pairs={{0,1},{1,2},{2,3},{4,5},{5,6},{6,7},{8,9},{9,10},{10,11},{12,13},{... | collective-permute-start | bytes 294920 | tf_op jit(solution)/shard_map/ppermute | solution.py:410
  4.5 3.6 %collective-permute-start.2 = (f32[6,4,1024]{2,1,0:T(4,128)S(1)}, f32[6,4,1024]{2,1,0:T(4,128)S(1)}, u32[]{:S(2)}, u32[]{:S(2)}) collective-permute-start(f32[6,4,1024]{2,1,0:T(4,128)S(1)} %pad_maximum_fusion.5), channel_id=1, source_target_pairs={{1,0},{2,1},{3,2},{5,4},{6,5},{7,6},{9,8},{10,9},{11,10},{13,12},{... | collective-permute-start | bytes 294920 | tf_op jit(solution)/shard_map/ppermute | solution.py:411
  8.1 0.0 copy-start
  8.2 1.6 %copy-done = f32[1,2,256,1024]{3,2,1,0:T(8,128)S(1)} copy-done((f32[1,2,256,1024]{3,2,1,0:T(8,128)S(1)}, f32[1,2,256,1024]{3,2,1,0:T(8,128)}, u32[]{:S(2)}) %copy-start) | copy-done | bytes 2097176
  9.7 2.2 %copy-done.2 = f32[1,2,2,256,1024]{4,3,2,1,0:T(8,128)S(1)} copy-done((f32[1,2,2,256,1024]{4,3,2,1,0:T(8,128)S(1)}, f32[1,2,2,256,1024]{4,3,2,1,0:T(8,128)}, u32[]{:S(2)}) %copy-start.2) | copy-done | bytes 4194328
  11.9 3.0 %fine.2 = (f32[2,2,256,1024]{3,2,1,0:T(8,128)}, f32[2,240,384]{2,1,0:T(8,128)}) custom-call(f32[2,256,1024]{2,1,0:T(8,128)S(1)} %bitcast.13, f32[2,2,256,1024]{3,2,1,0:T(8,128)S(1)} %bitcast.22), custom_call_target="tpu_custom_call" | custom-call | tf_op jit(solution)/shard_map/fine/pallas_call | solution.py:204
  14.9 0.0 copy-done.1
  14.9 2.2 %copy-done.3 = f32[1,2,2,256,1024]{4,3,2,1,0:T(8,128)S(1)} copy-done((f32[1,2,2,256,1024]{4,3,2,1,0:T(8,128)S(1)}, f32[1,2,2,256,1024]{4,3,2,1,0:T(8,128)}, u32[]{:S(2)}) %copy-start.3) | copy-done | bytes 4194328
  17.1 2.7 %fine.3 = (f32[2,2,256,1024]{3,2,1,0:T(8,128)}, f32[2,240,384]{2,1,0:T(8,128)S(1)}) custom-call(f32[2,256,1024]{2,1,0:T(8,128)S(1)} %bitcast.14, f32[2,2,256,1024]{3,2,1,0:T(8,128)S(1)} %bitcast.23, f32[2,2,256,1024]{3,2,1,0:T(8,128)} %get-tuple-element.14.refs_2_), custom_call_target="tpu_custom_call", output_to_operand_aliasing={{0}: (2, {})} | custom-call | tf_op jit(solution)/shard_map/fine/pallas_call | solution.py:204
  19.8 0.0 collective-permute-done.1.refs_2_.before
  19.8 0.0 collective-permute-done.2.refs_3_.after
  19.8 0.0 copy-start.4
  19.8 2.4 %copy-done.4 = f32[1,2,2,256,1024]{4,3,2,1,0:T(8,128)S(1)} copy-done((f32[1,2,2,256,1024]{4,3,2,1,0:T(8,128)S(1)}, f32[1,2,2,256,1024]{4,3,2,1,0:T(8,128)}, u32[]{:S(2)}) %copy-start.4) | copy-done | bytes 4194328
  22.2 2.2 %fine_coarse.1 = (f32[2,2,256,1024]{3,2,1,0:T(8,128)}, f32[2,128,256]{2,1,0:T(8,128)S(1)}, f32[2,128,256]{2,1,0:T(8,128)S(1)}, f32[2,128,256]{2,1,0:T(8,128)S(1)}) custom-call(f32[2,256,1024]{2,1,0:T(8,128)S(1)} %bitcast.15, f32[2,2,256,1024]{3,2,1,0:T(8,128)S(1)} %bitcast.24, ...), custom_call_target="tpu_custom_call", output_to_operand_aliasing={{0}: (4, {})} | custom-call | tf_op jit(solution)/shard_map/fine_coarse/pallas_call | solution.py:204
  24.4 0.0 copy-done.6
  24.4 3.5 %collective-permute-start.8 = (f32[2,128,256]{2,1,0:T(8,128)S(1)}, f32[2,128,256]{2,1,0:T(8,128)S(1)}, u32[]{:S(2)}, u32[]{:S(2)}) collective-permute-start(f32[2,128,256]{2,1,0:T(8,128)S(1)} %get-tuple-element.23), channel_id=1, source_target_pairs={{1,9},{2,10},{5,13},{6,14},{9,17},{10,18},{13,21},{14,22},{17,25},... | collective-permute-start | bytes 786440 | tf_op jit(solution)/shard_map/ppermute | solution.py:415
  27.9 3.4 %collective-permute-start.7 = (f32[2,128,256]{2,1,0:T(8,128)S(1)}, f32[2,128,256]{2,1,0:T(8,128)S(1)}, u32[]{:S(2)}, u32[]{:S(2)}) collective-permute-start(f32[2,128,256]{2,1,0:T(8,128)S(1)} %get-tuple-element.23), channel_id=1, source_target_pairs={{1,5},{2,6},{5,9},{6,10},{9,13},{10,14},{13,17},{14,18},{17,21},{1... | collective-permute-start | bytes 786440 | tf_op jit(solution)/shard_map/ppermute | solution.py:415
  31.4 0.0 copy-start.19
  31.4 0.0 copy-start.17
  31.4 0.0 copy-start.13
  31.4 0.0 copy-start.15
  31.4 1.3 %collective-permute-done.8 = f32[2,128,256]{2,1,0:T(8,128)S(1)} collective-permute-done((f32[2,128,256]{2,1,0:T(8,128)S(1)}, f32[2,128,256]{2,1,0:T(8,128)S(1)}, u32[]{:S(2)}, u32[]{:S(2)}) %collective-permute-start.8) | collective-permute-done | bytes 262176 | tf_op jit(solution)/shard_map/ppermute | solution.py:415
  32.7 7.2 %collective-permute-done.7 = f32[2,128,256]{2,1,0:T(8,128)S(1)} collective-permute-done((f32[2,128,256]{2,1,0:T(8,128)S(1)}, f32[2,128,256]{2,1,0:T(8,128)S(1)}, u32[]{:S(2)}, u32[]{:S(2)}) %collective-permute-start.7) | collective-permute-done | bytes 262176 | tf_op jit(solution)/shard_map/ppermute | solution.py:415
  39.9 0.1 slice_add_fusion.1
  40.1 3.0 %collective-permute-start.9 = (f32[2,128,256]{2,1,0:T(8,128)S(1)}, f32[2,128,256]{2,1,0:T(8,128)S(1)}, u32[]{:S(2)}, u32[]{:S(2)}) collective-permute-start(f32[2,128,256]{2,1,0:T(8,128)S(1)} %pad_maximum_fusion), channel_id=1, source_target_pairs={{1,9},{2,10},{5,13},{6,14},{9,17},{10,18},{13,21},{14,22},{17,25},... | collective-permute-start | bytes 786440 | tf_op jit(solution)/shard_map/ppermute | solution.py:415
  43.1 5.3 %collective-permute-done.9 = f32[2,128,256]{2,1,0:T(8,128)S(1)} collective-permute-done((f32[2,128,256]{2,1,0:T(8,128)S(1)}, f32[2,128,256]{2,1,0:T(8,128)S(1)}, u32[]{:S(2)}, u32[]{:S(2)}) %collective-permute-start.9) | collective-permute-done | bytes 262176 | tf_op jit(solution)/shard_map/ppermute | solution.py:415
  48.3 0.2 subtract_add_fusion.2
  48.5 0.0 copy-start.9
  48.5 0.0 copy-start.11
  48.5 0.8 pad_maximum_fusion.1
  49.3 1.3 %collective-permute-start.10 = (f32[2,128,256]{2,1,0:T(8,128)}, f32[2,128,256]{2,1,0:T(8,128)}, u32[]{:S(2)}, u32[]{:S(2)}) collective-permute-start(f32[2,128,256]{2,1,0:T(8,128)} %pad_maximum_fusion.1), channel_id=1, source_target_pairs={{1,17},{2,18},{5,21},{6,22},{9,25},{10,26},{13,29},{14,30}} | collective-permute-start | bytes 786440 | tf_op jit(solution)/shard_map/ppermute | solution.py:415
  50.6 5.3 %collective-permute-start.4 = (f32[2,240,384]{2,1,0:T(8,128)}, f32[2,240,384]{2,1,0:T(8,128)}, u32[]{:S(2)}, u32[]{:S(2)}) collective-permute-start(f32[2,240,384]{2,1,0:T(8,128)} %get-tuple-element.19), channel_id=1, source_target_pairs={{0,4},{1,5},{2,6},{3,7},{4,8},{5,9},{6,10},{7,11},{8,12},{9,13},{1... | collective-permute-start | bytes 2211848 | tf_op jit(solution)/shard_map/ppermute | solution.py:415
  55.9 0.0 copy-done.7
  55.9 0.0 copy-done.19
  56.0 0.0 copy-done.17
  56.0 0.0 copy-done.13
  56.0 0.0 copy-done.15
  56.0 0.0 copy-done.9
  56.0 0.0 copy-done.11
  56.0 1.9 %collective-permute-start = (f32[2,240,384]{2,1,0:T(8,128)}, f32[2,240,384]{2,1,0:T(8,128)S(1)}, u32[]{:S(2)}, u32[]{:S(2)}) collective-permute-start(f32[2,240,384]{2,1,0:T(8,128)} %copy-done.6), channel_id=1, source_target_pairs={{0,4},{1,5},{2,6},{3,7},{4,8},{5,9},{6,10},{7,11},{8,12},{9,13},{1... | collective-permute-start | bytes 2211848 | tf_op jit(solution)/shard_map/ppermute | solution.py:415
  57.9 0.0 copy-start.5
  58.0 2.2 %copy-done.5 = f32[1,2,2,256,1024]{4,3,2,1,0:T(8,128)S(1)} copy-done((f32[1,2,2,256,1024]{4,3,2,1,0:T(8,128)S(1)}, f32[1,2,2,256,1024]{4,3,2,1,0:T(8,128)}, u32[]{:S(2)}) %copy-start.5) | copy-done | bytes 4194328
  60.1 0.0 copy-start.16
  60.2 0.0 copy-start.18
  60.2 0.0 copy-start.20
  60.2 1.2 %edges.1 = (f32[2,2,256,1024]{3,2,1,0:T(8,128)}, f32[2,16,768]{2,1,0:T(8,128)S(1)}) custom-call(f32[2,256,1024]{2,1,0:T(8,128)S(1)} %bitcast.16, f32[2,2,256,1024]{3,2,1,0:T(8,128)S(1)} %bitcast.25, f32[2,256,1024]{2,1,0:T(8,128)S(1)} %bitcast.17, f32[2,2,256,1024]{3,2,1,0:T(8,128)S(1)} %bitcast.26, ...), custom_call_target="tpu_custom_call", output_to_operand_aliasing={{0}: (6, {})} | custom-call | tf_op jit(solution)/shard_map/edges/pallas_call | solution.py:288
  61.4 3.4 %collective-permute-start.3 = (f32[2,16,768]{2,1,0:T(8,128)S(1)}, f32[2,16,768]{2,1,0:T(8,128)S(1)}, u32[]{:S(2)}, u32[]{:S(2)}) collective-permute-start(f32[2,16,768]{2,1,0:T(8,128)S(1)} %get-tuple-element.18), channel_id=1, source_target_pairs={{0,4},{1,5},{2,6},{3,7},{4,8},{5,9},{6,10},{7,11},{8,12},{9,13},{1... | collective-permute-start | bytes 294920 | tf_op jit(solution)/shard_map/ppermute | solution.py:415
  64.8 0.0 copy-done.8
  64.8 0.7 collective-permute-start.5
  65.5 0.0 collective-permute-done.10
  65.5 1.9 %collective-permute-start.6 = (f32[2,128,256]{2,1,0:T(8,128)S(1)}, f32[2,128,256]{2,1,0:T(8,128)S(1)}, u32[]{:S(2)}, u32[]{:S(2)}) collective-permute-start(f32[2,128,256]{2,1,0:T(8,128)S(1)} %get-tuple-element.22), channel_id=1, source_target_pairs={{0,4},{2,6},{3,7},{4,8},{6,10},{7,11},{8,12},{10,14},{11,15},{12,1... | collective-permute-start | bytes 786440 | tf_op jit(solution)/shard_map/ppermute | solution.py:415
  67.4 0.0 copy-done.10
  67.5 1.2 %subtract_add_fusion.1 = (f32[1,128,256]{2,1,0:T(8,128)S(1)}, f32[1,128,256]{2,1,0:T(8,128)S(1)}) fusion(f32[1,128,256]{2,1,0:T(8,128)S(1)} %copy-done.10, f32[2,128,256]{2,1,0:T(8,128)} %collective-permute-done.10, f32[256]{0:T(256)S(1)} %copy-done.16, f32[256]{0:T(256)S(1)} %copy-done.18, f32[256]{0:T(256)S(1)} %copy-done.14, f32[128]{0:T(128)S(1)} %copy-done.20, ...), kind=kLoop, calls=%fused_computation.12 | loop fusion | flops 851968 | bytes 790016 | tf_op jit(solution)/shard_map/add | solution.py:447
  68.7 0.1 subtract_add_fusion
  68.9 0.0 collective-permute-done.5.refs_2_
  68.9 18.1 %collective-permute-done.6.refs_3_ = f32[2,128,256]{2,1,0:T(8,128)S(1)} collective-permute-done((f32[2,128,256]{2,1,0:T(8,128)S(1)}, f32[2,128,256]{2,1,0:T(8,128)S(1)}, u32[]{:S(2)}, u32[]{:S(2)}) %collective-permute-start.6) | collective-permute-done | bytes 262176 | tf_op jit(solution)/shard_map/ppermute | solution.py:415
  87.0 2.3 %patch.1 = (f32[2,256,1024]{2,1,0:T(8,128)}, f32[2,2,256,1024]{3,2,1,0:T(8,128)}) custom-call(f32[2,256,1024]{2,1,0:T(8,128)S(1)} %bitcast.18, f32[2,2,256,1024]{3,2,1,0:T(8,128)} %get-tuple-element.20.refs_1_, f32[2,128,256]{2,1,0:T(8,128)S(1)} %collective-permute-done.5.refs_2_, ...), custom_call_target="tpu_custom_call", output_to_operand_aliasing={{1}: (1, {})} | custom-call | tf_op jit(solution)/shard_map/patch/pallas_call | solution.py:350
  89.3 0.0 collective-permute-done.3.edges
  89.3 0.0 collective-permute-done.4.middle
  89.4 2.7 %place.2._ = f32[2,256,1024]{2,1,0:T(8,128)} custom-call(f32[2,256,1024]{2,1,0:T(8,128)S(1)} %bitcast.19, f32[2,240,384]{2,1,0:T(8,128)} %collective-permute-done.4.middle, f32[2,16,768]{2,1,0:T(8,128)S(1)} %collective-permute-done.3.edges, f32[2,256,1024]{2,1,0:T(8,128)} %get-tuple-element.24._), custom_call_target="tpu_custom_call", output_to_operand_aliasing={{}: (3, {})} | custom-call | tf_op jit(solution)/shard_map/place/pallas_call | solution.py:376
  92.0 0.0 collective-permute-done.middle
  92.0 1.6 %place.3 = f32[2,256,1024]{2,1,0:T(8,128)} custom-call(f32[2,256,1024]{2,1,0:T(8,128)S(1)} %bitcast.20, f32[2,240,384]{2,1,0:T(8,128)S(1)} %collective-permute-done.middle, f32[2,16,768]{2,1,0:T(8,128)S(1)} %collective-permute-done.3.edges, f32[2,256,1024]{2,1,0:T(8,128)} %place.2._), custom_call_target="tpu_custom_call", output_to_operand_aliasing={{}: (3, {})} | custom-call | tf_op jit(solution)/shard_map/place/pallas_call | solution.py:376
  (22 shorter events, 0.2 us)
Async XLA Ops:
  2.5 17.2 %collective-permute-start.1 = (f32[6,4,1024]{2,1,0:T(4,128)S(1)}, f32[6,4,1024]{2,1,0:T(4,128)S(1)}, u32[]{:S(2)}, u32[]{:S(2)}) collective-permute-start(f32[6,4,1024]{2,1,0:T(4,128)S(1)} %pad_maximum_fusion.4), channel_id=1, source_target_pairs={{0,1},{1,2},{2,3},{4,5},{5,6},{6,7},{8,9},{9,10},{10,11},{12,13},{... | collective-permute-start | bytes 294920 | tf_op jit(solution)/shard_map/ppermute | solution.py:410
  4.5 15.3 %collective-permute-start.2 = (f32[6,4,1024]{2,1,0:T(4,128)S(1)}, f32[6,4,1024]{2,1,0:T(4,128)S(1)}, u32[]{:S(2)}, u32[]{:S(2)}) collective-permute-start(f32[6,4,1024]{2,1,0:T(4,128)S(1)} %pad_maximum_fusion.5), channel_id=1, source_target_pairs={{1,0},{2,1},{3,2},{5,4},{6,5},{7,6},{9,8},{10,9},{11,10},{13,12},{... | collective-permute-start | bytes 294920 | tf_op jit(solution)/shard_map/ppermute | solution.py:411
  8.1 1.6 %copy-start = (f32[1,2,256,1024]{3,2,1,0:T(8,128)S(1)}, f32[1,2,256,1024]{3,2,1,0:T(8,128)}, u32[]{:S(2)}) copy-start(f32[1,2,256,1024]{3,2,1,0:T(8,128)} %param.2) | copy-start | bytes 6291460
  9.7 2.2 %copy-start.2 = (f32[1,2,2,256,1024]{4,3,2,1,0:T(8,128)S(1)}, f32[1,2,2,256,1024]{4,3,2,1,0:T(8,128)}, u32[]{:S(2)}) copy-start(f32[1,2,2,256,1024]{4,3,2,1,0:T(8,128)} %param.3) | copy-start | bytes 12582916
  11.9 3.0 %copy-start.1 = (f32[1,2,256,1024]{3,2,1,0:T(8,128)S(1)}, f32[1,2,256,1024]{3,2,1,0:T(8,128)}, u32[]{:S(2)}) copy-start(f32[1,2,256,1024]{3,2,1,0:T(8,128)} %param.2) | copy-start | bytes 6291460
  14.9 2.2 %copy-start.3 = (f32[1,2,2,256,1024]{4,3,2,1,0:T(8,128)S(1)}, f32[1,2,2,256,1024]{4,3,2,1,0:T(8,128)}, u32[]{:S(2)}) copy-start(f32[1,2,2,256,1024]{4,3,2,1,0:T(8,128)} %param.3) | copy-start | bytes 12582916
  19.8 4.7 %copy-start.6 = (f32[2,240,384]{2,1,0:T(8,128)}, f32[2,240,384]{2,1,0:T(8,128)S(1)}, u32[]{:S(2)}) copy-start(f32[2,240,384]{2,1,0:T(8,128)S(1)} %get-tuple-element.15) | copy-start | bytes 2211844
  19.8 2.5 %copy-start.4 = (f32[1,2,2,256,1024]{4,3,2,1,0:T(8,128)S(1)}, f32[1,2,2,256,1024]{4,3,2,1,0:T(8,128)}, u32[]{:S(2)}) copy-start(f32[1,2,2,256,1024]{4,3,2,1,0:T(8,128)} %param.3) | copy-start | bytes 12582916
  24.4 31.5 %copy-start.7 = (f32[2,128,256]{2,1,0:T(8,128)}, f32[2,128,256]{2,1,0:T(8,128)S(1)}, u32[]{:S(2)}) copy-start(f32[2,128,256]{2,1,0:T(8,128)S(1)} %get-tuple-element.21) | copy-start | bytes 786436
  24.4 8.3 %collective-permute-start.8 = (f32[2,128,256]{2,1,0:T(8,128)S(1)}, f32[2,128,256]{2,1,0:T(8,128)S(1)}, u32[]{:S(2)}, u32[]{:S(2)}) collective-permute-start(f32[2,128,256]{2,1,0:T(8,128)S(1)} %get-tuple-element.23), channel_id=1, source_target_pairs={{1,9},{2,10},{5,13},{6,14},{9,17},{10,18},{13,21},{14,22},{17,25},... | collective-permute-start | bytes 786440 | tf_op jit(solution)/shard_map/ppermute | solution.py:415
  27.9 12.0 %collective-permute-start.7 = (f32[2,128,256]{2,1,0:T(8,128)S(1)}, f32[2,128,256]{2,1,0:T(8,128)S(1)}, u32[]{:S(2)}, u32[]{:S(2)}) collective-permute-start(f32[2,128,256]{2,1,0:T(8,128)S(1)} %get-tuple-element.23), channel_id=1, source_target_pairs={{1,5},{2,6},{5,9},{6,10},{9,13},{10,14},{13,17},{14,18},{17,21},{1... | collective-permute-start | bytes 786440 | tf_op jit(solution)/shard_map/ppermute | solution.py:415
  31.4 24.6 %copy-start.19 = (f32[128]{0:T(128)}, f32[128]{0:T(128)S(1)}, u32[]{:S(2)}) copy-start(f32[128]{0:T(128)S(1)} %multiply_multiply_fusion.1) | copy-start | bytes 1540
  31.4 24.6 %copy-start.17 = (f32[256]{0:T(256)}, f32[256]{0:T(256)S(1)}, u32[]{:S(2)}) copy-start(f32[256]{0:T(256)S(1)} %fusion.2) | copy-start | bytes 3076
  31.4 24.5 %copy-start.13 = (f32[256]{0:T(256)}, f32[256]{0:T(256)S(1)}, u32[]{:S(2)}) copy-start(f32[256]{0:T(256)S(1)} %get-tuple-element.42) | copy-start | bytes 3076
  31.4 24.5 %copy-start.15 = (f32[256]{0:T(256)}, f32[256]{0:T(256)S(1)}, u32[]{:S(2)}) copy-start(f32[256]{0:T(256)S(1)} %get-tuple-element.43) | copy-start | bytes 3076
  40.1 8.3 %collective-permute-start.9 = (f32[2,128,256]{2,1,0:T(8,128)S(1)}, f32[2,128,256]{2,1,0:T(8,128)S(1)}, u32[]{:S(2)}, u32[]{:S(2)}) collective-permute-start(f32[2,128,256]{2,1,0:T(8,128)S(1)} %pad_maximum_fusion), channel_id=1, source_target_pairs={{1,9},{2,10},{5,13},{6,14},{9,17},{10,18},{13,21},{14,22},{17,25},... | collective-permute-start | bytes 786440 | tf_op jit(solution)/shard_map/ppermute | solution.py:415
  48.5 7.5 %copy-start.9 = (f32[1,128,256]{2,1,0:T(8,128)}, f32[1,128,256]{2,1,0:T(8,128)S(1)}, u32[]{:S(2)}) copy-start(f32[1,128,256]{2,1,0:T(8,128)S(1)} %get-tuple-element.38) | copy-start | bytes 393220
  48.5 7.5 %copy-start.11 = (f32[1,128,256]{2,1,0:T(8,128)}, f32[1,128,256]{2,1,0:T(8,128)S(1)}, u32[]{:S(2)}) copy-start(f32[1,128,256]{2,1,0:T(8,128)S(1)} %get-tuple-element.39) | copy-start | bytes 393220
  49.3 16.2 %collective-permute-start.10 = (f32[2,128,256]{2,1,0:T(8,128)}, f32[2,128,256]{2,1,0:T(8,128)}, u32[]{:S(2)}, u32[]{:S(2)}) collective-permute-start(f32[2,128,256]{2,1,0:T(8,128)} %pad_maximum_fusion.1), channel_id=1, source_target_pairs={{1,17},{2,18},{5,21},{6,22},{9,25},{10,26},{13,29},{14,30}} | collective-permute-start | bytes 786440 | tf_op jit(solution)/shard_map/ppermute | solution.py:415
  50.6 38.8 %collective-permute-start.4 = (f32[2,240,384]{2,1,0:T(8,128)}, f32[2,240,384]{2,1,0:T(8,128)}, u32[]{:S(2)}, u32[]{:S(2)}) collective-permute-start(f32[2,240,384]{2,1,0:T(8,128)} %get-tuple-element.19), channel_id=1, source_target_pairs={{0,4},{1,5},{2,6},{3,7},{4,8},{5,9},{6,10},{7,11},{8,12},{9,13},{1... | collective-permute-start | bytes 2211848 | tf_op jit(solution)/shard_map/ppermute | solution.py:415
  56.0 36.0 %collective-permute-start = (f32[2,240,384]{2,1,0:T(8,128)}, f32[2,240,384]{2,1,0:T(8,128)S(1)}, u32[]{:S(2)}, u32[]{:S(2)}) collective-permute-start(f32[2,240,384]{2,1,0:T(8,128)} %copy-done.6), channel_id=1, source_target_pairs={{0,4},{1,5},{2,6},{3,7},{4,8},{5,9},{6,10},{7,11},{8,12},{9,13},{1... | collective-permute-start | bytes 2211848 | tf_op jit(solution)/shard_map/ppermute | solution.py:415
  57.9 2.2 %copy-start.5 = (f32[1,2,2,256,1024]{4,3,2,1,0:T(8,128)S(1)}, f32[1,2,2,256,1024]{4,3,2,1,0:T(8,128)}, u32[]{:S(2)}) copy-start(f32[1,2,2,256,1024]{4,3,2,1,0:T(8,128)} %param.3) | copy-start | bytes 12582916
  60.1 4.7 %copy-start.8 = (f32[2,128,256]{2,1,0:T(8,128)S(1)}, f32[2,128,256]{2,1,0:T(8,128)}, u32[]{:S(2)}) copy-start(f32[2,128,256]{2,1,0:T(8,128)} %copy-done.7) | copy-start | bytes 786436
  60.1 7.3 %copy-start.10 = (f32[1,128,256]{2,1,0:T(8,128)S(1)}, f32[1,128,256]{2,1,0:T(8,128)}, u32[]{:S(2)}) copy-start(f32[1,128,256]{2,1,0:T(8,128)} %copy-done.9) | copy-start | bytes 393220
  60.1 7.3 %copy-start.12 = (f32[1,128,256]{2,1,0:T(8,128)S(1)}, f32[1,128,256]{2,1,0:T(8,128)}, u32[]{:S(2)}) copy-start(f32[1,128,256]{2,1,0:T(8,128)} %copy-done.11) | copy-start | bytes 393220
  60.1 7.3 %copy-start.14 = (f32[256]{0:T(256)S(1)}, f32[256]{0:T(256)}, u32[]{:S(2)}) copy-start(f32[256]{0:T(256)} %copy-done.13) | copy-start | bytes 3076
  60.1 7.3 %copy-start.16 = (f32[256]{0:T(256)S(1)}, f32[256]{0:T(256)}, u32[]{:S(2)}) copy-start(f32[256]{0:T(256)} %copy-done.15) | copy-start | bytes 3076
  60.2 7.3 %copy-start.18 = (f32[256]{0:T(256)S(1)}, f32[256]{0:T(256)}, u32[]{:S(2)}) copy-start(f32[256]{0:T(256)} %copy-done.17) | copy-start | bytes 3076
  60.2 7.3 %copy-start.20 = (f32[128]{0:T(128)S(1)}, f32[128]{0:T(128)}, u32[]{:S(2)}) copy-start(f32[128]{0:T(128)} %copy-done.19) | copy-start | bytes 1540
  61.4 27.9 %collective-permute-start.3 = (f32[2,16,768]{2,1,0:T(8,128)S(1)}, f32[2,16,768]{2,1,0:T(8,128)S(1)}, u32[]{:S(2)}, u32[]{:S(2)}) collective-permute-start(f32[2,16,768]{2,1,0:T(8,128)S(1)} %get-tuple-element.18), channel_id=1, source_target_pairs={{0,4},{1,5},{2,6},{3,7},{4,8},{5,9},{6,10},{7,11},{8,12},{9,13},{1... | collective-permute-start | bytes 294920 | tf_op jit(solution)/shard_map/ppermute | solution.py:415
  64.8 4.1 %collective-permute-start.5 = (f32[2,128,256]{2,1,0:T(8,128)S(1)}, f32[2,128,256]{2,1,0:T(8,128)S(1)}, u32[]{:S(2)}, u32[]{:S(2)}) collective-permute-start(f32[2,128,256]{2,1,0:T(8,128)S(1)} %copy-done.8), channel_id=1, source_target_pairs={{0,4},{1,5},{3,7},{4,8},{5,9},{7,11},{8,12},{9,13},{11,15},{12,16}... | collective-permute-start | bytes 786440 | tf_op jit(solution)/shard_map/ppermute | solution.py:415
  65.5 21.5 %collective-permute-start.6 = (f32[2,128,256]{2,1,0:T(8,128)S(1)}, f32[2,128,256]{2,1,0:T(8,128)S(1)}, u32[]{:S(2)}, u32[]{:S(2)}) collective-permute-start(f32[2,128,256]{2,1,0:T(8,128)S(1)} %get-tuple-element.22), channel_id=1, source_target_pairs={{0,4},{2,6},{3,7},{4,8},{6,10},{7,11},{8,12},{10,14},{11,15},{12,1... | collective-permute-start | bytes 786440 | tf_op jit(solution)/shard_map/ppermute | solution.py:415

commit v3 on v2

--- a/solution.py
+++ b/solution.py
@@ -6,6 +6,7 @@
 from jax.experimental import pallas as pl
 from jax.experimental.pallas import tpu as pltpu
 from jax.sharding import PartitionSpec as P
+
 
 COARSE_SHARE = 4
 LANES = 128
@@ -32,7 +33,7 @@
 
 
 def fine_kernel(*refs, first_block, coarse, size_x, size_y, coarse_rows, pieces, aliased):
-    begin, old = refs[:2]
+    begin_hbm, old_hbm = refs[:2]
     refs = refs[2:]
     if coarse:
         before, after = refs[:2]
@@ -43,8 +44,25 @@
     offset = None
     if coarse:
         offset, refs = refs[0], refs[1:]
-    wide_one, wide_two, inner, inverse = refs
-    rows = begin.shape[1]
+    wide_one, wide_two, inner, inverse, begin_all, old_all, sems = refs
+    rows = begin_hbm.shape[1]
+    step = pl.program_id(0)
+
+    def loads(k):
+        cut = pl.ds((first_block + k) * LANES, LANES)
+        return (pltpu.make_async_copy(begin_hbm.at[:, :, cut], begin_all.at[k], sems.at[0, k]),
+                pltpu.make_async_copy(old_hbm.at[:, :, :, cut], old_all.at[k], sems.at[1, k]))
+
+    @pl.when(step == 0)
+    def _():
+        for k in range(begin_all.shape[0]):
+            for copy in loads(k):
+                copy.start()
+
+    for copy in loads(step):
+        copy.wait()
+    begin = begin_all.at[step]
+    old = old_all.at[step]
     rank = lax.axis_index("space")
     ranks = lax.axis_size("space")
     spot = pl.ds(pl.multiple_of(pl.program_id(0) * LANES, LANES), LANES)
@@ -168,10 +186,17 @@
 
 VMEM = pl.BlockSpec(memory_space=pltpu.VMEM)
 ANY = pl.BlockSpec(memory_space=pl.ANY)
-PARAMS = pltpu.CompilerParams(vmem_limit_bytes=28 * 1024 * 1024)
-
-
-def fine_call(begin, old, halo, nodes, first, width, pieces, size_x, coarse_rows):
+HBM = pl.BlockSpec(memory_space=pltpu.HBM)
+
+
+def grant(mebibytes):
+    return pltpu.CompilerParams(vmem_limit_bytes=mebibytes * 1024 * 1024)
+
+
+PARAMS = grant(28)
+
+
+def fine_call(begin, old, halo, nodes, first, width, pieces, size_x, coarse_rows, params):
     rows, columns = begin.shape[1:]
     coarse = halo is not None
     base = first // LANES
@@ -184,10 +209,7 @@
     if coarse:
         out_shape.append(jax.ShapeDtypeStruct((2, coarse_rows, width), f32))
         out_specs.append(VMEM)
-    in_specs = [
-        pl.BlockSpec((2, rows, LANES), lambda j: (0, 0, base + j)),
-        pl.BlockSpec((2, 2, rows, LANES), lambda j: (0, 0, 0, base + j)),
-    ]
+    in_specs = [HBM, HBM]
     operands = [begin, old]
     if coarse:
         operands += list(halo)
@@ -200,20 +222,33 @@
     kernel = functools.partial(
         fine_kernel, first_block=base, coarse=coarse, size_x=size_x, size_y=columns,
         coarse_rows=coarse_rows, pieces=pieces, aliased=len(aliases))
+    blocks = width // LANES
     scratch = [pltpu.VMEM((2, rows + 2 * PAD, LANES), f32) for _ in range(4)]
+    scratch += [pltpu.VMEM((blocks, 2, rows, LANES), f32), pltpu.VMEM((blocks, 2, 2, rows, LANES), f32),
+                pltpu.SemaphoreType.DMA((2, blocks))]
     return pl.pallas_call(
-        kernel, grid=(width // LANES,), in_specs=in_specs, out_specs=out_specs, out_shape=out_shape,
-        scratch_shapes=scratch, input_output_aliases=aliases, compiler_params=PARAMS,
+        kernel, grid=(blocks,), in_specs=in_specs, out_specs=out_specs, out_shape=out_shape,
+        scratch_shapes=scratch, input_output_aliases=aliases, compiler_params=params,
         name="fine_coarse" if coarse else "fine",
     )(*operands)
 
 
-def edge_kernel(begin_top, old_top, begin_end, old_end, before, after, _, nodes, send, wide, fixed, sems,
+def edge_kernel(begin_hbm, old_hbm, before, after, _, nodes, send, wide, fixed, begin_sides, old_sides, sems,
                 *, rows, size_x, size_y, outer):
     rank = lax.axis_index("space")
-    ranks = lax.axis_size("space")
-    side_rows = begin_top.shape[1]
+    side_rows = begin_sides.shape[2]
     height = HALO + side_rows
+    loads = []
+    for k in range(2):
+        cut = pl.ds(0 if k == 0 else rows - side_rows, side_rows)
+        loads.append(pltpu.make_async_copy(begin_hbm.at[:, cut, :], begin_sides.at[k], sems.at[k]))
+        loads.append(pltpu.make_async_copy(old_hbm.at[:, :, cut, :], old_sides.at[k], sems.at[2 + k]))
+    for copy in loads:
+        copy.start()
+    for copy in loads:
+        copy.wait()
+    begin_top, begin_end = begin_sides.at[0], begin_sides.at[1]
+    old_top, old_end = old_sides.at[0], old_sides.at[1]
     copies = []
     for k, (low, width, spot) in enumerate(outer):
         cut = pl.ds(low, width)
@@ -265,7 +300,7 @@
                 send[part, pl.ds(at, PAD), pl.ds(spot, width)] = n2[part][keep]
             copy = pltpu.make_async_copy(
                 fixed.at[:, :, pl.ds(at, PAD), pl.ds(spot, width)],
-                nodes.at[:, :, pl.ds(0 if top else rows - PAD, PAD), cut], sems.at[2 * k + (not top)])
+                nodes.at[:, :, pl.ds(0 if top else rows - PAD, PAD), cut], sems.at[4 + 2 * k + (not top)])
             copy.start()
             copies.append(copy)
     for copy in copies:
@@ -275,7 +310,6 @@
 def edge_call(begin, old, halo, nodes, outer, size_x):
     rows, columns = begin.shape[1:]
     side = 2 * PAD
-    last = rows // side - 1
     total = sum(width for _, width in outer)
     f32 = jnp.float32
     spots, at = [], 0
@@ -287,17 +321,14 @@
     kernel = functools.partial(edge_kernel, rows=rows, size_x=size_x, size_y=columns, outer=spots)
     return pl.pallas_call(
         kernel, grid=(1,),
-        in_specs=[pl.BlockSpec((2, side, columns), lambda j: (0, 0, 0)),
-                  pl.BlockSpec((2, 2, side, columns), lambda j: (0, 0, 0, 0)),
-                  pl.BlockSpec((2, side, columns), lambda j: (0, last, 0)),
-                  pl.BlockSpec((2, 2, side, columns), lambda j: (0, 0, last, 0)),
-                  VMEM, VMEM, ANY],
+        in_specs=[HBM, HBM, VMEM, VMEM, ANY],
         out_specs=[ANY, VMEM],
         out_shape=[jax.ShapeDtypeStruct(nodes.shape, f32), jax.ShapeDtypeStruct((2, side, total), f32)],
         scratch_shapes=[pltpu.VMEM((2, 2 * PAD + HALO + side + PAD, widest), f32),
-                        pltpu.VMEM((2, 2, side, total), f32), pltpu.SemaphoreType.DMA((2 * len(outer),))],
-        input_output_aliases={6: 0}, compiler_params=PARAMS, name="edges",
-    )(begin, old, begin, old, halo[0], halo[1], nodes)
+                        pltpu.VMEM((2, 2, side, total), f32), pltpu.VMEM((2, 2, side, columns), f32),
+                        pltpu.VMEM((2, 2, 2, side, columns), f32), pltpu.SemaphoreType.DMA((4 + 2 * len(outer),))],
+        input_output_aliases={4: 0}, compiler_params=grant(57), name="edges",
+    )(begin, old, halo[0], halo[1], nodes)
 
 
 def patch_kernel(*refs, count, pieces, coarse_rows):
@@ -428,13 +459,13 @@
     second = low_column + width
     rest = columns - second
     inside = [(PAD, rows - PAD)]
-    nodes, left = fine_call(begin, old, None, None, 0, low_column, inside, size_x, coarse_rows)
+    nodes, left = fine_call(begin, old, None, None, 0, low_column, inside, size_x, coarse_rows, grant(62))
     left = ahead(left, 1, everyone)
-    nodes, right = fine_call(begin, old, None, nodes, second, rest, inside, size_x, coarse_rows)
-    made = fine_call(begin, old, (before, after), nodes, low_column, width, pieces, size_x, coarse_rows)
+    made = fine_call(begin, old, (before, after), nodes, low_column, width, pieces, size_x, coarse_rows, grant(60))
     nodes, inner_sends, offset = made[0], made[1:-1], made[-1]
     one_back = ahead(offset, 1, middle)
     two_back = ahead(offset, 2, middle)
+    nodes, right = fine_call(begin, old, None, nodes, second, rest, inside, size_x, coarse_rows, grant(58))
     right = ahead(right, 1, everyone)
     nodes, edges = edge_call(begin, old, (before, after), nodes, [(0, low_column), (second, rest)], size_x)
     edges = ahead(edges, 1, everyone)

time: 94.3 us -> 85 us (0.901)
  local copies, waits for them, and re-layouts: 12.5 us -> 2.53 us
  Pallas kernels: 15.6 us -> 21.8 us
  waiting for transfers between devices: 31.9 us -> 28.6 us
  other arithmetic: 2.54 us -> 0.8 us
    unnamed x42 -> x14, local copies, waits for them, and re-layouts: 10.7 us -> 0.68 us
    pallas_call x4, Pallas kernels: 9.08 us -> 16.4 us  [the longest x3 12.2 us: fine_call(): pl.pallas_call(kernel, grid=(blocks,), in_specs=in_specs, out_specs=out_s...]
    ppermute x9, waiting for transfers between devices: 31.9 us -> 28.6 us  [ahead(): return lax.ppermute(value, ('tm', 'space'), pairs)]
    pallas_call x2, Pallas kernels: 4.22 us -> 3.14 us  [place_call(): pl.pallas_call(functools.partial(place_kernel, spot=spot), grid=(middle.s...]
    add x4, other arithmetic: 1.61 us -> 0.63 us  [add(): return jnp.stack([total[0] + grown[0], total[1] + grown[1]])]
  transfers between devices with their start and end apart: 11 -> 11, of which waited for: 4 -> 4; matrix products, arithmetic and copies ran while one was open for 2% -> 1% of each run, Pallas kernels for 13% -> 19%
where the time goes in v3:
time: 85 us; the launch traced here: 84.4 us
  starting transfers between devices  29.6 us (35%)
  waiting for transfers between devices  28.6 us (34%)
  Pallas kernels  21.8 us (26%)
  local copies, waits for them, and re-layouts  2.53 us (3%)
  between operations  0.98 us (1%)
    ppermute x9, waiting for transfers between devices, ahead(): return lax.ppermute(value, ('tm', 'space'), pairs)  28.6 us
    ppermute x9, starting transfers between devices, ahead(): return lax.ppermute(value, ('tm', 'space'), pairs)  24.1 us
    pallas_call x3, Pallas kernels, fine_call(): pl.pallas_call(kernel, grid=(blocks,), in_specs=in_specs, out_specs=out_s...  12.2 us
    pallas_call x1, Pallas kernels, edge_call(): pl.pallas_call(kernel, grid=(1,), in_specs=[HBM, HBM, VMEM, VMEM, ANY], o...  4.13 us
    ppermute x1, starting transfers between devices, body(): after = lax.ppermute(edge(0), 'space', [(j, i) for i, j in up])  3.64 us
    pallas_call x2, Pallas kernels, place_call(): pl.pallas_call(functools.partial(place_kernel, spot=spot), grid=(middle.s...  3.14 us
    pallas_call x1, Pallas kernels, patch_call(): pl.pallas_call(kernel, grid=(fresh.shape[2] // LANES,), in_specs=[begin_s...  2.32 us
    ppermute x1, starting transfers between devices, body(): before = lax.ppermute(edge(rows - HALO), 'space', up)  1.92 us
  transfers between devices with their start and end apart: 11, of which 4 were waited for; matrix products, arithmetic and copies ran while one was open for 1% of the time, Pallas kernels for 19%

profile of v3, /device:TPU:18, one launch (start us, length us, event | category | flops | bytes accessed | tf_op | source)
XLA Modules:
  0.0 84.4 jit_solution(6202639947981766697)
XLA Ops:
  0.6 0.9 %fusion.3 = (f32[2,4,1024]{2,1,0:T(4,128)S(1)}, f32[2,4,1024]{2,1,0:T(4,128)S(1)}) fusion(f32[2,256,1024]{2,1,0:T(8,128)} %bitcast.12), kind=kLoop, calls=%fused_computation.31 | loop fusion | bytes 131072 | tf_op jit(solution)/shard_map/slice | solution.py:437
  1.5 1.0 %slice_bitcast_fusion.1 = (f32[2,4,1024]{2,1,0:T(4,128)S(1)}, f32[2,4,1024]{2,1,0:T(4,128)S(1)}, f32[2,4,1024]{2,1,0:T(4,128)S(1)}, f32[2,4,1024]{2,1,0:T(4,128)S(1)}) fusion(f32[2,2,256,1024]{3,2,1,0:T(8,128)} %bitcast.20), kind=kLoop, calls=%fused_computation.23 | loop fusion | bytes 262144 | tf_op jit(solution)/shard_map/squeeze | solution.py:437
  2.5 1.9 %collective-permute-start = (f32[6,4,1024]{2,1,0:T(4,128)S(1)}, f32[6,4,1024]{2,1,0:T(4,128)S(1)}, u32[]{:S(2)}, u32[]{:S(2)}) collective-permute-start(f32[6,4,1024]{2,1,0:T(4,128)S(1)} %pad_maximum_fusion.4), channel_id=1, source_target_pairs={{0,1},{1,2},{2,3},{4,5},{5,6},{6,7},{8,9},{9,10},{10,11},{12,13},{... | collective-permute-start | bytes 294920 | tf_op jit(solution)/shard_map/ppermute | solution.py:441
  4.5 3.6 %collective-permute-start.1 = (f32[6,4,1024]{2,1,0:T(4,128)S(1)}, f32[6,4,1024]{2,1,0:T(4,128)S(1)}, u32[]{:S(2)}, u32[]{:S(2)}) collective-permute-start(f32[6,4,1024]{2,1,0:T(4,128)S(1)} %pad_maximum_fusion.5), channel_id=1, source_target_pairs={{1,0},{2,1},{3,2},{5,4},{6,5},{7,6},{9,8},{10,9},{11,10},{13,12},{... | collective-permute-start | bytes 294920 | tf_op jit(solution)/shard_map/ppermute | solution.py:442
  8.1 3.9 %fine.2 = (f32[2,2,256,1024]{3,2,1,0:T(8,128)}, f32[2,240,384]{2,1,0:T(8,128)}) custom-call(f32[2,256,1024]{2,1,0:T(8,128)} %bitcast.13, f32[2,2,256,1024]{3,2,1,0:T(8,128)} %bitcast.21), custom_call_target="tpu_custom_call" | custom-call | tf_op jit(solution)/shard_map/fine/pallas_call | solution.py:229
  12.0 0.0 collective-permute-done.refs_2_.before
  12.0 0.0 copy-start.1
  12.1 0.0 collective-permute-done.1.refs_3_.after
  12.1 0.0 copy-start.2
  12.1 0.6 copy-done.1
  12.7 0.0 copy-done.2
  12.7 0.0 copy-start.4
  12.7 4.4 %fine_coarse.1 = (f32[2,2,256,1024]{3,2,1,0:T(8,128)}, f32[2,128,256]{2,1,0:T(8,128)}, f32[2,128,256]{2,1,0:T(8,128)}, f32[2,128,256]{2,1,0:T(8,128)}) custom-call(f32[2,256,1024]{2,1,0:T(8,128)} %bitcast.14, f32[2,2,256,1024]{3,2,1,0:T(8,128)} %bitcast.22, f32[6,4,1024]{2,1,0:T(4,128)} %copy-done.1, ...), custom_call_target="tpu_custom_call", output_to_operand_aliasing={{0}: (4, {})} | custom-call | tf_op jit(solution)/shard_map/fine_coarse/pallas_call | solution.py:229
  17.2 3.5 %collective-permute-start.8 = (f32[2,128,256]{2,1,0:T(8,128)}, f32[2,128,256]{2,1,0:T(8,128)S(1)}, u32[]{:S(2)}, u32[]{:S(2)}) collective-permute-start(f32[2,128,256]{2,1,0:T(8,128)} %get-tuple-element.23), channel_id=1, source_target_pairs={{1,9},{2,10},{5,13},{6,14},{9,17},{10,18},{13,21},{14,22},{17,25},... | collective-permute-start | bytes 786440 | tf_op jit(solution)/shard_map/ppermute | solution.py:446
  20.7 3.4 %collective-permute-start.7 = (f32[2,128,256]{2,1,0:T(8,128)}, f32[2,128,256]{2,1,0:T(8,128)S(1)}, u32[]{:S(2)}, u32[]{:S(2)}) collective-permute-start(f32[2,128,256]{2,1,0:T(8,128)} %get-tuple-element.23), channel_id=1, source_target_pairs={{1,5},{2,6},{5,9},{6,10},{9,13},{10,14},{13,17},{14,18},{17,21},{1... | collective-permute-start | bytes 786440 | tf_op jit(solution)/shard_map/ppermute | solution.py:446
  24.1 1.5 %collective-permute-done.8 = f32[2,128,256]{2,1,0:T(8,128)S(1)} collective-permute-done((f32[2,128,256]{2,1,0:T(8,128)}, f32[2,128,256]{2,1,0:T(8,128)S(1)}, u32[]{:S(2)}, u32[]{:S(2)}) %collective-permute-start.8) | collective-permute-done | bytes 262176 | tf_op jit(solution)/shard_map/ppermute | solution.py:446
  25.6 8.6 %collective-permute-done.7 = f32[2,128,256]{2,1,0:T(8,128)S(1)} collective-permute-done((f32[2,128,256]{2,1,0:T(8,128)}, f32[2,128,256]{2,1,0:T(8,128)S(1)}, u32[]{:S(2)}, u32[]{:S(2)}) %collective-permute-start.7) | collective-permute-done | bytes 262176 | tf_op jit(solution)/shard_map/ppermute | solution.py:446
  34.3 0.1 slice_add_fusion.1
  34.4 3.5 %collective-permute-start.9 = (f32[2,128,256]{2,1,0:T(8,128)S(1)}, f32[2,128,256]{2,1,0:T(8,128)S(1)}, u32[]{:S(2)}, u32[]{:S(2)}) collective-permute-start(f32[2,128,256]{2,1,0:T(8,128)S(1)} %pad_maximum_fusion), channel_id=1, source_target_pairs={{1,9},{2,10},{5,13},{6,14},{9,17},{10,18},{13,21},{14,22},{17,25},... | collective-permute-start | bytes 786440 | tf_op jit(solution)/shard_map/ppermute | solution.py:446
  37.9 4.8 %collective-permute-done.9 = f32[2,128,256]{2,1,0:T(8,128)S(1)} collective-permute-done((f32[2,128,256]{2,1,0:T(8,128)S(1)}, f32[2,128,256]{2,1,0:T(8,128)S(1)}, u32[]{:S(2)}, u32[]{:S(2)}) %collective-permute-start.9) | collective-permute-done | bytes 262176 | tf_op jit(solution)/shard_map/ppermute | solution.py:446
  42.7 0.2 subtract_add_fusion.2
  42.9 1.3 %collective-permute-start.10 = (f32[2,128,256]{2,1,0:T(8,128)S(1)}, f32[2,128,256]{2,1,0:T(8,128)S(1)}, u32[]{:S(2)}, u32[]{:S(2)}) collective-permute-start(f32[2,128,256]{2,1,0:T(8,128)S(1)} %pad_maximum_fusion.1), channel_id=1, source_target_pairs={{1,17},{2,18},{5,21},{6,22},{9,25},{10,26},{13,29},{14,30}} | collective-permute-start | bytes 786440 | tf_op jit(solution)/shard_map/ppermute | solution.py:446
  44.2 0.0 copy-done.4
  44.2 4.5 %collective-permute-start.4 = (f32[2,240,384]{2,1,0:T(8,128)S(1)}, f32[2,240,384]{2,1,0:T(8,128)S(1)}, u32[]{:S(2)}, u32[]{:S(2)}) collective-permute-start(f32[2,240,384]{2,1,0:T(8,128)S(1)} %copy-done.4), channel_id=1, source_target_pairs={{0,4},{1,5},{2,6},{3,7},{4,8},{5,9},{6,10},{7,11},{8,12},{9,13},{1... | collective-permute-start | bytes 2211848 | tf_op jit(solution)/shard_map/ppermute | solution.py:446
  48.7 0.0 copy-start.6
  48.7 0.0 copy-start.5
  48.7 3.9 %fine.3 = (f32[2,2,256,1024]{3,2,1,0:T(8,128)}, f32[2,240,384]{2,1,0:T(8,128)}) custom-call(f32[2,256,1024]{2,1,0:T(8,128)} %bitcast.15, f32[2,2,256,1024]{3,2,1,0:T(8,128)} %bitcast.23, f32[2,2,256,1024]{3,2,1,0:T(8,128)} %get-tuple-element.15.refs_2_), custom_call_target="tpu_custom_call", output_to_operand_aliasing={{0}: (2, {})} | custom-call | tf_op jit(solution)/shard_map/fine/pallas_call | solution.py:229
  52.7 2.4 %collective-permute-start.2 = (f32[2,240,384]{2,1,0:T(8,128)}, f32[2,240,384]{2,1,0:T(8,128)S(1)}, u32[]{:S(2)}, u32[]{:S(2)}) collective-permute-start(f32[2,240,384]{2,1,0:T(8,128)} %get-tuple-element.16), channel_id=1, source_target_pairs={{0,4},{1,5},{2,6},{3,7},{4,8},{5,9},{6,10},{7,11},{8,12},{9,13},{1... | collective-permute-start | bytes 2211848 | tf_op jit(solution)/shard_map/ppermute | solution.py:446
  55.1 0.0 copy-done.6
  55.1 0.7 collective-permute-start.5
  55.8 0.0 copy-done.5
  55.8 2.9 %collective-permute-start.6 = (f32[2,128,256]{2,1,0:T(8,128)S(1)}, f32[2,128,256]{2,1,0:T(8,128)S(1)}, u32[]{:S(2)}, u32[]{:S(2)}) collective-permute-start(f32[2,128,256]{2,1,0:T(8,128)S(1)} %copy-done.5), channel_id=1, source_target_pairs={{0,4},{2,6},{3,7},{4,8},{6,10},{7,11},{8,12},{10,14},{11,15},{12,1... | collective-permute-start | bytes 786440 | tf_op jit(solution)/shard_map/ppermute | solution.py:446
  58.7 0.0 copy-start.3
  58.7 0.0 copy-start
  58.7 4.1 %edges.1 = (f32[2,2,256,1024]{3,2,1,0:T(8,128)}, f32[2,16,768]{2,1,0:T(8,128)}) custom-call(f32[2,256,1024]{2,1,0:T(8,128)} %bitcast.16, f32[2,2,256,1024]{3,2,1,0:T(8,128)} %bitcast.24, f32[6,4,1024]{2,1,0:T(4,128)} %copy-done.1, f32[6,4,1024]{2,1,0:T(4,128)} %copy-done.2, f32[2,2,256,1024]{3,2,1,0:T(8,128)} %get-tuple-element.17._), custom_call_target="tpu_custom_call", output_to_operand_aliasing={{0}: (4, {})} | custom-call | tf_op jit(solution)/shard_map/edges/pallas_call | solution.py:322
  62.9 0.0 collective-permute-done.10
  62.9 1.9 %collective-permute-start.3 = (f32[2,16,768]{2,1,0:T(8,128)}, f32[2,16,768]{2,1,0:T(8,128)S(1)}, u32[]{:S(2)}, u32[]{:S(2)}) collective-permute-start(f32[2,16,768]{2,1,0:T(8,128)} %get-tuple-element.18), channel_id=1, source_target_pairs={{0,4},{1,5},{2,6},{3,7},{4,8},{5,9},{6,10},{7,11},{8,12},{9,13},{1... | collective-permute-start | bytes 294920 | tf_op jit(solution)/shard_map/ppermute | solution.py:446
  64.8 0.2 subtract_add_fusion.1
  65.0 0.0 copy-done.3
  65.0 0.1 subtract_add_fusion
  65.2 0.0 collective-permute-done.5.refs_2_
  65.2 13.7 %collective-permute-done.6.refs_3_ = f32[2,128,256]{2,1,0:T(8,128)S(1)} collective-permute-done((f32[2,128,256]{2,1,0:T(8,128)S(1)}, f32[2,128,256]{2,1,0:T(8,128)S(1)}, u32[]{:S(2)}, u32[]{:S(2)}) %collective-permute-start.6) | collective-permute-done | bytes 262176 | tf_op jit(solution)/shard_map/ppermute | solution.py:446
  78.9 0.0 copy-done
  78.9 2.3 %patch.1 = (f32[2,256,1024]{2,1,0:T(8,128)}, f32[2,2,256,1024]{3,2,1,0:T(8,128)}) custom-call(f32[2,256,1024]{2,1,0:T(8,128)S(1)} %bitcast.17, f32[2,2,256,1024]{3,2,1,0:T(8,128)} %get-tuple-element.20.refs_1_, f32[2,128,256]{2,1,0:T(8,128)S(1)} %collective-permute-done.5.refs_2_, ...), custom_call_target="tpu_custom_call", output_to_operand_aliasing={{1}: (1, {})} | custom-call | tf_op jit(solution)/shard_map/patch/pallas_call | solution.py:381
  81.2 0.0 collective-permute-done.3.edges
  81.2 0.0 collective-permute-done.4.middle
  81.2 1.6 %place.2._ = f32[2,256,1024]{2,1,0:T(8,128)} custom-call(f32[2,256,1024]{2,1,0:T(8,128)S(1)} %bitcast.18, f32[2,240,384]{2,1,0:T(8,128)S(1)} %collective-permute-done.4.middle, f32[2,16,768]{2,1,0:T(8,128)S(1)} %collective-permute-done.3.edges, f32[2,256,1024]{2,1,0:T(8,128)} %get-tuple-element.24._), custom_call_target="tpu_custom_call", output_to_operand_aliasing={{}: (3, {})} | custom-call | tf_op jit(solution)/shard_map/place/pallas_call | solution.py:407
  82.8 0.0 collective-permute-done.2.middle
  82.8 1.6 %place.3 = f32[2,256,1024]{2,1,0:T(8,128)} custom-call(f32[2,256,1024]{2,1,0:T(8,128)S(1)} %bitcast.19, f32[2,240,384]{2,1,0:T(8,128)S(1)} %collective-permute-done.2.middle, f32[2,16,768]{2,1,0:T(8,128)S(1)} %collective-permute-done.3.edges, f32[2,256,1024]{2,1,0:T(8,128)} %place.2._), custom_call_target="tpu_custom_call", output_to_operand_aliasing={{}: (3, {})} | custom-call | tf_op jit(solution)/shard_map/place/pallas_call | solution.py:407
  (9 shorter events, 0.2 us)
Async XLA Ops:
  2.5 9.5 %collective-permute-start = (f32[6,4,1024]{2,1,0:T(4,128)S(1)}, f32[6,4,1024]{2,1,0:T(4,128)S(1)}, u32[]{:S(2)}, u32[]{:S(2)}) collective-permute-start(f32[6,4,1024]{2,1,0:T(4,128)S(1)} %pad_maximum_fusion.4), channel_id=1, source_target_pairs={{0,1},{1,2},{2,3},{4,5},{5,6},{6,7},{8,9},{9,10},{10,11},{12,13},{... | collective-permute-start | bytes 294920 | tf_op jit(solution)/shard_map/ppermute | solution.py:441
  4.5 7.6 %collective-permute-start.1 = (f32[6,4,1024]{2,1,0:T(4,128)S(1)}, f32[6,4,1024]{2,1,0:T(4,128)S(1)}, u32[]{:S(2)}, u32[]{:S(2)}) collective-permute-start(f32[6,4,1024]{2,1,0:T(4,128)S(1)} %pad_maximum_fusion.5), channel_id=1, source_target_pairs={{1,0},{2,1},{3,2},{5,4},{6,5},{7,6},{9,8},{10,9},{11,10},{13,12},{... | collective-permute-start | bytes 294920 | tf_op jit(solution)/shard_map/ppermute | solution.py:442
  12.0 0.6 copy-start.1
  12.1 0.7 copy-start.2
  12.7 31.5 %copy-start.4 = (f32[2,240,384]{2,1,0:T(8,128)S(1)}, f32[2,240,384]{2,1,0:T(8,128)}, u32[]{:S(2)}) copy-start(f32[2,240,384]{2,1,0:T(8,128)} %get-tuple-element.19) | copy-start | bytes 2211844
  17.2 8.5 %collective-permute-start.8 = (f32[2,128,256]{2,1,0:T(8,128)}, f32[2,128,256]{2,1,0:T(8,128)S(1)}, u32[]{:S(2)}, u32[]{:S(2)}) collective-permute-start(f32[2,128,256]{2,1,0:T(8,128)} %get-tuple-element.23), channel_id=1, source_target_pairs={{1,9},{2,10},{5,13},{6,14},{9,17},{10,18},{13,21},{14,22},{17,25},... | collective-permute-start | bytes 786440 | tf_op jit(solution)/shard_map/ppermute | solution.py:446
  20.7 13.6 %collective-permute-start.7 = (f32[2,128,256]{2,1,0:T(8,128)}, f32[2,128,256]{2,1,0:T(8,128)S(1)}, u32[]{:S(2)}, u32[]{:S(2)}) collective-permute-start(f32[2,128,256]{2,1,0:T(8,128)} %get-tuple-element.23), channel_id=1, source_target_pairs={{1,5},{2,6},{5,9},{6,10},{9,13},{10,14},{13,17},{14,18},{17,21},{1... | collective-permute-start | bytes 786440 | tf_op jit(solution)/shard_map/ppermute | solution.py:446
  34.4 8.3 %collective-permute-start.9 = (f32[2,128,256]{2,1,0:T(8,128)S(1)}, f32[2,128,256]{2,1,0:T(8,128)S(1)}, u32[]{:S(2)}, u32[]{:S(2)}) collective-permute-start(f32[2,128,256]{2,1,0:T(8,128)S(1)} %pad_maximum_fusion), channel_id=1, source_target_pairs={{1,9},{2,10},{5,13},{6,14},{9,17},{10,18},{13,21},{14,22},{17,25},... | collective-permute-start | bytes 786440 | tf_op jit(solution)/shard_map/ppermute | solution.py:446
  42.9 19.9 %collective-permute-start.10 = (f32[2,128,256]{2,1,0:T(8,128)S(1)}, f32[2,128,256]{2,1,0:T(8,128)S(1)}, u32[]{:S(2)}, u32[]{:S(2)}) collective-permute-start(f32[2,128,256]{2,1,0:T(8,128)S(1)} %pad_maximum_fusion.1), channel_id=1, source_target_pairs={{1,17},{2,18},{5,21},{6,22},{9,25},{10,26},{13,29},{14,30}} | collective-permute-start | bytes 786440 | tf_op jit(solution)/shard_map/ppermute | solution.py:446
  44.2 37.0 %collective-permute-start.4 = (f32[2,240,384]{2,1,0:T(8,128)S(1)}, f32[2,240,384]{2,1,0:T(8,128)S(1)}, u32[]{:S(2)}, u32[]{:S(2)}) collective-permute-start(f32[2,240,384]{2,1,0:T(8,128)S(1)} %copy-done.4), channel_id=1, source_target_pairs={{0,4},{1,5},{2,6},{3,7},{4,8},{5,9},{6,10},{7,11},{8,12},{9,13},{1... | collective-permute-start | bytes 2211848 | tf_op jit(solution)/shard_map/ppermute | solution.py:446
  48.7 6.4 %copy-start.6 = (f32[2,128,256]{2,1,0:T(8,128)S(1)}, f32[2,128,256]{2,1,0:T(8,128)}, u32[]{:S(2)}) copy-start(f32[2,128,256]{2,1,0:T(8,128)} %get-tuple-element.21) | copy-start | bytes 786436
  48.7 7.0 %copy-start.5 = (f32[2,128,256]{2,1,0:T(8,128)S(1)}, f32[2,128,256]{2,1,0:T(8,128)}, u32[]{:S(2)}) copy-start(f32[2,128,256]{2,1,0:T(8,128)} %get-tuple-element.22) | copy-start | bytes 786436
  52.7 30.1 %collective-permute-start.2 = (f32[2,240,384]{2,1,0:T(8,128)}, f32[2,240,384]{2,1,0:T(8,128)S(1)}, u32[]{:S(2)}, u32[]{:S(2)}) collective-permute-start(f32[2,240,384]{2,1,0:T(8,128)} %get-tuple-element.16), channel_id=1, source_target_pairs={{0,4},{1,5},{2,6},{3,7},{4,8},{5,9},{6,10},{7,11},{8,12},{9,13},{1... | collective-permute-start | bytes 2211848 | tf_op jit(solution)/shard_map/ppermute | solution.py:446
  55.1 10.1 %collective-permute-start.5 = (f32[2,128,256]{2,1,0:T(8,128)S(1)}, f32[2,128,256]{2,1,0:T(8,128)S(1)}, u32[]{:S(2)}, u32[]{:S(2)}) collective-permute-start(f32[2,128,256]{2,1,0:T(8,128)S(1)} %copy-done.6), channel_id=1, source_target_pairs={{0,4},{1,5},{3,7},{4,8},{5,9},{7,11},{8,12},{9,13},{11,15},{12,16}... | collective-permute-start | bytes 786440 | tf_op jit(solution)/shard_map/ppermute | solution.py:446
  55.8 23.1 %collective-permute-start.6 = (f32[2,128,256]{2,1,0:T(8,128)S(1)}, f32[2,128,256]{2,1,0:T(8,128)S(1)}, u32[]{:S(2)}, u32[]{:S(2)}) collective-permute-start(f32[2,128,256]{2,1,0:T(8,128)S(1)} %copy-done.5), channel_id=1, source_target_pairs={{0,4},{2,6},{3,7},{4,8},{6,10},{7,11},{8,12},{10,14},{11,15},{12,1... | collective-permute-start | bytes 786440 | tf_op jit(solution)/shard_map/ppermute | solution.py:446
  58.7 6.3 %copy-start.3 = (f32[2,128,256]{2,1,0:T(8,128)S(1)}, f32[2,128,256]{2,1,0:T(8,128)}, u32[]{:S(2)}) copy-start(f32[2,128,256]{2,1,0:T(8,128)} %get-tuple-element.23) | copy-start | bytes 786436
  58.7 20.2 %copy-start = (f32[1,2,256,1024]{3,2,1,0:T(8,128)S(1)}, f32[1,2,256,1024]{3,2,1,0:T(8,128)}, u32[]{:S(2)}) copy-start(f32[1,2,256,1024]{3,2,1,0:T(8,128)} %param.2) | copy-start | bytes 6291460
  62.9 18.4 %collective-permute-start.3 = (f32[2,16,768]{2,1,0:T(8,128)}, f32[2,16,768]{2,1,0:T(8,128)S(1)}, u32[]{:S(2)}, u32[]{:S(2)}) collective-permute-start(f32[2,16,768]{2,1,0:T(8,128)} %get-tuple-element.18), channel_id=1, source_target_pairs={{0,4},{1,5},{2,6},{3,7},{4,8},{5,9},{6,10},{7,11},{8,12},{9,13},{1... | collective-permute-start | bytes 294920 | tf_op jit(solution)/shard_map/ppermute | solution.py:446

commit v4 on v3

--- a/solution.py
+++ b/solution.py
@@ -13,6 +13,7 @@
 STRIP = 32
 HALO = 4
 PAD = 8
+
 
 diffusion = 1.5
 drift = 0.8
@@ -145,6 +146,8 @@
             if kind == "in":
                 nodes[1, part, pl.ds(start, count), :] = value
                 for (low, high), send in zip(pieces, sends):
+                    if high - low == rows - coarse_rows and coarse:
+                        continue
                     a, z = max(low, start), min(high, start + count)
                     if a < z:
                         send[part, pl.ds(a - low, z - a), spot] = value[a - start:z - start]
@@ -168,6 +171,10 @@
                 off = tuple(off[part] + jnp.where(lead, begin[part, pl.ds(at, count), :], 0.0) for part in range(2))
                 offset[0, pl.ds(start, count), spot] = (off[0] * step_real + off[1] * step_imag) * share
                 offset[1, pl.ds(start, count), spot] = (off[1] * step_real - off[0] * step_imag) * share
+            if rows > coarse_rows:
+                from_row = 0 if shift else coarse_rows
+                for part in range(2):
+                    sends[1][part, :, spot] = nodes[1, part, pl.ds(from_row, rows - coarse_rows), :]
 
         low_shift = rows - coarse_rows
         if low_shift == 0:
@@ -331,32 +338,77 @@
     )(begin, old, halo[0], halo[1], nodes)
 
 
-def patch_kernel(*refs, count, pieces, coarse_rows):
-    begin, nodes_in = refs[:2]
-    arrived = refs[2:2 + count]
-    fresh, finish, start, nodes = refs[2 + count:]
+def power_of(row_base, rows, column_base, columns, size_x, size_y, doublings):
+    real, imag, _ = rates(row_base, rows, column_base, columns, size_x, size_y)
+    step_real = 1.0 - real
+    step_imag = -imag
+    share = 1.0 / (step_real * step_real + step_imag * step_imag)
+    power = (step_real * share, -step_imag * share)
+    first = power
+    for _ in range(doublings):
+        power = turned(power[0], power[1], power[0], power[1])
+    return first, power
+
+
+def step_kernel(total, field, out, *, doublings, rows, size_x, size_y, low_column):
+    rank = lax.axis_index("space")
+    coarse_rows, width = total.shape[1:]
+    shift = jnp.where(rank >= lax.axis_size("space") // 2, 0, rows - coarse_rows)
+    for start in range(0, coarse_rows, STRIP):
+        here = pl.ds(start, STRIP)
+        _, power = power_of(rank * rows + shift + start, STRIP, low_column, width, size_x, size_y, doublings)
+        grown = turned(power[0], power[1], field[0, here, :], field[1, here, :])
+        for part in range(2):
+            out[part, here, :] = total[part, here, :] + grown[part]
+
+
+def step_call(total, field, doublings, rows, size_x, size_y, low_column):
+    kernel = functools.partial(step_kernel, doublings=doublings, rows=rows, size_x=size_x, size_y=size_y,
+                               low_column=low_column)
+    return pl.pallas_call(kernel, in_specs=[VMEM, VMEM], out_specs=VMEM,
+                          out_shape=jax.ShapeDtypeStruct(total.shape, jnp.float32),
+                          compiler_params=PARAMS, name="step")(total, field)
+
+
+def patch_kernel(begin, nodes_in, outer_piece, *refs, doublings, coarse_rows, size_x, size_y, first_block):
+    prior, received, offset, start, nodes = refs[-5:]
     rows = begin.shape[1]
     rank = lax.axis_index("space")
     ranks = lax.axis_size("space")
     lead = lax.axis_index("tm") == 0
     spot = pl.ds(pl.multiple_of(pl.program_id(0) * LANES, LANES), LANES)
     middle = jnp.logical_or(rank == ranks // 2, rank == ranks // 2 - 1)
-    for (low, high), piece in zip(pieces, arrived):
-        here = pl.ds(low, high - low)
-        for part in range(2):
-            start[part, here, :] = jnp.where(lead, begin[part, here, :], piece[part, :, spot])
-    nodes[...] = nodes_in[...]
+
+    @pl.when(jnp.logical_not(middle))
+    def _():
+        nodes[...] = nodes_in[...]
+        for part in range(2):
+            start[part] = jnp.where(lead, begin[part], outer_piece[part, :, spot])
 
     def fix(shift):
-        here = pl.ds(shift, coarse_rows)
-        for part in range(2):
-            old_begin = begin[part, here, :]
-            n2 = nodes_in[1, part, here, :]
-            now = jnp.where(lead, old_begin, fresh[part, :, spot])
-            change = finish[part, :, spot] - n2
-            nodes[0, part, here, :] = nodes_in[0, part, here, :] + 0.5 * ((now - old_begin) + change)
-            nodes[1, part, here, :] = n2 + change
-            start[part, here, :] = now
+        if rows > coarse_rows:
+            other = pl.ds(0 if shift else coarse_rows, rows - coarse_rows)
+            piece = refs[0]
+            for part in range(2):
+                start[part, other, :] = jnp.where(lead, begin[part, other, :], piece[part, :, spot])
+                for k in range(2):
+                    nodes[k, part, other, :] = nodes_in[k, part, other, :]
+        for low in range(0, coarse_rows, STRIP):
+            at = pl.ds(low, STRIP)
+            here = pl.ds(shift + low, STRIP)
+            first, power = power_of(rank * rows + shift + low, STRIP, (first_block + pl.program_id(0)) * LANES, LANES,
+                                    size_x, size_y, doublings)
+            grown = turned(power[0], power[1], received[0, at, spot], received[1, at, spot])
+            total = [jnp.where(lead, 0.0, prior[part, at, spot] + grown[part]) for part in range(2)]
+            carried = turned(first[0], first[1], total[0], total[1])
+            for part in range(2):
+                old_begin = begin[part, here, :]
+                n2 = nodes_in[1, part, here, :]
+                now = jnp.where(lead, old_begin, total[part])
+                change = (offset[part, at, spot] + carried[part]) - n2
+                nodes[0, part, here, :] = nodes_in[0, part, here, :] + 0.5 * ((now - old_begin) + change)
+                nodes[1, part, here, :] = n2 + change
+                start[part, here, :] = now
 
     if rows == coarse_rows:
         @pl.when(middle)
@@ -372,52 +424,58 @@
             fix(rows - coarse_rows)
 
 
-def patch_call(begin, nodes, arrived, pieces, fresh, finish, low_column, coarse_rows):
-    rows = begin.shape[1]
+def patch_call(begin, nodes, arrived, scan, low_column, size_x, doublings):
+    rows, columns = begin.shape[1:]
     base = low_column // LANES
+    coarse_rows, width = scan[0].shape[1:]
     begin_spec = pl.BlockSpec((2, rows, LANES), lambda j: (0, 0, base + j))
     nodes_spec = pl.BlockSpec((2, 2, rows, LANES), lambda j: (0, 0, 0, base + j))
-    kernel = functools.partial(patch_kernel, count=len(arrived), pieces=pieces, coarse_rows=coarse_rows)
+    kernel = functools.partial(patch_kernel, doublings=doublings, coarse_rows=coarse_rows, size_x=size_x,
+                               size_y=columns, first_block=base)
     return pl.pallas_call(
-        kernel, grid=(fresh.shape[2] // LANES,),
-        in_specs=[begin_spec, nodes_spec] + [VMEM] * (len(arrived) + 2),
+        kernel, grid=(width // LANES,),
+        in_specs=[begin_spec, nodes_spec] + [VMEM] * (len(arrived) + 3),
         out_specs=[begin_spec, nodes_spec],
         out_shape=[jax.ShapeDtypeStruct(begin.shape, jnp.float32), jax.ShapeDtypeStruct(nodes.shape, jnp.float32)],
         input_output_aliases={1: 1}, compiler_params=PARAMS, name="patch",
-    )(begin, nodes, *arrived, fresh, finish)
-
-
-def place_kernel(begin, middle, edges, _, start, *, spot):
+    )(begin, nodes, *arrived, *scan)
+
+
+def place_kernel(begin, outer_part, middle_part, edges, _, start, *, spot):
     lead = lax.axis_index("tm") == 0
+    rank = lax.axis_index("space")
+    ranks = lax.axis_size("space")
+    middle = jnp.logical_or(rank == ranks // 2, rank == ranks // 2 - 1)
     rows = begin.shape[1]
     here = pl.ds(pl.multiple_of(pl.program_id(0) * LANES, LANES), LANES)
     side = pl.ds(pl.multiple_of(spot + pl.program_id(0) * LANES, LANES), LANES)
+    inside = pl.ds(PAD, rows - 2 * PAD)
     for part in range(2):
         start[part, pl.ds(0, PAD), :] = jnp.where(lead, begin[part, pl.ds(0, PAD), :], edges[part, pl.ds(0, PAD), side])
-        start[part, pl.ds(PAD, rows - 2 * PAD), :] = jnp.where(
-            lead, begin[part, pl.ds(PAD, rows - 2 * PAD), :], middle[part, :, here])
         start[part, pl.ds(rows - PAD, PAD), :] = jnp.where(
             lead, begin[part, pl.ds(rows - PAD, PAD), :], edges[part, pl.ds(PAD, PAD), side])
 
-
-def place_call(begin, middle, edges, start, first, spot):
+    @pl.when(middle)
+    def _():
+        for part in range(2):
+            start[part, inside, :] = jnp.where(lead, begin[part, inside, :], middle_part[part, :, here])
+
+    @pl.when(jnp.logical_not(middle))
+    def _():
+        for part in range(2):
+            start[part, inside, :] = jnp.where(lead, begin[part, inside, :], outer_part[part, :, here])
+
+
+def place_call(begin, outer_part, middle_part, edges, start, first, spot):
     rows = begin.shape[1]
     base = first // LANES
     spec = pl.BlockSpec((2, rows, LANES), lambda j: (0, 0, base + j))
     return pl.pallas_call(
-        functools.partial(place_kernel, spot=spot), grid=(middle.shape[2] // LANES,),
-        in_specs=[spec, VMEM, VMEM, ANY], out_specs=spec,
+        functools.partial(place_kernel, spot=spot), grid=(outer_part.shape[2] // LANES,),
+        in_specs=[spec, VMEM, VMEM, VMEM, ANY], out_specs=spec,
         out_shape=jax.ShapeDtypeStruct(begin.shape, jnp.float32),
-        input_output_aliases={3: 0}, compiler_params=PARAMS, name="place",
-    )(begin, middle, edges, start)
-
-
-def powers(row_base, rows, low_column, width, size_x, size_y):
-    real, imag, _ = rates(row_base, rows, low_column, width, size_x, size_y)
-    step_real = 1.0 - real
-    step_imag = -imag
-    share = 1.0 / (step_real * step_real + step_imag * step_imag)
-    return step_real * share, -step_imag * share
+        input_output_aliases={4: 0}, compiler_params=PARAMS, name="place",
+    )(begin, outer_part, middle_part, edges, start)
 
 
 def body(start_values, node_values):
@@ -429,9 +487,9 @@
     width = columns // COARSE_SHARE
     low_column = columns // 2 - width // 2
     coarse_rows = min(rows, size_x // COARSE_SHARE // 2)
-    lower, upper = ranks // 2 - 1, ranks // 2
-    rank = lax.axis_index("space")
-    lead = lax.axis_index("tm") == 0
+    middle = (ranks // 2 - 1, ranks // 2)
+    outer = [s for s in range(ranks) if s not in middle]
+    everyone = range(ranks)
 
     def edge(low):
         cut = [begin[:, low:low + HALO], old[0, :, low:low + HALO], old[1, :, low:low + HALO]]
@@ -445,50 +503,34 @@
         pairs = [(n * ranks + s, (n + steps) * ranks + s) for n in range(slices - steps) for s in members]
         return lax.ppermute(value, ("tm", "space"), pairs)
 
-    everyone = range(ranks)
-    middle = (lower, upper)
-    if rows == coarse_rows:
-        pieces = [(0, rows)]
-        holders = [[s for s in everyone if s not in middle]]
-    else:
-        cuts = [0, coarse_rows, rows - coarse_rows, rows]
-        pieces = [(a, b) for a, b in zip(cuts, cuts[1:]) if a < b]
-        holders = [[s for s in everyone
-                    if not (s == upper and b <= coarse_rows) and not (s == lower and a >= rows - coarse_rows)]
-                   for a, b in pieces]
+    pieces = [(0, rows)] + ([(0, rows - coarse_rows)] if rows > coarse_rows else [])
     second = low_column + width
     rest = columns - second
     inside = [(PAD, rows - PAD)]
     nodes, left = fine_call(begin, old, None, None, 0, low_column, inside, size_x, coarse_rows, grant(62))
-    left = ahead(left, 1, everyone)
+    left_outer = ahead(left, 1, outer)
     made = fine_call(begin, old, (before, after), nodes, low_column, width, pieces, size_x, coarse_rows, grant(60))
     nodes, inner_sends, offset = made[0], made[1:-1], made[-1]
     one_back = ahead(offset, 1, middle)
     two_back = ahead(offset, 2, middle)
+    inner = [ahead(inner_sends[0], 1, outer)]
+    left_middle = ahead(left, 1, middle)
     nodes, right = fine_call(begin, old, None, nodes, second, rest, inside, size_x, coarse_rows, grant(58))
-    right = ahead(right, 1, everyone)
+    right_outer = ahead(right, 1, outer)
     nodes, edges = edge_call(begin, old, (before, after), nodes, [(0, low_column), (second, rest)], size_x)
     edges = ahead(edges, 1, everyone)
-
-    shift = jnp.where(rank >= ranks // 2, 0, rows - coarse_rows)
-    d_real, d_imag = powers(rank * rows + shift, coarse_rows, low_column, width, size_x, columns)
-
-    def add(total, field, real, imag):
-        grown = turned(real, imag, field[0], field[1])
-        return jnp.stack([total[0] + grown[0], total[1] + grown[1]])
-
-    total = add(one_back, two_back, d_real, d_imag)
-    inner = [ahead(piece, 1, members) for piece, members in zip(inner_sends, holders)]
-    power = turned(d_real, d_imag, d_real, d_imag)
-    reach = 2
-    while reach < slices:
-        total = add(total, ahead(total, reach, middle), *power)
-        power = turned(power[0], power[1], power[0], power[1])
-        reach *= 2
-    end = add(offset, jnp.where(lead, 0.0, total), d_real, d_imag)
-    next_start, nodes = patch_call(begin, nodes, inner, pieces, total, end, low_column, coarse_rows)
-    next_start = place_call(begin, left, edges, next_start, 0, 0)
-    next_start = place_call(begin, right, edges, next_start, second, low_column)
+    inner += [ahead(piece, 1, middle) for piece in inner_sends[1:]]
+    right_middle = ahead(right, 1, middle)
+
+    total, field, reach, doublings = one_back, two_back, 1, 0
+    while 2 * reach < slices:
+        total = step_call(total, field, doublings, rows, size_x, columns, low_column)
+        reach, doublings = 2 * reach, doublings + 1
+        field = ahead(total, reach, middle)
+    scan = (total, field, offset)
+    next_start, nodes = patch_call(begin, nodes, inner, scan, low_column, size_x, doublings)
+    next_start = place_call(begin, left_outer, left_middle, edges, next_start, 0, 0)
+    next_start = place_call(begin, right_outer, right_middle, edges, next_start, second, low_column)
     return next_start[None], nodes[None]
 
 

time: 85 us -> 87.1 us (1.025)
  the two profiles are of different devices: /device:TPU:18 before, /device:TPU:30 now
where the time goes in v4:
time: 87.1 us; the launch traced here: 86.5 us
  waiting for transfers between devices  44.1 us (51%)
  Pallas kernels  22.1 us (25%)
  starting transfers between devices  16.8 us (19%)
  local copies, waits for them, and re-layouts  2.51 us (3%)
  between operations  0.88 us (1%)
    ppermute x11, waiting for transfers between devices, ahead(): return lax.ppermute(value, ('tm', 'space'), pairs)  44.1 us
    ppermute x11, starting transfers between devices, ahead(): return lax.ppermute(value, ('tm', 'space'), pairs)  12.4 us
    pallas_call x3, Pallas kernels, fine_call(): pl.pallas_call(kernel, grid=(blocks,), in_specs=in_specs, out_specs=out_s...  12.2 us
    pallas_call x1, Pallas kernels, edge_call(): pl.pallas_call(kernel, grid=(1,), in_specs=[HBM, HBM, VMEM, VMEM, ANY], o...  4.14 us
    pallas_call x2, Pallas kernels, place_call(): pl.pallas_call(functools.partial(place_kernel, spot=spot), grid=(outer_pa...  3.16 us
    ppermute x1, starting transfers between devices, body(): before = lax.ppermute(edge(rows - HALO), 'space', up)  2.41 us
    pallas_call x1, Pallas kernels, patch_call(): pl.pallas_call(kernel, grid=(width // LANES,), in_specs=[begin_spec, node...  2.38 us
    ppermute x1, starting transfers between devices, body(): after = lax.ppermute(edge(0), 'space', [(j, i) for i, j in up])  1.92 us
  transfers between devices with their start and end apart: 13, of which 5 were waited for; matrix products, arithmetic and copies ran while one was open for 0% of the time, Pallas kernels for 19%

profile of v4, /device:TPU:30, one launch (start us, length us, event | category | flops | bytes accessed | tf_op | source)
XLA Modules:
  0.0 86.5 jit_solution(17965836382298112258)
XLA Ops:
  0.6 0.9 %fusion = (f32[2,4,1024]{2,1,0:T(4,128)S(1)}, f32[2,4,1024]{2,1,0:T(4,128)S(1)}) fusion(f32[2,256,1024]{2,1,0:T(8,128)} %bitcast.12), kind=kLoop, calls=%fused_computation.6 | loop fusion | bytes 131072 | tf_op jit(solution)/shard_map/slice | solution.py:495
  1.5 1.0 %slice_bitcast_fusion.1 = (f32[2,4,1024]{2,1,0:T(4,128)S(1)}, f32[2,4,1024]{2,1,0:T(4,128)S(1)}, f32[2,4,1024]{2,1,0:T(4,128)S(1)}, f32[2,4,1024]{2,1,0:T(4,128)S(1)}) fusion(f32[2,2,256,1024]{3,2,1,0:T(8,128)} %bitcast.20), kind=kLoop, calls=%fused_computation.3 | loop fusion | bytes 262144 | tf_op jit(solution)/shard_map/squeeze | solution.py:495
  2.5 1.9 %collective-permute-start.1 = (f32[6,4,1024]{2,1,0:T(4,128)S(1)}, f32[6,4,1024]{2,1,0:T(4,128)S(1)}, u32[]{:S(2)}, u32[]{:S(2)}) collective-permute-start(f32[6,4,1024]{2,1,0:T(4,128)S(1)} %pad_maximum_fusion.1), channel_id=1, source_target_pairs={{1,0},{2,1},{3,2},{5,4},{6,5},{7,6},{9,8},{10,9},{11,10},{13,12},{... | collective-permute-start | bytes 294920 | tf_op jit(solution)/shard_map/ppermute | solution.py:500
  4.5 2.4 %collective-permute-start = (f32[6,4,1024]{2,1,0:T(4,128)S(1)}, f32[6,4,1024]{2,1,0:T(4,128)S(1)}, u32[]{:S(2)}, u32[]{:S(2)}) collective-permute-start(f32[6,4,1024]{2,1,0:T(4,128)S(1)} %pad_maximum_fusion), channel_id=1, source_target_pairs={{0,1},{1,2},{2,3},{4,5},{5,6},{6,7},{8,9},{9,10},{10,11},{12,13},{... | collective-permute-start | bytes 294920 | tf_op jit(solution)/shard_map/ppermute | solution.py:499
  6.9 3.9 %fine.2 = (f32[2,2,256,1024]{3,2,1,0:T(8,128)}, f32[2,240,384]{2,1,0:T(8,128)}) custom-call(f32[2,256,1024]{2,1,0:T(8,128)} %bitcast.13, f32[2,2,256,1024]{3,2,1,0:T(8,128)} %bitcast.21), custom_call_target="tpu_custom_call" | custom-call | tf_op jit(solution)/shard_map/fine/pallas_call | solution.py:236
  10.8 0.0 collective-permute-done.1.refs_3_.after
  10.8 0.0 copy-start.2
  10.8 0.0 collective-permute-done.refs_2_.before
  10.8 0.0 copy-start.3
  10.8 0.6 copy-done.2
  11.4 0.0 copy-done.3
  11.5 4.4 %fine_coarse.1 = (f32[2,2,256,1024]{3,2,1,0:T(8,128)}, f32[2,256,256]{2,1,0:T(8,128)}, f32[2,128,256]{2,1,0:T(8,128)}, f32[2,128,256]{2,1,0:T(8,128)}) custom-call(f32[2,256,1024]{2,1,0:T(8,128)} %bitcast.14, f32[2,2,256,1024]{3,2,1,0:T(8,128)} %bitcast.22, f32[6,4,1024]{2,1,0:T(4,128)} %copy-done.3, ...), custom_call_target="tpu_custom_call", output_to_operand_aliasing={{0}: (4, {})} | custom-call | tf_op jit(solution)/shard_map/fine_coarse/pallas_call | solution.py:236
  15.9 1.3 %collective-permute-start.10 = (f32[2,128,256]{2,1,0:T(8,128)}, f32[2,128,256]{2,1,0:T(8,128)S(1)}, u32[]{:S(2)}, u32[]{:S(2)}) collective-permute-start(f32[2,128,256]{2,1,0:T(8,128)} %get-tuple-element.23.refs_3_), channel_id=1, source_target_pairs={{1,9},{2,10},{5,13},{6,14},{9,17},{10,18},{13,21},{14,22},{17,25},... | collective-permute-start | bytes 786440 | tf_op jit(solution)/shard_map/ppermute | solution.py:504
  17.2 1.3 %collective-permute-start.9 = (f32[2,128,256]{2,1,0:T(8,128)}, f32[2,128,256]{2,1,0:T(8,128)S(1)}, u32[]{:S(2)}, u32[]{:S(2)}) collective-permute-start(f32[2,128,256]{2,1,0:T(8,128)} %get-tuple-element.23.refs_3_), channel_id=1, source_target_pairs={{1,5},{2,6},{5,9},{6,10},{9,13},{10,14},{13,17},{14,18},{17,21},{1... | collective-permute-start | bytes 786440 | tf_op jit(solution)/shard_map/ppermute | solution.py:504
  18.5 1.3 %collective-permute-start.8 = (f32[2,128,256]{2,1,0:T(8,128)}, f32[2,128,256]{2,1,0:T(8,128)S(1)}, u32[]{:S(2)}, u32[]{:S(2)}) collective-permute-start(f32[2,128,256]{2,1,0:T(8,128)} %get-tuple-element.22), channel_id=1, source_target_pairs={{1,5},{2,6},{5,9},{6,10},{9,13},{10,14},{13,17},{14,18},{17,21},{1... | collective-permute-start | bytes 786440 | tf_op jit(solution)/shard_map/ppermute | solution.py:504
  19.8 6.2 %collective-permute-done.10.field = f32[2,128,256]{2,1,0:T(8,128)S(1)} collective-permute-done((f32[2,128,256]{2,1,0:T(8,128)}, f32[2,128,256]{2,1,0:T(8,128)S(1)}, u32[]{:S(2)}, u32[]{:S(2)}) %collective-permute-start.10) | collective-permute-done | bytes 262176 | tf_op jit(solution)/shard_map/ppermute | solution.py:504
  26.0 2.5 %collective-permute-done.9.total = f32[2,128,256]{2,1,0:T(8,128)S(1)} collective-permute-done((f32[2,128,256]{2,1,0:T(8,128)}, f32[2,128,256]{2,1,0:T(8,128)S(1)}, u32[]{:S(2)}, u32[]{:S(2)}) %collective-permute-start.9) | collective-permute-done | bytes 262176 | tf_op jit(solution)/shard_map/ppermute | solution.py:504
  28.5 0.1 step.2.total
  28.6 1.3 %collective-permute-start.11 = (f32[2,128,256]{2,1,0:T(8,128)S(1)}, f32[2,128,256]{2,1,0:T(8,128)S(1)}, u32[]{:S(2)}, u32[]{:S(2)}) collective-permute-start(f32[2,128,256]{2,1,0:T(8,128)S(1)} %step.2.total), channel_id=1, source_target_pairs={{1,9},{2,10},{5,13},{6,14},{9,17},{10,18},{13,21},{14,22},{17,25},... | collective-permute-start | bytes 786440 | tf_op jit(solution)/shard_map/ppermute | solution.py:504
  29.9 0.7 collective-permute-start.7
  30.6 0.7 collective-permute-start.5
  31.3 1.3 %collective-permute-start.6 = (f32[2,240,384]{2,1,0:T(8,128)}, f32[2,240,384]{2,1,0:T(8,128)S(1)}, u32[]{:S(2)}, u32[]{:S(2)}) collective-permute-start(f32[2,240,384]{2,1,0:T(8,128)} %get-tuple-element.19), channel_id=1, source_target_pairs={{1,5},{2,6},{5,9},{6,10},{9,13},{10,14},{13,17},{14,18},{17,21},{1... | collective-permute-start | bytes 2211848 | tf_op jit(solution)/shard_map/ppermute | solution.py:504
  32.6 3.9 %fine.3 = (f32[2,2,256,1024]{3,2,1,0:T(8,128)}, f32[2,240,384]{2,1,0:T(8,128)}) custom-call(f32[2,256,1024]{2,1,0:T(8,128)} %bitcast.15, f32[2,2,256,1024]{3,2,1,0:T(8,128)} %bitcast.23, f32[2,2,256,1024]{3,2,1,0:T(8,128)} %get-tuple-element.15.refs_2_), custom_call_target="tpu_custom_call", output_to_operand_aliasing={{0}: (2, {})} | custom-call | tf_op jit(solution)/shard_map/fine/pallas_call | solution.py:236
  36.6 0.0 collective-permute-done.8.refs_0_
  36.6 0.7 collective-permute-start.2
  37.3 5.6 %collective-permute-done.11.field = f32[2,128,256]{2,1,0:T(8,128)S(1)} collective-permute-done((f32[2,128,256]{2,1,0:T(8,128)S(1)}, f32[2,128,256]{2,1,0:T(8,128)S(1)}, u32[]{:S(2)}, u32[]{:S(2)}) %collective-permute-start.11) | collective-permute-done | bytes 262176 | tf_op jit(solution)/shard_map/ppermute | solution.py:504
  42.8 1.3 %collective-permute-start.3 = (f32[2,240,384]{2,1,0:T(8,128)}, f32[2,240,384]{2,1,0:T(8,128)S(1)}, u32[]{:S(2)}, u32[]{:S(2)}) collective-permute-start(f32[2,240,384]{2,1,0:T(8,128)} %get-tuple-element.16), channel_id=1, source_target_pairs={{1,5},{2,6},{5,9},{6,10},{9,13},{10,14},{13,17},{14,18},{17,21},{1... | collective-permute-start | bytes 2211848 | tf_op jit(solution)/shard_map/ppermute | solution.py:504
  44.1 0.1 step.3.refs_1_
  44.3 0.0 collective-permute-done.7.outer_piece
  44.3 1.3 %collective-permute-start.12 = (f32[2,128,256]{2,1,0:T(8,128)S(1)}, f32[2,128,256]{2,1,0:T(8,128)S(1)}, u32[]{:S(2)}, u32[]{:S(2)}) collective-permute-start(f32[2,128,256]{2,1,0:T(8,128)S(1)} %step.3.refs_1_), channel_id=1, source_target_pairs={{1,17},{2,18},{5,21},{6,22},{9,25},{10,26},{13,29},{14,30}} | collective-permute-start | bytes 786440 | tf_op jit(solution)/shard_map/ppermute | solution.py:504
  45.6 0.0 copy-start
  45.6 0.0 copy-start.1
  45.6 4.1 %edges.1 = (f32[2,2,256,1024]{3,2,1,0:T(8,128)}, f32[2,16,768]{2,1,0:T(8,128)}) custom-call(f32[2,256,1024]{2,1,0:T(8,128)} %bitcast.16, f32[2,2,256,1024]{3,2,1,0:T(8,128)} %bitcast.24, f32[6,4,1024]{2,1,0:T(4,128)} %copy-done.3, f32[6,4,1024]{2,1,0:T(4,128)} %copy-done.2, f32[2,2,256,1024]{3,2,1,0:T(8,128)} %get-tuple-element.17._), custom_call_target="tpu_custom_call", output_to_operand_aliasing={{0}: (4, {})} | custom-call | tf_op jit(solution)/shard_map/edges/pallas_call | solution.py:329
  49.7 26.9 %collective-permute-done.12.refs_2_ = f32[2,128,256]{2,1,0:T(8,128)S(1)} collective-permute-done((f32[2,128,256]{2,1,0:T(8,128)S(1)}, f32[2,128,256]{2,1,0:T(8,128)S(1)}, u32[]{:S(2)}, u32[]{:S(2)}) %collective-permute-start.12) | collective-permute-done | bytes 262176 | tf_op jit(solution)/shard_map/ppermute | solution.py:504
  76.6 1.3 %collective-permute-start.4 = (f32[2,16,768]{2,1,0:T(8,128)}, f32[2,16,768]{2,1,0:T(8,128)S(1)}, u32[]{:S(2)}, u32[]{:S(2)}) collective-permute-start(f32[2,16,768]{2,1,0:T(8,128)} %get-tuple-element.18), channel_id=1, source_target_pairs={{0,4},{1,5},{2,6},{3,7},{4,8},{5,9},{6,10},{7,11},{8,12},{9,13},{1... | collective-permute-start | bytes 294920 | tf_op jit(solution)/shard_map/ppermute | solution.py:504
  77.9 0.0 copy-done
  77.9 0.0 copy-done.1
  77.9 2.4 %patch.1 = (f32[2,256,1024]{2,1,0:T(8,128)}, f32[2,2,256,1024]{3,2,1,0:T(8,128)}) custom-call(f32[2,256,1024]{2,1,0:T(8,128)S(1)} %bitcast.17, f32[2,2,256,1024]{3,2,1,0:T(8,128)} %get-tuple-element.20.nodes_in, f32[2,256,256]{2,1,0:T(8,128)S(1)} %collective-permute-done.7.outer_piece, ...), custom_call_target="tpu_custom_call", output_to_operand_aliasing={{1}: (1, {})} | custom-call | tf_op jit(solution)/shard_map/patch/pallas_call | solution.py:435
  80.3 3.0 %collective-permute-done.4.edges = f32[2,16,768]{2,1,0:T(8,128)S(1)} collective-permute-done((f32[2,16,768]{2,1,0:T(8,128)}, f32[2,16,768]{2,1,0:T(8,128)S(1)}, u32[]{:S(2)}, u32[]{:S(2)}) %collective-permute-start.4) | collective-permute-done | bytes 98336 | tf_op jit(solution)/shard_map/ppermute | solution.py:504
  83.3 0.0 collective-permute-done.5.outer_part
  83.3 0.0 collective-permute-done.6.middle_part
  83.3 1.6 %place.2._ = f32[2,256,1024]{2,1,0:T(8,128)} custom-call(f32[2,256,1024]{2,1,0:T(8,128)S(1)} %bitcast.18, f32[2,240,384]{2,1,0:T(8,128)S(1)} %collective-permute-done.5.outer_part, f32[2,240,384]{2,1,0:T(8,128)S(1)} %collective-permute-done.6.middle_part, f32[2,16,768]{2,1,0:T(8,128)S(1)} %collective-permute-done.4.edges, ...), custom_call_target="tpu_custom_call", output_to_operand_aliasing={{}: (4, {})} | custom-call | tf_op jit(solution)/shard_map/place/pallas_call | solution.py:473
  84.9 0.0 collective-permute-done.2.outer_part
  84.9 0.0 collective-permute-done.3.middle_part
  84.9 1.6 %place.3 = f32[2,256,1024]{2,1,0:T(8,128)} custom-call(f32[2,256,1024]{2,1,0:T(8,128)S(1)} %bitcast.19, f32[2,240,384]{2,1,0:T(8,128)S(1)} %collective-permute-done.2.outer_part, f32[2,240,384]{2,1,0:T(8,128)S(1)} %collective-permute-done.3.middle_part, f32[2,16,768]{2,1,0:T(8,128)S(1)} %collective-permute-done.4.edges, ...), custom_call_target="tpu_custom_call", output_to_operand_aliasing={{}: (4, {})} | custom-call | tf_op jit(solution)/shard_map/place/pallas_call | solution.py:473
  (2 shorter events, 0.1 us)
Async XLA Ops:
  2.5 8.3 %collective-permute-start.1 = (f32[6,4,1024]{2,1,0:T(4,128)S(1)}, f32[6,4,1024]{2,1,0:T(4,128)S(1)}, u32[]{:S(2)}, u32[]{:S(2)}) collective-permute-start(f32[6,4,1024]{2,1,0:T(4,128)S(1)} %pad_maximum_fusion.1), channel_id=1, source_target_pairs={{1,0},{2,1},{3,2},{5,4},{6,5},{7,6},{9,8},{10,9},{11,10},{13,12},{... | collective-permute-start | bytes 294920 | tf_op jit(solution)/shard_map/ppermute | solution.py:500
  4.5 6.3 %collective-permute-start = (f32[6,4,1024]{2,1,0:T(4,128)S(1)}, f32[6,4,1024]{2,1,0:T(4,128)S(1)}, u32[]{:S(2)}, u32[]{:S(2)}) collective-permute-start(f32[6,4,1024]{2,1,0:T(4,128)S(1)} %pad_maximum_fusion), channel_id=1, source_target_pairs={{0,1},{1,2},{2,3},{4,5},{5,6},{6,7},{8,9},{9,10},{10,11},{12,13},{... | collective-permute-start | bytes 294920 | tf_op jit(solution)/shard_map/ppermute | solution.py:499
  10.8 0.6 copy-start.2
  10.8 0.7 copy-start.3
  15.9 10.1 %collective-permute-start.10 = (f32[2,128,256]{2,1,0:T(8,128)}, f32[2,128,256]{2,1,0:T(8,128)S(1)}, u32[]{:S(2)}, u32[]{:S(2)}) collective-permute-start(f32[2,128,256]{2,1,0:T(8,128)} %get-tuple-element.23.refs_3_), channel_id=1, source_target_pairs={{1,9},{2,10},{5,13},{6,14},{9,17},{10,18},{13,21},{14,22},{17,25},... | collective-permute-start | bytes 786440 | tf_op jit(solution)/shard_map/ppermute | solution.py:504
  17.2 11.3 %collective-permute-start.9 = (f32[2,128,256]{2,1,0:T(8,128)}, f32[2,128,256]{2,1,0:T(8,128)S(1)}, u32[]{:S(2)}, u32[]{:S(2)}) collective-permute-start(f32[2,128,256]{2,1,0:T(8,128)} %get-tuple-element.23.refs_3_), channel_id=1, source_target_pairs={{1,5},{2,6},{5,9},{6,10},{9,13},{10,14},{13,17},{14,18},{17,21},{1... | collective-permute-start | bytes 786440 | tf_op jit(solution)/shard_map/ppermute | solution.py:504
  18.5 18.0 %collective-permute-start.8 = (f32[2,128,256]{2,1,0:T(8,128)}, f32[2,128,256]{2,1,0:T(8,128)S(1)}, u32[]{:S(2)}, u32[]{:S(2)}) collective-permute-start(f32[2,128,256]{2,1,0:T(8,128)} %get-tuple-element.22), channel_id=1, source_target_pairs={{1,5},{2,6},{5,9},{6,10},{9,13},{10,14},{13,17},{14,18},{17,21},{1... | collective-permute-start | bytes 786440 | tf_op jit(solution)/shard_map/ppermute | solution.py:504
  28.6 14.2 %collective-permute-start.11 = (f32[2,128,256]{2,1,0:T(8,128)S(1)}, f32[2,128,256]{2,1,0:T(8,128)S(1)}, u32[]{:S(2)}, u32[]{:S(2)}) collective-permute-start(f32[2,128,256]{2,1,0:T(8,128)S(1)} %step.2.total), channel_id=1, source_target_pairs={{1,9},{2,10},{5,13},{6,14},{9,17},{10,18},{13,21},{14,22},{17,25},... | collective-permute-start | bytes 786440 | tf_op jit(solution)/shard_map/ppermute | solution.py:504
  29.9 14.4 %collective-permute-start.7 = (f32[2,256,256]{2,1,0:T(8,128)}, f32[2,256,256]{2,1,0:T(8,128)S(1)}, u32[]{:S(2)}, u32[]{:S(2)}) collective-permute-start(f32[2,256,256]{2,1,0:T(8,128)} %get-tuple-element.21), channel_id=1, source_target_pairs={{0,4},{3,7},{4,8},{7,11},{8,12},{11,15},{12,16},{15,19},{16,20},{1... | collective-permute-start | bytes 1572872 | tf_op jit(solution)/shard_map/ppermute | solution.py:504
  30.6 52.7 %collective-permute-start.5 = (f32[2,240,384]{2,1,0:T(8,128)}, f32[2,240,384]{2,1,0:T(8,128)S(1)}, u32[]{:S(2)}, u32[]{:S(2)}) collective-permute-start(f32[2,240,384]{2,1,0:T(8,128)} %get-tuple-element.19), channel_id=1, source_target_pairs={{0,4},{3,7},{4,8},{7,11},{8,12},{11,15},{12,16},{15,19},{16,20},{1... | collective-permute-start | bytes 2211848 | tf_op jit(solution)/shard_map/ppermute | solution.py:504
  31.3 52.0 %collective-permute-start.6 = (f32[2,240,384]{2,1,0:T(8,128)}, f32[2,240,384]{2,1,0:T(8,128)S(1)}, u32[]{:S(2)}, u32[]{:S(2)}) collective-permute-start(f32[2,240,384]{2,1,0:T(8,128)} %get-tuple-element.19), channel_id=1, source_target_pairs={{1,5},{2,6},{5,9},{6,10},{9,13},{10,14},{13,17},{14,18},{17,21},{1... | collective-permute-start | bytes 2211848 | tf_op jit(solution)/shard_map/ppermute | solution.py:504
  36.6 48.3 %collective-permute-start.2 = (f32[2,240,384]{2,1,0:T(8,128)}, f32[2,240,384]{2,1,0:T(8,128)S(1)}, u32[]{:S(2)}, u32[]{:S(2)}) collective-permute-start(f32[2,240,384]{2,1,0:T(8,128)} %get-tuple-element.16), channel_id=1, source_target_pairs={{0,4},{3,7},{4,8},{7,11},{8,12},{11,15},{12,16},{15,19},{16,20},{1... | collective-permute-start | bytes 2211848 | tf_op jit(solution)/shard_map/ppermute | solution.py:504
  42.8 42.1 %collective-permute-start.3 = (f32[2,240,384]{2,1,0:T(8,128)}, f32[2,240,384]{2,1,0:T(8,128)S(1)}, u32[]{:S(2)}, u32[]{:S(2)}) collective-permute-start(f32[2,240,384]{2,1,0:T(8,128)} %get-tuple-element.16), channel_id=1, source_target_pairs={{1,5},{2,6},{5,9},{6,10},{9,13},{10,14},{13,17},{14,18},{17,21},{1... | collective-permute-start | bytes 2211848 | tf_op jit(solution)/shard_map/ppermute | solution.py:504
  44.3 32.3 %collective-permute-start.12 = (f32[2,128,256]{2,1,0:T(8,128)S(1)}, f32[2,128,256]{2,1,0:T(8,128)S(1)}, u32[]{:S(2)}, u32[]{:S(2)}) collective-permute-start(f32[2,128,256]{2,1,0:T(8,128)S(1)} %step.3.refs_1_), channel_id=1, source_target_pairs={{1,17},{2,18},{5,21},{6,22},{9,25},{10,26},{13,29},{14,30}} | collective-permute-start | bytes 786440 | tf_op jit(solution)/shard_map/ppermute | solution.py:504
  45.6 32.3 %copy-start = (f32[1,2,256,1024]{3,2,1,0:T(8,128)S(1)}, f32[1,2,256,1024]{3,2,1,0:T(8,128)}, u32[]{:S(2)}) copy-start(f32[1,2,256,1024]{3,2,1,0:T(8,128)} %param.2) | copy-start | bytes 6291460
  45.6 32.3 %copy-start.1 = (f32[2,128,256]{2,1,0:T(8,128)S(1)}, f32[2,128,256]{2,1,0:T(8,128)}, u32[]{:S(2)}) copy-start(f32[2,128,256]{2,1,0:T(8,128)} %get-tuple-element.23.refs_3_) | copy-start | bytes 786436
  76.6 6.7 %collective-permute-start.4 = (f32[2,16,768]{2,1,0:T(8,128)}, f32[2,16,768]{2,1,0:T(8,128)S(1)}, u32[]{:S(2)}, u32[]{:S(2)}) collective-permute-start(f32[2,16,768]{2,1,0:T(8,128)} %get-tuple-element.18), channel_id=1, source_target_pairs={{0,4},{1,5},{2,6},{3,7},{4,8},{5,9},{6,10},{7,11},{8,12},{9,13},{1... | collective-permute-start | bytes 294920 | tf_op jit(solution)/shard_map/ppermute | solution.py:504
